TPU v7x, 32 devices: a whole 2x2x4 slice. The times are simulated.
32 devices in a mesh: grp: 2 (over core), tok: 16 (over z, y, x).
Axes of the slice: x: 2, y: 2, z: 4, core: 2. Of those that a mesh axis runs over, the one named last changes fastest.
Arguments:
- tokens: bfloat16 [2, 8192, 768], P('grp', 'tok'), may hold values from -6 to 6
- branch_points: int32 [2, 16], P('grp', 'tok'), may hold values from 512 to 4096, as said below
- qkv_weight: bfloat16 [768, 896], P(('grp', 'tok')), may hold values from -0.21875 to 0.21875
- out_weight: bfloat16 [768, 768], P(('grp', 'tok')), may hold values from -3 to 3
- up_weight: bfloat16 [768, 3072], P(('grp', 'tok')), may hold values from -0.21875 to 0.21875
- down_weight: bfloat16 [3072, 768], P(('grp', 'tok')), may hold values from -0.109375 to 0.109375
- query_bias: bfloat16 [768], P(('grp', 'tok')), may hold values from -1.796875 to 1.796875
- out_bias: bfloat16 [768], P(('grp', 'tok')), may hold values from -1.796875 to 1.796875
- up_bias: bfloat16 [3072], P(('grp', 'tok')), may hold values from -3 to 3
- down_bias: bfloat16 [768], P(('grp', 'tok')), may hold values from -1.796875 to 1.796875
- first_gain: bfloat16 [768], P(('grp', 'tok')), may hold values from 0.25 to 1.75
- first_shift: bfloat16 [768], P(('grp', 'tok')), may hold values from -1.796875 to 1.796875
- second_gain: bfloat16 [768], P(('grp', 'tok')), may hold values from 0.25 to 1.75
- second_shift: bfloat16 [768], P(('grp', 'tok')), may hold values from -1.796875 to 1.796875
- cotangent: bfloat16 [2, 8192, 768], P('grp', 'tok'), may hold values from -6 to 6
Outputs:
- layer_out: bfloat16 [2, 8192, 768], P('grp', 'tok')
- kv_cache: bfloat16 [2, 8192, 128], P('grp', 'tok')
- input_grad: float32 [2, 8192, 768], P('grp', 'tok')
- qkv_weight_grad: float32 [768, 896], P(('grp', 'tok'))
- out_weight_grad: float32 [768, 768], P(('grp', 'tok'))
- up_weight_grad: float32 [768, 3072], P(('grp', 'tok'))
- down_weight_grad: float32 [3072, 768], P(('grp', 'tok'))
- query_bias_grad: float32 [768], P(('grp', 'tok'))
- out_bias_grad: float32 [768], P(('grp', 'tok'))
- up_bias_grad: float32 [3072], P(('grp', 'tok'))
- down_bias_grad: float32 [768], P(('grp', 'tok'))
- first_gain_grad: float32 [768], P(('grp', 'tok'))
- first_shift_grad: float32 [768], P(('grp', 'tok'))
- second_gain_grad: float32 [768], P(('grp', 'tok'))
- second_shift_grad: float32 [768], P(('grp', 'tok'))
Inputs may be any that keep to these rules, and one draw needn't show every extreme that they name: `branch_points`: entries of prompt blocks (b < 8) and of block 8, the first continuation, are 4096; the others lie in 512 to 4096.
All inputs are finite; a program needn't handle non-finite values.
Results may differ from a plain program's by a relative error of at most 0.01.
Values may be sent and summed in bfloat16 or wider, within the bound.
A program may use at most 192 MiB of HBM per device.

v0:
```python
from functools import partial

import jax
import jax.numpy as jnp
from jax import lax
from jax.sharding import PartitionSpec as P

HEADS = 12
HDIM = 64
ROT = 16
PDEV = 8


SCORE_SCALE = 0.125
NEGATIVE = -1e30


def layer_norm(values, gain, shift):
    centered = values - jnp.mean(values, axis=-1, keepdims=True)
    variance = jnp.mean(centered * centered, axis=-1, keepdims=True)
    return centered * lax.rsqrt(variance + 1e-05) * gain + shift


def rotate(values, positions, turn_sign):
    half_dims = ROT // 2
    frequency = 10000.0 ** (-(jnp.arange(half_dims, dtype=jnp.float32) * 2.0) / ROT)
    angles = positions[:, None] * frequency[None, :]
    new_shape = (values.shape[0],) + (1,) * (values.ndim - 2) + (half_dims,)
    cosine = jnp.cos(angles).reshape(new_shape)
    sine_part = (turn_sign * jnp.sin(angles)).reshape(new_shape)
    lower_part = values[..., :half_dims]
    upper_part = values[..., half_dims:ROT]
    return jnp.concatenate(
        [
            lower_part * cosine - upper_part * sine_part,
            upper_part * cosine + lower_part * sine_part,
            values[..., ROT:],
        ],
        axis=-1,
    )


def per_device(
    tokens,
    branch_points,
    qkv_weight,
    out_weight,
    up_weight,
    down_weight,
    query_bias,
    out_bias,
    up_bias,
    down_bias,
    first_gain,
    first_shift,
    second_gain,
    second_shift,
    cotangent,
):
    row_count = tokens.shape[1]
    width = tokens.shape[2]
    gathered = (
        lax.all_gather(qkv_weight, ("grp", "tok"), axis=0, tiled=True),
        lax.all_gather(out_weight, ("grp", "tok"), axis=0, tiled=True),
        lax.all_gather(up_weight, ("grp", "tok"), axis=0, tiled=True),
        lax.all_gather(down_weight, ("grp", "tok"), axis=0, tiled=True),
        lax.all_gather(query_bias, ("grp", "tok"), axis=0, tiled=True),
        lax.all_gather(out_bias, ("grp", "tok"), axis=0, tiled=True),
        lax.all_gather(up_bias, ("grp", "tok"), axis=0, tiled=True),
        lax.all_gather(down_bias, ("grp", "tok"), axis=0, tiled=True),
        lax.all_gather(first_gain, ("grp", "tok"), axis=0, tiled=True),
        lax.all_gather(first_shift, ("grp", "tok"), axis=0, tiled=True),
        lax.all_gather(second_gain, ("grp", "tok"), axis=0, tiled=True),
        lax.all_gather(second_shift, ("grp", "tok"), axis=0, tiled=True),
    )
    (
        qkv_full,
        out_full,
        up_full,
        down_full,
        query_full,
        out_bias_full,
        up_bias_full,
        down_bias_full,
        gain_one,
        shift_one,
        gain_two,
        shift_two,
    ) = gathered
    block_index = lax.axis_index("tok")
    is_cont = block_index >= PDEV
    local_branch = branch_points[0, 0]
    offsets = jnp.arange(row_count, dtype=jnp.int32)
    positions = jnp.where(is_cont, local_branch, block_index * row_count) + offsets
    angle_pos = positions.astype(jnp.float32)
    inputs = tokens[0].astype(jnp.float32)
    first_norm, first_back = jax.vjp(
        layer_norm, inputs, gain_one.astype(jnp.float32), shift_one.astype(jnp.float32)
    )
    second_norm, second_back = jax.vjp(
        layer_norm, inputs, gain_two.astype(jnp.float32), shift_two.astype(jnp.float32)
    )
    first_low = first_norm.astype(jnp.bfloat16)
    second_low = second_norm.astype(jnp.bfloat16)
    qkv_bias = jnp.concatenate(
        [query_full.astype(jnp.float32), jnp.zeros((2 * HDIM,), jnp.float32)]
    )
    projected = jnp.dot(first_low, qkv_full, preferred_element_type=jnp.float32) + qkv_bias
    queries = rotate(projected[:, :width].reshape(row_count, HEADS, HDIM), angle_pos, 1.0).astype(
        jnp.bfloat16
    )
    key_rot = rotate(projected[:, width : width + HDIM], angle_pos, 1.0)
    key_value = jnp.concatenate([key_rot, projected[:, width + HDIM :]], axis=1).astype(
        jnp.bfloat16
    )
    prompt_len = PDEV * row_count
    all_kv = lax.all_gather(key_value, "tok", axis=0, tiled=True)
    prompt_rows = all_kv[:prompt_len]
    key_block = 2 * row_count
    prompt_kv = prompt_rows.reshape(prompt_len // key_block, key_block, 2 * HDIM)
    block_firsts = jnp.arange(prompt_len // key_block, dtype=jnp.int32) * key_block
    own_visible = jnp.logical_and(is_cont, offsets[None, :] <= offsets[:, None])

    def prompt_visible(first_row):
        columns = first_row + jnp.arange(key_block, dtype=jnp.int32)
        return jnp.where(
            is_cont, columns[None, :] < local_branch, columns[None, :] <= positions[:, None]
        )

    def scores_of(kv_block):
        raw = jnp.einsum(
            "thd,jd->thj", queries, kv_block[:, :HDIM], preferred_element_type=jnp.float32
        )
        return raw * SCORE_SCALE

    def stat_step(carry, kv_block, visible):
        running_max, running_sum = carry
        scores = jnp.where(visible[:, None, :], scores_of(kv_block), NEGATIVE)
        new_max = jnp.maximum(running_max, jnp.max(scores, axis=-1))
        weights = jnp.where(visible[:, None, :], jnp.exp(scores - new_max[..., None]), 0.0)
        return (new_max, running_sum * jnp.exp(running_max - new_max) + jnp.sum(weights, axis=-1))

    def stat_scan(carry, kv_item):
        return (stat_step(carry, kv_item[0], prompt_visible(kv_item[1])), None)

    stat_init = (
        jnp.full((row_count, HEADS), NEGATIVE, jnp.float32),
        jnp.zeros((row_count, HEADS), jnp.float32),
    )
    stat_carry, _ = lax.scan(stat_scan, stat_init, (prompt_kv, block_firsts))
    final_max, final_sum = stat_step(stat_carry, key_value, own_visible)
    log_total = final_max + jnp.log(final_sum)

    def probs_of(kv_block, visible):
        return jnp.where(
            visible[:, None, :], jnp.exp(scores_of(kv_block) - log_total[..., None]), 0.0
        )

    def context_part(kv_block, visible):
        low_probs = probs_of(kv_block, visible).astype(jnp.bfloat16)
        return jnp.einsum(
            "thj,jd->thd", low_probs, kv_block[:, HDIM:], preferred_element_type=jnp.float32
        )

    def context_scan(accum, kv_item):
        return (accum + context_part(kv_item[0], prompt_visible(kv_item[1])), None)

    context_sum, _ = lax.scan(
        context_scan, jnp.zeros((row_count, HEADS, HDIM), jnp.float32), (prompt_kv, block_firsts)
    )
    context_sum = context_sum + context_part(key_value, own_visible)
    context_low = context_sum.reshape(row_count, width).astype(jnp.bfloat16)
    pre_act = jnp.dot(
        second_low, up_full, preferred_element_type=jnp.float32
    ) + up_bias_full.astype(jnp.float32)
    hidden, gelu_back = jax.vjp(partial(jax.nn.gelu, approximate=False), pre_act)
    hidden_low = hidden.astype(jnp.bfloat16)
    result = (
        inputs
        + jnp.dot(context_low, out_full, preferred_element_type=jnp.float32)
        + out_bias_full.astype(jnp.float32)
    )
    result = (
        result
        + jnp.dot(hidden_low, down_full, preferred_element_type=jnp.float32)
        + down_bias_full.astype(jnp.float32)
    )
    layer_out = result.astype(jnp.bfloat16)[None]
    qkv_back, out_back, up_back, down_back = (
        lax.all_gather(qkv_weight, ("grp", "tok"), axis=0, tiled=True),
        lax.all_gather(out_weight, ("grp", "tok"), axis=0, tiled=True),
        lax.all_gather(up_weight, ("grp", "tok"), axis=0, tiled=True),
        lax.all_gather(down_weight, ("grp", "tok"), axis=0, tiled=True),
    )
    grad_rows = cotangent[0]
    grad_float = grad_rows.astype(jnp.float32)
    d_context = jnp.dot(grad_rows, out_back.T, preferred_element_type=jnp.float32)
    d_context_low = d_context.astype(jnp.bfloat16).reshape(row_count, HEADS, HDIM)
    d_hidden = jnp.dot(grad_rows, down_back.T, preferred_element_type=jnp.float32)
    d_pre_low = gelu_back(d_hidden)[0].astype(jnp.bfloat16)

    def value_dots(kv_block):
        return jnp.einsum(
            "thd,jd->thj", d_context_low, kv_block[:, HDIM:], preferred_element_type=jnp.float32
        )

    def delta_part(kv_block, visible):
        return jnp.sum(probs_of(kv_block, visible) * value_dots(kv_block), axis=-1)

    def delta_scan(accum, kv_item):
        return (accum + delta_part(kv_item[0], prompt_visible(kv_item[1])), None)

    row_delta, _ = lax.scan(
        delta_scan, jnp.zeros((row_count, HEADS), jnp.float32), (prompt_kv, block_firsts)
    )
    row_delta = row_delta + delta_part(key_value, own_visible)

    def grad_part(d_query, kv_block, visible):
        key_probs = probs_of(kv_block, visible)
        d_scores = (key_probs * (value_dots(kv_block) - row_delta[..., None])).astype(jnp.bfloat16)
        d_query = d_query + SCORE_SCALE * jnp.einsum(
            "thj,jd->thd", d_scores, kv_block[:, :HDIM], preferred_element_type=jnp.float32
        )
        d_keys = SCORE_SCALE * jnp.einsum(
            "thj,thd->jd", d_scores, queries, preferred_element_type=jnp.float32
        )
        d_values = jnp.einsum(
            "thj,thd->jd",
            key_probs.astype(jnp.bfloat16),
            d_context_low,
            preferred_element_type=jnp.float32,
        )
        return (d_query, jnp.concatenate([d_keys, d_values], axis=1))

    def grad_scan(d_query, kv_item):
        return grad_part(d_query, kv_item[0], prompt_visible(kv_item[1]))

    d_query, prompt_grads = lax.scan(
        grad_scan, jnp.zeros((row_count, HEADS, HDIM), jnp.float32), (prompt_kv, block_firsts)
    )
    d_query, own_grads = grad_part(d_query, key_value, own_visible)
    group_rows = row_count * lax.axis_size("tok")
    grad_term = jnp.zeros((group_rows, 2 * HDIM), jnp.float32)
    grad_term = lax.dynamic_update_slice_in_dim(
        grad_term, prompt_grads.reshape(prompt_len, 2 * HDIM), 0, 0
    )
    own_term = lax.dynamic_update_slice_in_dim(
        jnp.zeros((group_rows, 2 * HDIM), jnp.float32), own_grads, block_index * row_count, 0
    )
    grad_term = grad_term + own_term
    kv_grad = lax.psum_scatter(
        grad_term.astype(jnp.bfloat16), "tok", scatter_dimension=0, tiled=True
    ).astype(jnp.float32)
    d_query_back = rotate(d_query, angle_pos, -1.0).reshape(row_count, width)
    d_key_back = rotate(kv_grad[:, :HDIM], angle_pos, -1.0)
    d_projected = jnp.concatenate([d_query_back, d_key_back, kv_grad[:, HDIM:]], axis=1).astype(
        jnp.bfloat16
    )
    grad_qkv_w = jnp.dot(first_low.T, d_projected, preferred_element_type=jnp.float32)
    grad_query_b = jnp.sum(d_projected[:, :width].astype(jnp.float32), axis=0)
    grad_out_w = jnp.dot(context_low.T, grad_rows, preferred_element_type=jnp.float32)
    grad_out_b = jnp.sum(grad_float, axis=0)
    grad_up_w = jnp.dot(second_low.T, d_pre_low, preferred_element_type=jnp.float32)
    grad_up_b = jnp.sum(d_pre_low.astype(jnp.float32), axis=0)
    grad_down_w = jnp.dot(hidden_low.T, grad_rows, preferred_element_type=jnp.float32)
    d_first = jnp.dot(d_projected, qkv_back.T, preferred_element_type=jnp.float32)
    d_second = jnp.dot(d_pre_low, up_back.T, preferred_element_type=jnp.float32)
    input_one, grad_gain_one, grad_shift_one = first_back(d_first)
    input_two, grad_gain_two, grad_shift_two = second_back(d_second)
    input_grad = (grad_float + input_one + input_two)[None]
    summed = (
        lax.psum_scatter(grad_qkv_w, ("grp", "tok"), scatter_dimension=0, tiled=True),
        lax.psum_scatter(grad_out_w, ("grp", "tok"), scatter_dimension=0, tiled=True),
        lax.psum_scatter(grad_up_w, ("grp", "tok"), scatter_dimension=0, tiled=True),
        lax.psum_scatter(grad_down_w, ("grp", "tok"), scatter_dimension=0, tiled=True),
        lax.psum_scatter(grad_query_b, ("grp", "tok"), scatter_dimension=0, tiled=True),
        lax.psum_scatter(grad_out_b, ("grp", "tok"), scatter_dimension=0, tiled=True),
        lax.psum_scatter(grad_up_b, ("grp", "tok"), scatter_dimension=0, tiled=True),
        lax.psum_scatter(grad_gain_one, ("grp", "tok"), scatter_dimension=0, tiled=True),
        lax.psum_scatter(grad_shift_one, ("grp", "tok"), scatter_dimension=0, tiled=True),
        lax.psum_scatter(grad_gain_two, ("grp", "tok"), scatter_dimension=0, tiled=True),
        lax.psum_scatter(grad_shift_two, ("grp", "tok"), scatter_dimension=0, tiled=True),
    )
    (
        sum_qkv_w,
        sum_out_w,
        sum_up_w,
        sum_down_w,
        sum_query_b,
        sum_out_b,
        sum_up_b,
        sum_gain_one,
        sum_shift_one,
        sum_gain_two,
        sum_shift_two,
    ) = summed
    return (
        layer_out,
        key_value[None],
        input_grad,
        sum_qkv_w,
        sum_out_w,
        sum_up_w,
        sum_down_w,
        sum_query_b,
        sum_out_b,
        sum_up_b,
        sum_out_b,
        sum_gain_one,
        sum_shift_one,
        sum_gain_two,
        sum_shift_two,
    )


def solution(mesh):
    placed = (
        P("grp", "tok", None),
        P("grp", "tok"),
        P(("grp", "tok"), None),
        P(("grp", "tok"), None),
        P(("grp", "tok"), None),
        P(("grp", "tok"), None),
        P(("grp", "tok")),
        P(("grp", "tok")),
        P(("grp", "tok")),
        P(("grp", "tok")),
        P(("grp", "tok")),
        P(("grp", "tok")),
        P(("grp", "tok")),
        P(("grp", "tok")),
        P("grp", "tok", None),
    )
    return jax.shard_map(
        per_device,
        mesh=mesh,
        in_specs=placed,
        out_specs=(
            P("grp", "tok", None),
            P("grp", "tok", None),
            P("grp", "tok", None),
            P(("grp", "tok"), None),
            P(("grp", "tok"), None),
            P(("grp", "tok"), None),
            P(("grp", "tok"), None),
            P(("grp", "tok")),
            P(("grp", "tok")),
            P(("grp", "tok")),
            P(("grp", "tok")),
            P(("grp", "tok")),
            P(("grp", "tok")),
            P(("grp", "tok")),
            P(("grp", "tok")),
        ),
        check_vma=False,
    )
```

profile of v0, /device:TPU:0, one launch (start us, length us, event | category | flops | bytes accessed | tf_op | source)
XLA Modules:
  0.0 1372.1 jit_solution(10828990252151677755)
XLA Ops:
  16.2 42.5 %all-reduce.19 = (bf16[768]{0:T(1024)(128)(2,1)}, bf16[768]{0:T(1024)(128)(2,1)}, bf16[3072]{0:T(1024)(128)(2,1)}, bf16[768]{0:T(1024)(128)(2,1)S(1)}, bf16[768]...) all-reduce(bf16[768]{0:T(1024)(128)(2,1)S(1)} %dynamic-update-slice, ...), channel_id=1, replica_groups=mesh['grp'=2,'tok'=16] {'grp','tok'}, use_global_device_ids=true, to_apply=%add.7 | all-reduce | flops 8448 | bytes 33792
  72.8 51.3 %all-gather.10.cloned.1.call-done = bf16[768,768]{1,0:T(8,128)(2,1)} async-done(((bf16[24,768]{1,0:T(8,128)(2,1)}), bf16[768,768]{1,0:T(8,128)(2,1)}) %all-gather.10.cloned.1.call-update) | async-done | bytes 1179664 | tf_op jit(solution)/shard_map/all_gather | solution.py:64
  136.7 50.6 %all-gather.8.cloned.1.call-done = bf16[8192,128]{0,1:T(8,128)(2,1)} async-done(((bf16[512,128]{0,1:T(8,128)(2,1)}), bf16[8192,128]{0,1:T(8,128)(2,1)}) %all-gather.8.cloned.1.call-update) | async-done | bytes 2097168 | tf_op jit(solution)/shard_map/all_gather | solution.py:117
  189.7 57.9 %while.48 = (s32[]{:T(128)}, f32[512,12]{0,1:T(8,128)S(1)}, f32[512,12]{0,1:T(8,128)S(1)}, pred[]{:T(512)}, s32[4]{0:T(128)S(1)}, /*index=5*/s32[]{:T(128)}, bf1...) while((s32[]{:T(128)}, f32[512,12]{0,1:T(8,128)S(1)}, ...), condition=%wide.region_5.6_spmd.clone, body=%wide.region_2.5_spmd.clone.sunk | while | flops 856720896 | bytes 53680284 | solution.py:150
  266.8 108.0 %while.50 = (s32[]{:T(128)}, f32[512,12]{0,1:T(8,128)S(1)}, pred[]{:T(512)}, s32[4]{0:T(128)S(1)}, s32[]{:T(128)}, /*index=5*/bf16[4,1024,128]{1,2,0:T(8,128)(2,...) while((s32[]{:T(128)}, f32[512,12]{0,1:T(8,128)S(1)}, ...), condition=%wide.region_12.13_spmd.clone, body=%wide.region_10.12_spmd.clone.sunk | while | flops 1643128320 | bytes 53885092 | solution.py:213
  281.7 12.3 fusion.180
  308.6 12.3 fusion.180
  335.6 12.3 fusion.180
  362.5 12.3 fusion.180
  390.1 267.7 %while.51 = (s32[]{:T(128)}, f32[512,12,64]{0,2,1:T(8,128)}, f32[4,1024,128]{1,0,2:T(4,128)}, pred[]{:T(512)}, s32[4]{0:T(128)S(1)}, /*index=5*/s32[]{:T(128)}, ...) while((s32[]{:T(128)}, f32[512,12,64]{0,2,1:T(8,128)}, ...), condition=%wide.region_15.16_spmd.clone, body=%wide.region_14.15_spmd.clone.sunk | while | flops 4091874816 | bytes 176134368 | solution.py:238
  415.9 17.2 %fusion.189 = bf16[512,12,1024]{0,2,1:T(8,128)(2,1)} fusion(f32[1024,512,12]{1,0,2:T(8,128)} %fusion.188, f32[512,12]{0,1:T(8,128)S(1)} %get-tuple-element.1076, f32[512,12]{0,1:T(8,128)S(1)} %get-tuple-element.1074, pred[512,1024]{0,1:T(8,128)(4,1)S(1)} %compare_select_fusion.11, bf16[512,12,64]{0,2,1:T(8,128)(2,1)S(1)} %get-tuple-element.1075, ...), kind=kOutput, calls=%fused_computation.45.clone.1 | convolution fusion | flops 843055104 | bytes 39256064 | tf_op jit(solution)/shard_map/while/body/eval_jaxpr/thd,jd->thj/dot_general | solution.py:203
  470.9 10.7 fusion.190
  481.6 17.2 %fusion.189 = bf16[512,12,1024]{0,2,1:T(8,128)(2,1)} fusion(f32[1024,512,12]{1,0,2:T(8,128)} %fusion.188, f32[512,12]{0,1:T(8,128)S(1)} %get-tuple-element.1076, f32[512,12]{0,1:T(8,128)S(1)} %get-tuple-element.1074, pred[512,1024]{0,1:T(8,128)(4,1)S(1)} %compare_select_fusion.11, bf16[512,12,64]{0,2,1:T(8,128)(2,1)S(1)} %get-tuple-element.1075, ...), kind=kOutput, calls=%fused_computation.45.clone.1 | convolution fusion | flops 843055104 | bytes 39256064 | tf_op jit(solution)/shard_map/while/body/eval_jaxpr/thd,jd->thj/dot_general | solution.py:203
  548.7 17.2 %fusion.189 = bf16[512,12,1024]{0,2,1:T(8,128)(2,1)} fusion(f32[1024,512,12]{1,0,2:T(8,128)} %fusion.188, f32[512,12]{0,1:T(8,128)S(1)} %get-tuple-element.1076, f32[512,12]{0,1:T(8,128)S(1)} %get-tuple-element.1074, pred[512,1024]{0,1:T(8,128)(4,1)S(1)} %compare_select_fusion.11, bf16[512,12,64]{0,2,1:T(8,128)(2,1)S(1)} %get-tuple-element.1075, ...), kind=kOutput, calls=%fused_computation.45.clone.1 | convolution fusion | flops 843055104 | bytes 39256064 | tf_op jit(solution)/shard_map/while/body/eval_jaxpr/thd,jd->thj/dot_general | solution.py:203
  615.9 17.2 %fusion.189 = bf16[512,12,1024]{0,2,1:T(8,128)(2,1)} fusion(f32[1024,512,12]{1,0,2:T(8,128)} %fusion.188, f32[512,12]{0,1:T(8,128)S(1)} %get-tuple-element.1076, f32[512,12]{0,1:T(8,128)S(1)} %get-tuple-element.1074, pred[512,1024]{0,1:T(8,128)(4,1)S(1)} %compare_select_fusion.11, bf16[512,12,64]{0,2,1:T(8,128)(2,1)S(1)} %get-tuple-element.1075, ...), kind=kOutput, calls=%fused_computation.45.clone.1 | convolution fusion | flops 843055104 | bytes 39256064 | tf_op jit(solution)/shard_map/while/body/eval_jaxpr/thd,jd->thj/dot_general | solution.py:203
  664.7 54.6 %while.49 = (s32[]{:T(128)}, f32[512,12,64]{0,2,1:T(8,128)}, pred[]{:T(512)}, s32[4]{0:T(128)S(1)}, s32[]{:T(128)}, /*index=5*/bf16[4,1024,128]{1,2,0:T(8,128)(2...) while((s32[]{:T(128)}, f32[512,12,64]{0,2,1:T(8,128)}, ...), condition=%wide.region_9.10_spmd.clone, body=%wide.region_8.9_spmd.clone.sunk | while | flops 1637617152 | bytes 5806240 | solution.py:168
  748.2 58.1 %all-gather.12.cloned.1.call-done = bf16[768,3072]{1,0:T(8,128)(2,1)} async-done(((bf16[24,3072]{1,0:T(8,128)(2,1)}), bf16[768,3072]{1,0:T(8,128)(2,1)}) %all-gather.12.cloned.1.call-update) | async-done | bytes 4718608 | tf_op jit(solution)/shard_map/all_gather | solution.py:65
  806.3 19.7 %multiply_convert_fusion.1 = (bf16[512,3072]{1,0:T(8,128)(2,1)}, f32[512,3072]{1,0:T(8,128)}, f32[512,3072]{1,0:T(8,128)}) fusion(f32[3072]{0:T(1024)S(1)} %convert_element_type.114, bf16[768,3072]{1,0:T(8,128)(2,1)} %all-gather.12.cloned.1.call-done, bf16[1,512,768]{2,1,0:T(8,128)(2,1)S(1)} %copy-done.4, f32[768]{0:T(1024)S(1)} %convert_element_type.112, ...), kind=kOutput, calls=%fused_computation.75 | convolution fusion | flops 2522087424 | bytes 21256192 | tf_op jit(solution)/shard_map/dot_general | solution.py:173
  826.0 44.9 %all-gather.14.cloned.1.call-done = bf16[3072,768]{1,0:T(8,128)(2,1)} async-done(((bf16[96,768]{1,0:T(8,128)(2,1)}), bf16[3072,768]{1,0:T(8,128)(2,1)}) %all-gather.14.cloned.1.call-update) | async-done | bytes 4718608 | tf_op jit(solution)/shard_map/all_gather | solution.py:66
  916.3 40.0 %all-reduce.18 = (f32[768]{0:T(1024)S(1)}, f32[768]{0:T(1024)S(1)}, f32[3072]{0:T(1024)S(1)}, f32[768]{0:T(1024)S(1)}, f32[768]{0:T(1024)S(1)}, /*index=5*/f32[768]{0:T(1024)S(1)}, f32[768]{0:T(1024)S(1)}) all-reduce(f32[768]{0:T(1024)S(1)} %convert_reduce_fusion.3, ...), channel_id=7, replica_groups=mesh['grp'=2,'tok'=16] {'grp','tok'}, use_global_device_ids=true, to_apply=%region_26.27.clone | all-reduce | flops 7680 | bytes 61440
  960.0 15.1 %reduce-scatter.10.cloned.1.call-done = f32[24,768]{1,0:T(8,128)} async-done(((f32[768,768]{1,0:T(8,128)}), f32[24,768]{1,0:T(8,128)}) %reduce-scatter.10.cloned.1.call-update) | async-done | bytes 73744 | tf_op jit(solution)/shard_map/reduce_scatter | solution.py:273
  975.0 105.9 %reduce-scatter.16.cloned.1.call-done = f32[24,896]{1,0:T(8,128)} async-done(((f32[768,896]{1,0:T(8,128)}), f32[24,896]{1,0:T(8,128)}) %reduce-scatter.16.cloned.1.call-update) | async-done | bytes 86032
  1081.0 141.7 %reduce-scatter.12.cloned.1.call-done = f32[24,3072]{1,0:T(8,128)} async-done(((f32[768,3072]{1,0:T(8,128)}), f32[24,3072]{1,0:T(8,128)}) %reduce-scatter.12.cloned.1.call-update) | async-done | bytes 294928 | tf_op jit(solution)/shard_map/reduce_scatter | solution.py:274
  1222.6 141.7 %reduce-scatter.14.cloned.1.call-done = f32[96,768]{1,0:T(8,128)} async-done(((f32[3072,768]{1,0:T(8,128)}), f32[96,768]{1,0:T(8,128)}) %reduce-scatter.14.cloned.1.call-update) | async-done | bytes 294928 | tf_op jit(solution)/shard_map/reduce_scatter | solution.py:275
  (390 shorter events, 514.2 us)
Async XLA Ops:
  7.2 61.0 %all-gather.6.cloned.1.call-start = ((), (), s32[]{:S(2)}) async-start(), calls=%async_computation.5 | async-start | bytes 1419264 | tf_op jit(solution)/shard_map/all_gather | solution.py:63
  7.9 116.2 %all-gather.10.cloned.1.call-start = ((), (), s32[]{:S(2)}) async-start(), calls=%async_computation.7 | async-start | bytes 1216512 | tf_op jit(solution)/shard_map/all_gather | solution.py:64
  8.7 115.5 %copy-start.10 = (bf16[1,512,768]{2,1,0:T(8,128)(2,1)S(1)}, bf16[1,512,768]{2,1,0:T(8,128)(2,1)}, u32[]{:S(2)}) copy-start(bf16[1,512,768]{2,1,0:T(8,128)(2,1)} %param.37) | copy-start | bytes 2359300
  8.7 178.6 %all-gather.8.cloned.1.call-start = ((), (), s32[]{:S(2)}) async-start(), calls=%async_computation.6 | async-start | bytes 2228224 | tf_op jit(solution)/shard_map/all_gather | solution.py:117
  58.7 68.4 %copy-start.38 = (f32[768]{0:T(1024)}, f32[768]{0:T(1024)S(1)}, u32[]{:S(2)}) copy-start(f32[768]{0:T(1024)S(1)} %convert_element_type.103) | copy-start | bytes 9220
  58.7 68.4 %copy-start.45 = (f32[768]{0:T(1024)}, f32[768]{0:T(1024)S(1)}, u32[]{:S(2)}) copy-start(f32[768]{0:T(1024)S(1)} %convert_element_type.104) | copy-start | bytes 9220
  60.1 67.0 %copy-start.25 = (f32[512]{0:T(512)}, f32[512]{0:T(512)S(1)}, u32[]{:S(2)}) copy-start(f32[512]{0:T(512)S(1)} %broadcast_multiply_fusion) | copy-start | bytes 6148
  62.2 64.9 %copy-start.27 = (f32[512]{0:T(512)}, f32[512]{0:T(512)S(1)}, u32[]{:S(2)}) copy-start(f32[512]{0:T(512)S(1)} %fusion.104) | copy-start | bytes 6148
  70.9 58.7 %copy-start.14 = (f32[512,896]{0,1:T(8,128)}, f32[512,896]{0,1:T(8,128)S(1)}, u32[]{:S(2)}) copy-start(f32[512,896]{0,1:T(8,128)S(1)} %convolution_add_fusion) | copy-start | bytes 5505028
  70.9 189.5 %copy-start.19 = (bf16[512,112]{0,1:T(8,128)(2,1)}, bf16[512,112]{0,1:T(8,128)(2,1)S(1)}, u32[]{:S(2)}) copy-start(bf16[512,112]{0,1:T(8,128)(2,1)S(1)} %slice.182) | copy-start | bytes 344068
  71.9 57.8 %copy-start.33 = (bf16[512,8]{0,1:T(8,128)(2,1)}, bf16[512,8]{0,1:T(8,128)(2,1)S(1)}, u32[]{:S(2)}) copy-start(bf16[512,8]{0,1:T(8,128)(2,1)S(1)} %get-tuple-element.673) | copy-start | bytes 24580
  71.9 57.8 %copy-start.35 = (bf16[512,8]{0,1:T(8,128)(2,1)}, bf16[512,8]{0,1:T(8,128)(2,1)S(1)}, u32[]{:S(2)}) copy-start(bf16[512,8]{0,1:T(8,128)(2,1)S(1)} %get-tuple-element.674) | copy-start | bytes 24580
  71.9 57.8 %copy-start.29 = (f32[512,8]{0,1:T(8,128)}, f32[512,8]{0,1:T(8,128)S(1)}, u32[]{:S(2)}) copy-start(f32[512,8]{0,1:T(8,128)S(1)} %get-tuple-element.675) | copy-start | bytes 49156
  72.6 670.6 %reduce-scatter.8.cloned.1.call-start = ((), (), s32[]{:S(2)}) async-start(), calls=%async_computation.10 | async-start | bytes 2228224 | tf_op jit(solution)/shard_map/reduce_scatter | solution.py:251
  72.8 302.1 %copy-start.5 = (pred[512,512]{0,1:T(8,128)(4,1)}, pred[512,512]{0,1:T(8,128)(4,1)S(1)}, u32[]{:S(2)}) copy-start(pred[512,512]{0,1:T(8,128)(4,1)S(1)} %fusion.71) | copy-start | bytes 786436
  663.4 142.8 %all-gather.12.cloned.1.call-start = ((), (), s32[]{:S(2)}) async-start(), calls=%async_computation.8 | async-start | bytes 4866048 | tf_op jit(solution)/shard_map/all_gather | solution.py:65
  664.0 206.9 %all-gather.14.cloned.1.call-start = ((), (), s32[]{:S(2)}) async-start(), calls=%async_computation.9 | async-start | bytes 4866048 | tf_op jit(solution)/shard_map/all_gather | solution.py:66
  664.6 310.4 %reduce-scatter.10.cloned.1.call-start = ((), (), s32[]{:S(2)}) async-start(), calls=%async_computation.11 | async-start | bytes 2433024 | tf_op jit(solution)/shard_map/reduce_scatter | solution.py:273
  664.7 54.6 %copy-start.6 = (pred[512,512]{0,1:T(8,128)(4,1)S(1)}, pred[512,512]{0,1:T(8,128)(4,1)}, u32[]{:S(2)}) copy-start(pred[512,512]{0,1:T(8,128)(4,1)} %copy-done.5) | copy-start | bytes 786436
  664.7 54.6 %copy-start.20 = (bf16[512,112]{0,1:T(8,128)(2,1)S(1)}, bf16[512,112]{0,1:T(8,128)(2,1)}, u32[]{:S(2)}) copy-start(bf16[512,112]{0,1:T(8,128)(2,1)} %copy-done.19) | copy-start | bytes 344068
  729.2 351.8 %reduce-scatter.16.cloned.1.call-start = ((), (), s32[]{:S(2)}) async-start(), calls=%async_computation.14 | async-start | bytes 2838528
  748.1 474.5 %reduce-scatter.12.cloned.1.call-start = ((), (), s32[]{:S(2)}) async-start(), calls=%async_computation.12 | async-start | bytes 9732096 | tf_op jit(solution)/shard_map/reduce_scatter | solution.py:274
  886.6 477.7 %reduce-scatter.14.cloned.1.call-start = ((), (), s32[]{:S(2)}) async-start(), calls=%async_computation.13 | async-start | bytes 9732096 | tf_op jit(solution)/shard_map/reduce_scatter | solution.py:275
  957.0 407.8 %copy-start.55 = (f32[24]{0:T(128)}, f32[24]{0:T(128)S(1)}, u32[]{:S(2)}) copy-start(f32[24]{0:T(128)S(1)} %dynamic-slice.3) | copy-start | bytes 292
  (45 other events, 305.9 us)
Sparse Core Ops, SparseCore 0:
  10.8 57.2 all-gather.5
  71.0 53.0 all-gather.9
  127.4 59.7 all-gather.7
  663.6 79.6 reduce-scatter.7
  746.0 60.2 all-gather.11
  809.0 61.8 all-gather.13
  876.7 98.2 reduce-scatter.9
  981.0 99.9 reduce-scatter.15
  1087.5 135.1 reduce-scatter.11
  1229.0 135.3 reduce-scatter.13
where the time goes:
time: 1380 us; the launch traced here: 1370 us
  waiting for transfers between devices  627 us (45%)
  matrix products  446 us (32%)
  local copies, waits for them, and re-layouts  99.7 us (7%)
  other arithmetic  98.2 us (7%)
  blocking collectives  82.5 us (6%)
  between operations  16.3 us (1%)
    reduce_scatter x1, waiting for transfers between devices, per_device(): lax.psum_scatter(grad_down_w, ('grp', 'tok'), scatter_dimension=0, tiled=...  142 us
    reduce_scatter x1, waiting for transfers between devices, per_device(): lax.psum_scatter(grad_up_w, ('grp', 'tok'), scatter_dimension=0, tiled=True)  142 us
    dot_general x9, matrix products, value_dots(): jnp.einsum('thd,jd->thj', d_context_low, kv_block[:, HDIM:], preferred_el...  124 us
    unnamed x11, waiting for transfers between devices  108 us
    dot_general x13, matrix products, scores_of(): jnp.einsum('thd,jd->thj', queries, kv_block[:, :HDIM], preferred_element_...  103 us
    unnamed x2, blocking collectives  82.5 us
    all_gather x1, waiting for transfers between devices, per_device(): lax.all_gather(up_weight, ('grp', 'tok'), axis=0, tiled=True)  58.1 us
    all_gather x1, waiting for transfers between devices, per_device(): lax.all_gather(out_weight, ('grp', 'tok'), axis=0, tiled=True)  51.3 us
  transfers between devices with their start and end apart: 10, of which 10 were waited for; matrix products, arithmetic and copies ran while one was open for 12% of the time, Pallas kernels for 0%

commit v1 on v0

v1 whole, which is shorter than its diff:
```python
from functools import partial

import jax
import jax.numpy as jnp
from jax import lax
from jax.experimental import pallas as pl
from jax.experimental.pallas import tpu as pltpu
from jax.sharding import PartitionSpec as P

HEADS = 12
HDIM = 64
ROT = 16
PDEV = 8
SCORE_SCALE = 0.125
NEGATIVE = -1e30
AXES = ("grp", "tok")
CHUNK = 512


def layer_norm(values, gain, shift):
    centered = values - jnp.mean(values, axis=-1, keepdims=True)
    variance = jnp.mean(centered * centered, axis=-1, keepdims=True)
    return centered * lax.rsqrt(variance + 1e-05) * gain + shift


def turn_tables(positions, width):
    half = ROT // 2
    lane = jnp.arange(width, dtype=jnp.int32) % HDIM
    frequency = 10000.0 ** (-((lane % half).astype(jnp.float32) * 2.0) / ROT)
    short = frequency[:half]
    angles = positions[:, None] * short[None, :]
    reps = width // half
    cosine = jnp.tile(jnp.cos(angles), (1, reps))
    sine = jnp.tile(jnp.sin(angles), (1, reps))
    own = jnp.where(lane < ROT, cosine, 1.0)
    from_right = jnp.where(lane < half, -sine, 0.0)
    from_left = jnp.where(jnp.logical_and(lane >= half, lane < ROT), sine, 0.0)
    return own, from_right, from_left


def turn(values, tables, sign):
    own, from_right, from_left = tables
    reps = values.shape[1] // own.shape[1]
    half = ROT // 2
    own, from_right, from_left = (jnp.tile(t, (1, reps)) for t in tables)
    return (
        values * own
        + sign * (jnp.roll(values, -half, axis=1) * from_right)
        + sign * (jnp.roll(values, half, axis=1) * from_left)
    )


def attention_kernel(
    key_count,
    q_ref,
    dc_ref,
    k2_ref,
    k2t_ref,
    v2_ref,
    v2t_ref,
    bias_ref,
    ctx_ref,
    dq_ref,
    dkt_ref,
    dvt_ref,
    s_ref,
    e_ref,
):
    rows = q_ref.shape[0]
    pair = 2 * HDIM
    prompt = key_count - rows
    unroll = 4

    @pl.when(pl.program_id(0) == 0)
    def _():
        dkt_ref[...] = jnp.zeros_like(dkt_ref)
        dvt_ref[...] = jnp.zeros_like(dvt_ref)

    first_head = lax.broadcasted_iota(jnp.int32, (rows, pair), 1) < HDIM

    def stacked(both):
        return jnp.concatenate(
            [jnp.where(first_head, both, 0.0), jnp.where(first_head, 0.0, both)], axis=0
        ).astype(jnp.bfloat16)

    def turned(both):
        flipped = both.T.astype(jnp.bfloat16)
        return jnp.concatenate([flipped[:HDIM], flipped[HDIM:]], axis=1)

    q_both = q_ref[...].astype(jnp.float32)
    q_rows = stacked(q_both)
    q_cols = turned(q_both)

    def lane_max(top, scores):
        for j in range(scores.shape[1] // pair):
            top = jnp.maximum(top, scores[:, j * pair : (j + 1) * pair])
        return top

    def score_step(c, top):
        cols = pl.ds(pl.multiple_of(c * CHUNK, CHUNK), CHUNK)
        scores = jnp.dot(q_rows, k2t_ref[:, cols], preferred_element_type=jnp.float32)
        scores = scores + bias_ref[0:1, cols]
        s_ref[:, cols] = scores
        return lane_max(top, scores)

    top = lax.fori_loop(
        0,
        prompt // CHUNK,
        score_step,
        jnp.full((2 * rows, pair), NEGATIVE, jnp.float32),
        unroll=unroll,
    )
    row_id = lax.broadcasted_iota(jnp.int32, (2 * rows, rows), 0) % rows
    col_id = lax.broadcasted_iota(jnp.int32, (2 * rows, rows), 1)
    scores = jnp.dot(q_rows, k2t_ref[:, prompt:], preferred_element_type=jnp.float32)
    scores = jnp.where(col_id <= row_id, scores, NEGATIVE)
    s_ref[:, prompt:] = scores
    top = jnp.max(lane_max(top, scores), axis=1, keepdims=True)

    def weight_step(c, carry):
        total, mixed = carry
        cols = pl.ds(pl.multiple_of(c * CHUNK, CHUNK), CHUNK)
        weights = jnp.exp(s_ref[:, cols] - top)
        for j in range(CHUNK // pair):
            total = total + weights[:, j * pair : (j + 1) * pair]
        low = weights.astype(jnp.bfloat16)
        e_ref[:, cols] = low
        mixed = mixed + jnp.dot(low, v2_ref[cols, :], preferred_element_type=jnp.float32)
        return total, mixed

    zero = jnp.zeros((2 * rows, pair), jnp.float32)
    total, mixed = lax.fori_loop(
        0, key_count // CHUNK, weight_step, (zero, zero), unroll=unroll
    )
    scale = 1.0 / jnp.sum(total, axis=1, keepdims=True)
    mixed = mixed * scale
    context = jnp.where(first_head, mixed[:rows], mixed[rows:])
    ctx_ref[...] = context.astype(ctx_ref.dtype)
    d_context = dc_ref[...]
    product = d_context * context
    delta_a = jnp.sum(jnp.where(first_head, product, 0.0), axis=1, keepdims=True)
    delta_b = jnp.sum(jnp.where(first_head, 0.0, product), axis=1, keepdims=True)
    delta = jnp.concatenate([delta_a, delta_b], axis=0) * scale
    d_both = d_context * jnp.where(first_head, scale[:rows], scale[rows:])
    d_rows = stacked(d_both)
    d_cols = turned(d_both)

    def grad_step(c, d_query):
        cols = pl.ds(pl.multiple_of(c * CHUNK, CHUNK), CHUNK)
        d_probs = jnp.dot(d_rows, v2t_ref[:, cols], preferred_element_type=jnp.float32)
        low = e_ref[:, cols]
        d_scores = (low.astype(jnp.float32) * (d_probs - delta)).astype(jnp.bfloat16)
        dvt_ref[:, cols] += jnp.dot(d_cols, low, preferred_element_type=jnp.float32)
        dkt_ref[:, cols] += jnp.dot(q_cols, d_scores, preferred_element_type=jnp.float32)
        return d_query + jnp.dot(d_scores, k2_ref[cols, :], preferred_element_type=jnp.float32)

    d_query = lax.fori_loop(0, key_count // CHUNK, grad_step, zero, unroll=unroll)
    dq_ref[...] = jnp.where(first_head, d_query[:rows], d_query[rows:]) * SCORE_SCALE


def attention(queries, d_context, keys_values, limit):
    key_count = keys_values.shape[0]
    rows, width = queries.shape
    pair = 2 * HDIM
    keys = keys_values[:, :HDIM]
    values = keys_values[:, HDIM:]
    k2 = jnp.concatenate([keys, keys], axis=1)
    v2 = jnp.concatenate([values, values], axis=1)
    column = jnp.arange(key_count, dtype=jnp.int32)
    shown = jnp.logical_or(column < limit, column >= key_count - rows)
    bias = jnp.broadcast_to(jnp.where(shown, 0.0, NEGATIVE)[None], (8, key_count))

    def whole(*shape):
        return pl.BlockSpec(shape, lambda i: (0, 0))

    block = pl.BlockSpec((rows, pair), lambda i: (0, i))
    return pl.pallas_call(
        partial(attention_kernel, key_count),
        grid=(width // pair,),
        in_specs=[
            block,
            block,
            whole(key_count, pair),
            whole(pair, key_count),
            whole(key_count, pair),
            whole(pair, key_count),
            whole(8, key_count),
        ],
        out_specs=[block, block, whole(HDIM, key_count), whole(HDIM, key_count)],
        out_shape=[
            jax.ShapeDtypeStruct((rows, width), jnp.bfloat16),
            jax.ShapeDtypeStruct((rows, width), jnp.float32),
            jax.ShapeDtypeStruct((HDIM, key_count), jnp.float32),
            jax.ShapeDtypeStruct((HDIM, key_count), jnp.float32),
        ],
        scratch_shapes=[
            pltpu.VMEM((2 * rows, key_count), jnp.float32),
            pltpu.VMEM((2 * rows, key_count), jnp.bfloat16),
        ],
        compiler_params=pltpu.CompilerParams(
            dimension_semantics=("arbitrary",), vmem_limit_bytes=58 << 20
        ),
        cost_estimate=pl.CostEstimate(
            flops=12 * rows * width * key_count,
            bytes_accessed=8 * rows * width + 16 * key_count * pair,
            transcendentals=rows * HEADS * key_count,
        ),
        name="attention",
    )(queries, d_context, k2, k2.T, v2, v2.T, bias)


def pack_small(parts, columns):
    flat = jnp.concatenate(parts)
    rows = -(-flat.shape[0] // columns)
    return jnp.pad(flat, (0, rows * columns - flat.shape[0])).reshape(rows, columns)


def unpack_small(packed, sizes):
    shards = packed.shape[0]
    flat = packed.reshape(shards, -1)
    parts = []
    start = 0
    for size in sizes:
        parts.append(flat[:, start : start + size].reshape(shards * size))
        start += size
    return parts


def per_device(
    tokens,
    branch_points,
    qkv_weight,
    out_weight,
    up_weight,
    down_weight,
    query_bias,
    out_bias,
    up_bias,
    down_bias,
    first_gain,
    first_shift,
    second_gain,
    second_shift,
    cotangent,
):
    row_count = tokens.shape[1]
    width = tokens.shape[2]
    shards = lax.axis_size("grp") * lax.axis_size("tok")
    small = [
        query_bias,
        out_bias,
        up_bias,
        down_bias,
        first_gain,
        first_shift,
        second_gain,
        second_shift,
    ]
    sizes = [s.shape[0] for s in small]
    head = jnp.concatenate([qkv_weight, pack_small(small, qkv_weight.shape[1])], axis=0)
    head_all = lax.all_gather(head, AXES, axis=0, tiled=False)
    qkv_rows = qkv_weight.shape[0]
    qkv_full = head_all[:, :qkv_rows].reshape(shards * qkv_rows, -1)
    (
        query_full,
        out_bias_full,
        up_bias_full,
        down_bias_full,
        gain_one,
        shift_one,
        gain_two,
        shift_two,
    ) = [p.astype(jnp.float32) for p in unpack_small(head_all[:, qkv_rows:], sizes)]
    out_full = lax.all_gather(out_weight, AXES, axis=0, tiled=True)
    up_full = lax.all_gather(up_weight, AXES, axis=0, tiled=True)
    down_full = lax.all_gather(down_weight, AXES, axis=0, tiled=True)

    block_index = lax.axis_index("tok")
    is_cont = block_index >= PDEV
    offsets = jnp.arange(row_count, dtype=jnp.int32)
    limit = jnp.where(is_cont, branch_points[0, 0], block_index * row_count)
    positions = (limit + offsets).astype(jnp.float32)
    tables = turn_tables(positions, 2 * HDIM)
    inputs = tokens[0].astype(jnp.float32)
    first_norm, first_back = jax.vjp(layer_norm, inputs, gain_one, shift_one)
    second_norm, second_back = jax.vjp(layer_norm, inputs, gain_two, shift_two)
    first_low = first_norm.astype(jnp.bfloat16)
    second_low = second_norm.astype(jnp.bfloat16)
    projected = jnp.dot(first_low, qkv_full, preferred_element_type=jnp.float32)
    queries = turn(projected[:, :width] + query_full, tables, 1.0).astype(jnp.bfloat16)
    queries = queries * jnp.asarray(SCORE_SCALE, jnp.bfloat16)
    key_lane = jnp.arange(2 * HDIM, dtype=jnp.int32) < HDIM
    key_tables = (
        jnp.where(key_lane, tables[0], 1.0),
        jnp.where(key_lane, tables[1], 0.0),
        jnp.where(key_lane, tables[2], 0.0),
    )
    key_value = turn(projected[:, width:], key_tables, 1.0).astype(jnp.bfloat16)
    prompt_len = PDEV * row_count
    all_kv = lax.all_gather(key_value, "tok", axis=0, tiled=True)
    keys_values = jnp.concatenate([all_kv[:prompt_len], key_value], axis=0)

    grad_rows = cotangent[0]
    grad_float = grad_rows.astype(jnp.float32)
    contract_last = (((1,), (1,)), ((), ()))
    contract_first = (((0,), (0,)), ((), ()))
    matmul = partial(lax.dot_general, preferred_element_type=jnp.float32)
    d_context = matmul(grad_rows, out_full, contract_last)
    context_low, d_query, d_keys_t, d_values_t = attention(
        queries, d_context, keys_values, limit
    )
    kv_terms = jnp.concatenate([d_keys_t, d_values_t], axis=0).T
    own_term = kv_terms[prompt_len:]
    group_rows = row_count * lax.axis_size("tok")
    sent = jnp.pad(
        kv_terms[:prompt_len].astype(jnp.bfloat16), ((0, group_rows - prompt_len), (0, 0))
    )
    kv_grad = own_term + lax.psum_scatter(
        sent, "tok", scatter_dimension=0, tiled=True
    ).astype(jnp.float32)

    pre_act = matmul(second_low, up_full, (((1,), (0,)), ((), ()))) + up_bias_full
    hidden, gelu_back = jax.vjp(partial(jax.nn.gelu, approximate=False), pre_act)
    hidden_low = hidden.astype(jnp.bfloat16)
    result = (
        inputs
        + jnp.dot(context_low, out_full, preferred_element_type=jnp.float32)
        + out_bias_full
    )
    result = (
        result
        + jnp.dot(hidden_low, down_full, preferred_element_type=jnp.float32)
        + down_bias_full
    )
    layer_out = result.astype(jnp.bfloat16)[None]
    d_hidden = matmul(grad_rows, down_full, contract_last)
    d_pre_low = gelu_back(d_hidden)[0].astype(jnp.bfloat16)
    d_query_back = turn(d_query, tables, -1.0)
    d_kv_back = turn(kv_grad, key_tables, -1.0)
    d_projected = jnp.concatenate([d_query_back, d_kv_back], axis=1).astype(jnp.bfloat16)
    grad_up_w = matmul(second_low, d_pre_low, contract_first)
    grad_down_w = matmul(hidden_low, grad_rows, contract_first)
    grad_out_w = matmul(context_low, grad_rows, contract_first)
    grad_qkv_w = matmul(first_low, d_projected, contract_first)
    grad_query_b = jnp.sum(d_projected[:, :width].astype(jnp.float32), axis=0)
    grad_out_b = jnp.sum(grad_float, axis=0)
    grad_up_b = jnp.sum(d_pre_low.astype(jnp.float32), axis=0)
    d_first = matmul(d_projected, qkv_full, contract_last)
    d_second = matmul(d_pre_low, up_full, contract_last)
    input_one, grad_gain_one, grad_shift_one = first_back(d_first)
    input_two, grad_gain_two, grad_shift_two = second_back(d_second)
    input_grad = (grad_float + input_one + input_two)[None]

    small_grads = [
        grad_query_b,
        grad_out_b,
        grad_up_b,
        grad_gain_one,
        grad_shift_one,
        grad_gain_two,
        grad_shift_two,
    ]
    grad_sizes = [g.shape[0] // shards for g in small_grads]
    small_flat = jnp.concatenate(
        [g.reshape(shards, -1) for g in small_grads], axis=1
    )
    columns = qkv_weight.shape[1]
    small_rows = -(-small_flat.shape[1] // columns)
    small_flat = jnp.pad(
        small_flat, ((0, 0), (0, small_rows * columns - small_flat.shape[1]))
    ).reshape(shards, small_rows, columns)
    tail = jnp.concatenate(
        [grad_qkv_w.reshape(shards, qkv_rows, columns), small_flat], axis=1
    )

    def scattered(term):
        return lax.psum_scatter(
            term.astype(jnp.bfloat16), AXES, scatter_dimension=0, tiled=True
        ).astype(jnp.float32)

    sum_up_w = scattered(grad_up_w)
    sum_down_w = scattered(grad_down_w)
    sum_out_w = scattered(grad_out_w)
    sum_tail = scattered(tail)[0]
    sum_qkv_w = sum_tail[:qkv_rows]
    (
        sum_query_b,
        sum_out_b,
        sum_up_b,
        sum_gain_one,
        sum_shift_one,
        sum_gain_two,
        sum_shift_two,
    ) = unpack_small(sum_tail[None, qkv_rows:], grad_sizes)
    return (
        layer_out,
        key_value[None],
        input_grad,
        sum_qkv_w,
        sum_out_w,
        sum_up_w,
        sum_down_w,
        sum_query_b,
        sum_out_b,
        sum_up_b,
        sum_out_b,
        sum_gain_one,
        sum_shift_one,
        sum_gain_two,
        sum_shift_two,
    )


def solution(mesh):
    placed = (
        P("grp", "tok", None),
        P("grp", "tok"),
        P(("grp", "tok"), None),
        P(("grp", "tok"), None),
        P(("grp", "tok"), None),
        P(("grp", "tok"), None),
        P(("grp", "tok")),
        P(("grp", "tok")),
        P(("grp", "tok")),
        P(("grp", "tok")),
        P(("grp", "tok")),
        P(("grp", "tok")),
        P(("grp", "tok")),
        P(("grp", "tok")),
        P("grp", "tok", None),
    )
    return jax.shard_map(
        per_device,
        mesh=mesh,
        in_specs=placed,
        out_specs=(
            P("grp", "tok", None),
            P("grp", "tok", None),
            P("grp", "tok", None),
            P(("grp", "tok"), None),
            P(("grp", "tok"), None),
            P(("grp", "tok"), None),
            P(("grp", "tok"), None),
            P(("grp", "tok")),
            P(("grp", "tok")),
            P(("grp", "tok")),
            P(("grp", "tok")),
            P(("grp", "tok")),
            P(("grp", "tok")),
            P(("grp", "tok")),
            P(("grp", "tok")),
        ),
        check_vma=False,
    )
```

time: 1380 us -> 884 us (0.64)
  matrix products: 446 us -> 69.4 us
  Pallas kernels: 0 us -> 109 us
  blocking collectives: 82.5 us -> 0 us
  other arithmetic: 98.2 us -> 30.4 us
  local copies, waits for them, and re-layouts: 99.7 us -> 40.1 us
  waiting for transfers between devices: 627 us -> 612 us
    dot_general x52 -> x10, matrix products: 438 us -> 61.7 us  [the longest x1 19.9 us: per_device(): matmul(second_low, up_full, (((1,), (0,)), ((), ()))) + up_bias_full]
    reduce_scatter x4 -> x5, waiting for transfers between devices: 308 us -> 466 us  [the longest x4 421 us: scattered(): lax.psum_scatter(term.astype(jnp.bfloat16), AXES, scatter_dimension=0, ti...]
    pallas_call x0 -> x1, Pallas kernels: none -> 109 us  [attention(): pl.pallas_call(partial(attention_kernel, key_count), grid=(width // pair,...]
    unnamed x11 -> x10, waiting for transfers between devices: 108 us -> 1.87 us
    unnamed x2 -> x0, blocking collectives: 82.5 us -> none
    all_gather x4, waiting for transfers between devices: 160 us -> 98.9 us  [the longest x1 54.2 us: per_device(): head_all = lax.all_gather(head, AXES, axis=0, tiled=False)]
    dynamic_update_slice x9 -> x0, local copies, waits for them, and re-layouts: 45.8 us -> none  [the longest x8 44.3 us: per_device(): lax.scan(grad_scan, jnp.zeros((row_count, HEADS, HDIM), jnp.float32), (pr...]
    reduce_sum x5 -> x0, other arithmetic: 32.8 us -> none  [stat_step(): jnp.sum(weights, axis=-1)]
  transfers between devices with their start and end apart: 10 -> 10, of which waited for: 10 -> 8; matrix products, arithmetic and copies ran while one was open for 12% -> 14% of each run, Pallas kernels for 0% -> 12%
where the time goes in v1:
time: 884 us; the launch traced here: 877 us
  waiting for transfers between devices  612 us (69%)
  Pallas kernels  109 us (12%)
  matrix products  69.4 us (8%)
  local copies, waits for them, and re-layouts  40.1 us (5%)
  other arithmetic  30.4 us (3%)
  between operations  16 us (2%)
    reduce_scatter x4, waiting for transfers between devices, scattered(): lax.psum_scatter(term.astype(jnp.bfloat16), AXES, scatter_dimension=0, ti...  421 us
    pallas_call x1, Pallas kernels, attention(): pl.pallas_call(partial(attention_kernel, key_count), grid=(width // pair,...  109 us
    all_gather x1, waiting for transfers between devices, per_device(): head_all = lax.all_gather(head, AXES, axis=0, tiled=False)  54.2 us
    reduce_scatter x1, waiting for transfers between devices, per_device(): lax.psum_scatter(sent, 'tok', scatter_dimension=0, tiled=True)  45 us
    all_gather x1, waiting for transfers between devices, per_device(): all_kv = lax.all_gather(key_value, 'tok', axis=0, tiled=True)  44.9 us
    all_gather x1, waiting for transfers between devices, per_device(): out_full = lax.all_gather(out_weight, AXES, axis=0, tiled=True)  44.7 us
    dot_general x1, matrix products, per_device(): matmul(second_low, up_full, (((1,), (0,)), ((), ()))) + up_bias_full  19.9 us
  transfers between devices with their start and end apart: 10, of which 8 were waited for; matrix products, arithmetic and copies ran while one was open for 14% of the time, Pallas kernels for 12%

profile of v1, /device:TPU:0, one launch (start us, length us, event | category | flops | bytes accessed | tf_op | source)
XLA Modules:
  0.0 877.3 jit_solution(13016033424833476647)
XLA Ops:
  7.2 5.5 concatenate.58
  18.6 54.2 %all-gather.16.cloned.1.call-done = bf16[32,25,896]{2,1,0:T(8,128)(2,1)} async-done(((bf16[1,25,896]{2,1,0:T(8,128)(2,1)}), bf16[32,25,896]{2,1,0:T(8,128)(2,1)}) %all-gather.16.cloned.1.call-update) | async-done | bytes 1433616 | tf_op jit(solution)/shard_map/all_gather | solution.py:261
  80.0 2.0 fusion.67
  83.8 44.7 %all-gather.8.cloned.1.call-done = bf16[768,768]{1,0:T(8,128)(2,1)} async-done(((bf16[24,768]{1,0:T(8,128)(2,1)}), bf16[768,768]{1,0:T(8,128)(2,1)}) %all-gather.8.cloned.1.call-update) | async-done | bytes 1179664 | tf_op jit(solution)/shard_map/all_gather | solution.py:274
  128.5 3.3 fusion.53.dc_ref
  132.4 2.3 tile.26
  138.2 3.1 copy.80
  146.8 44.9 %all-gather.10.cloned.1.call-done = bf16[8192,128]{0,1:T(8,128)(2,1)} async-done(((bf16[512,128]{0,1:T(8,128)(2,1)}), bf16[8192,128]{0,1:T(8,128)(2,1)}) %all-gather.10.cloned.1.call-update) | async-done | bytes 2097168 | tf_op jit(solution)/shard_map/all_gather | solution.py:300
  199.0 109.0 %attention.1 = (bf16[512,768]{1,0:T(8,128)(2,1)}, f32[512,768]{1,0:T(8,128)}, f32[64,4608]{1,0:T(8,128)}, f32[64,4608]{1,0:T(8,128)}) custom-call(bf16[512,768]{1,0:T(8,128)(2,1)} %fusion.61.q_ref, f32[512,768]{1,0:T(8,128)} %fusion.53.dc_ref, bf16[4608,128]{1,0:T(8,128)(2,1)} %copy.86.k2_ref, bf16[128,4608]{1,0:T(8,128)(2,1)} %get-tuple-element.116.k2t_ref, ...), custom_call_target="tpu_custom_call" | custom-call | flops 21743271936 | bytes 12582912 | tf_op jit(solution)/shard_map/attention/pallas_call | solution.py:177
  318.7 3.4 convolution_convert_fusion.3
  322.2 19.9 %multiply_convert_fusion = (bf16[512,3072]{1,0:T(8,128)(2,1)}, f32[512,3072]{1,0:T(8,128)}, f32[512,3072]{1,0:T(8,128)}) fusion(f32[3072]{0:T(1024)S(1)} %reshape.402, bf16[768,3072]{1,0:T(8,128)(2,1)} %all-gather.12.cloned.1.call-done, bf16[1,512,768]{2,1,0:T(8,128)(2,1)S(1)} %copy-done.6, f32[768]{0:T(1024)S(1)} %reshape.401, f32[768]{0:T(1024)S(1)} %reshape.400, ...), kind=kOutput, calls=%fused_computation.3 | convolution fusion | flops 2522087424 | bytes 21256192 | tf_op jit(solution)/shard_map/dot_general | solution.py:322
  342.1 9.7 %fusion.104 = (bf16[3072]{0:T(1024)(128)(2,1)S(1)}, bf16[512,3072]{1,0:T(8,128)(2,1)}) fusion(f32[512,3072]{1,0:T(8,128)} %get-tuple-element.96, bf16[3072,768]{1,0:T(8,128)(2,1)} %all-gather.14.cloned.1.call-done, bf16[1,512,768]{2,1,0:T(8,128)(2,1)S(1)} %copy-done.13, f32[512,3072]{1,0:T(8,128)} %get-tuple-element.143, f32[3072]{0:T(1024)S(1)} %reshape.402), kind=kOutput, calls=%fused_computation.180 | convolution fusion | flops 2441081856 | bytes 21252096 | tf_op jit(solution)/shard_map/dot_general | solution.py:336
  351.9 5.9 fusion.106
  357.9 45.0 %reduce-scatter.6.cloned.1.call-done = bf16[512,128]{0,1:T(8,128)(2,1)} async-done(((bf16[8192,128]{0,1:T(8,128)(2,1)}), bf16[512,128]{0,1:T(8,128)(2,1)}) %reduce-scatter.6.cloned.1.call-update) | async-done | bytes 131088 | tf_op jit(solution)/shard_map/reduce_scatter | solution.py:318
  404.4 2.9 fusion.92
  410.7 2.4 convolution_convert_fusion.2
  415.2 6.5 convolution_convert_fusion.1
  422.9 6.7 convolution_convert_fusion
  431.3 70.2 %reduce-scatter.10.cloned.1.call-done = bf16[24,768]{1,0:T(8,128)(2,1)} async-done(((bf16[768,768]{1,0:T(8,128)(2,1)}), bf16[24,768]{1,0:T(8,128)(2,1)}) %reduce-scatter.10.cloned.1.call-update) | async-done | bytes 36880 | tf_op jit(solution)/shard_map/reduce_scatter | solution.py:377
  502.9 6.0 fusion.105
  510.7 2.0 add_bitcast_fusion
  512.8 133.5 %reduce-scatter.8.cloned.1.call-done = bf16[1,25,896]{2,1,0:T(8,128)(2,1)} async-done(((bf16[32,25,896]{2,1,0:T(8,128)(2,1)}), bf16[1,25,896]{2,1,0:T(8,128)(2,1)}) %reduce-scatter.8.cloned.1.call-update) | async-done | bytes 44816 | tf_op jit(solution)/shard_map/reduce_scatter | solution.py:377
  648.9 107.2 %reduce-scatter.12.cloned.1.call-done = bf16[24,3072]{1,0:T(8,128)(2,1)} async-done(((bf16[768,3072]{1,0:T(8,128)(2,1)}), bf16[24,3072]{1,0:T(8,128)(2,1)}) %reduce-scatter.12.cloned.1.call-update) | async-done | bytes 147472 | tf_op jit(solution)/shard_map/reduce_scatter | solution.py:377
  757.8 110.1 %reduce-scatter.14.cloned.1.call-done = bf16[96,768]{1,0:T(8,128)(2,1)} async-done(((bf16[3072,768]{1,0:T(8,128)(2,1)}), bf16[96,768]{1,0:T(8,128)(2,1)}) %reduce-scatter.14.cloned.1.call-update) | async-done | bytes 147472 | tf_op jit(solution)/shard_map/reduce_scatter | solution.py:377
  (190 shorter events, 61.1 us)
Async XLA Ops:
  7.2 10.9 %copy-start.5 = (bf16[1,512,768]{2,1,0:T(8,128)(2,1)S(1)}, bf16[1,512,768]{2,1,0:T(8,128)(2,1)}, u32[]{:S(2)}) copy-start(bf16[1,512,768]{2,1,0:T(8,128)(2,1)} %param.15) | copy-start | bytes 2359300
  7.2 65.6 %all-gather.16.cloned.1.call-start = ((), (), s32[]{:S(2)}) async-start(), calls=%async_computation.14 | async-start | bytes 1892352 | tf_op jit(solution)/shard_map/all_gather | solution.py:261
  14.2 114.3 %all-gather.8.cloned.1.call-start = ((), (), s32[]{:S(2)}) async-start(), calls=%async_computation.5 | async-start | bytes 1216512 | tf_op jit(solution)/shard_map/all_gather | solution.py:274
  14.9 176.7 %all-gather.10.cloned.1.call-start = ((), (), s32[]{:S(2)}) async-start(), calls=%async_computation.6 | async-start | bytes 2228224 | tf_op jit(solution)/shard_map/all_gather | solution.py:300
  18.4 57.9 %copy-start.26 = (f32[512]{0:T(512)}, f32[512]{0:T(512)S(1)}, u32[]{:S(2)}) copy-start(f32[512]{0:T(512)S(1)} %fusion.24) | copy-start | bytes 6148
  18.4 57.9 %copy-start.24 = (f32[512]{0:T(512)}, f32[512]{0:T(512)S(1)}, u32[]{:S(2)}) copy-start(f32[512]{0:T(512)S(1)} %fusion.75) | copy-start | bytes 6148
  18.6 61.4 %copy-start.17 = (f32[512,8]{0,1:T(8,128)}, f32[512,8]{0,1:T(8,128)S(1)}, u32[]{:S(2)}) copy-start(f32[512,8]{0,1:T(8,128)S(1)} %get-tuple-element.140) | copy-start | bytes 49156
  79.8 48.8 %copy-start.12 = (bf16[1,512,768]{2,1,0:T(8,128)(2,1)S(1)}, bf16[1,512,768]{2,1,0:T(8,128)(2,1)}, u32[]{:S(2)}) copy-start(bf16[1,512,768]{2,1,0:T(8,128)(2,1)} %param.29) | copy-start | bytes 2359300
  82.0 240.2 %all-gather.12.cloned.1.call-start = ((), (), s32[]{:S(2)}) async-start(), calls=%async_computation.7 | async-start | bytes 4866048 | tf_op jit(solution)/shard_map/all_gather | solution.py:275
  82.6 259.5 %all-gather.14.cloned.1.call-start = ((), (), s32[]{:S(2)}) async-start(), calls=%async_computation.8 | async-start | bytes 4866048 | tf_op jit(solution)/shard_map/all_gather | solution.py:276
  83.2 319.7 %reduce-scatter.6.cloned.1.call-start = ((), (), s32[]{:S(2)}) async-start(), calls=%async_computation.9 | async-start | bytes 2228224 | tf_op jit(solution)/shard_map/reduce_scatter | solution.py:318
  146.8 44.9 %copy-start.15 = (bf16[512,128]{0,1:T(8,128)(2,1)S(1)}, bf16[512,128]{0,1:T(8,128)(2,1)}, u32[]{:S(2)}) copy-start(bf16[512,128]{0,1:T(8,128)(2,1)} %get-tuple-element.129) | copy-start | bytes 393220
  312.8 188.7 %reduce-scatter.10.cloned.1.call-start = ((), (), s32[]{:S(2)}) async-start(), calls=%async_computation.11 | async-start | bytes 1216512 | tf_op jit(solution)/shard_map/reduce_scatter | solution.py:377
  314.5 7.7 copy-start.30
  322.1 20.0 %copy-start.13 = (bf16[1,512,768]{2,1,0:T(8,128)(2,1)S(1)}, bf16[1,512,768]{2,1,0:T(8,128)(2,1)}, u32[]{:S(2)}) copy-start(bf16[1,512,768]{2,1,0:T(8,128)(2,1)} %param.29) | copy-start | bytes 2359300
  322.1 324.1 %reduce-scatter.8.cloned.1.call-start = ((), (), s32[]{:S(2)}) async-start(), calls=%async_computation.10 | async-start | bytes 1892352 | tf_op jit(solution)/shard_map/reduce_scatter | solution.py:377
  357.8 46.2 %copy-start.18 = (f32[512,8]{0,1:T(8,128)S(1)}, f32[512,8]{0,1:T(8,128)}, u32[]{:S(2)}) copy-start(f32[512,8]{0,1:T(8,128)} %copy-done.17) | copy-start | bytes 49156
  357.8 46.2 %copy-start.32 = (pred[128]{0:T(512)(128)(4,1)S(1)}, pred[128]{0:T(512)(128)(4,1)}, u32[]{:S(2)}) copy-start(pred[128]{0:T(512)(128)(4,1)} %get-tuple-element.147) | copy-start | bytes 388
  357.9 46.2 %copy-start.33 = (pred[128]{0:T(512)(128)(4,1)S(1)}, pred[128]{0:T(512)(128)(4,1)}, u32[]{:S(2)}) copy-start(pred[128]{0:T(512)(128)(4,1)} %get-tuple-element.148) | copy-start | bytes 388
  357.9 46.2 %copy-start.34 = (pred[128]{0:T(512)(128)(4,1)S(1)}, pred[128]{0:T(512)(128)(4,1)}, u32[]{:S(2)}) copy-start(pred[128]{0:T(512)(128)(4,1)} %get-tuple-element.149) | copy-start | bytes 388
  357.9 46.2 %copy-start.35 = (pred[128]{0:T(512)(128)(4,1)S(1)}, pred[128]{0:T(512)(128)(4,1)}, u32[]{:S(2)}) copy-start(pred[128]{0:T(512)(128)(4,1)} %get-tuple-element.150) | copy-start | bytes 388
  414.6 341.5 %reduce-scatter.12.cloned.1.call-start = ((), (), s32[]{:S(2)}) async-start(), calls=%async_computation.12 | async-start | bytes 4866048 | tf_op jit(solution)/shard_map/reduce_scatter | solution.py:377
  421.7 446.1 %reduce-scatter.14.cloned.1.call-start = ((), (), s32[]{:S(2)}) async-start(), calls=%async_computation.13 | async-start | bytes 4866048 | tf_op jit(solution)/shard_map/reduce_scatter | solution.py:377
  647.7 222.4 %copy-start.36 = (f32[24]{0:T(128)}, f32[24]{0:T(128)S(1)}, u32[]{:S(2)}) copy-start(f32[24]{0:T(128)S(1)} %get-tuple-element.176) | copy-start | bytes 292
  (26 other events, 60.6 us)
Sparse Core Ops, SparseCore 0:
  14.3 58.4 all-gather.15
  75.7 52.7 all-gather.7
  131.8 59.7 all-gather.9
  194.4 61.7 all-gather.11
  259.0 61.8 all-gather.13
  323.0 79.8 reduce-scatter.5
  408.0 93.4 reduce-scatter.9
  503.7 142.4 reduce-scatter.7
  651.7 104.3 reduce-scatter.11
  761.5 106.3 reduce-scatter.13

commit v2 on v1

--- a/solution.py
+++ b/solution.py
@@ -209,10 +209,496 @@
     )(queries, d_context, k2, k2.T, v2, v2.T, bias)
 
 
-def pack_small(parts, columns):
-    flat = jnp.concatenate(parts)
-    rows = -(-flat.shape[0] // columns)
-    return jnp.pad(flat, (0, rows * columns - flat.shape[0])).reshape(rows, columns)
+MESH = pl.DeviceIdType.MESH
+Z_CHIPS = 4
+ROUTES = ("yx", "xy", "yx", "xy")
+SLABS = 32
+
+
+def chip_place():
+    tok = lax.axis_index("tok")
+    return tok // 4, (tok // 2) % 2, tok % 2, lax.axis_index("grp")
+
+
+def near(place, k=0, fy=0, fx=0, fg=0):
+    z, y, x, g = place
+    zz = (z, z + 1 - 2 * (z % 2), (z + 2) % Z_CHIPS, Z_CHIPS - 1 - z)[k]
+    return zz, (1 - y if fy else y), (1 - x if fx else x), (1 - g if fg else g)
+
+
+def device_at(coords):
+    z, y, x, g = coords
+    return {"tok": z * 4 + y * 2 + x, "grp": g}
+
+
+def slot_at(coords):
+    z, y, x, g = coords
+    return g * 16 + z * 4 + y * 2 + x
+
+
+def near_pq(place, order, k=0, fp=0, fq=0, fg=0):
+    if order == "yx":
+        return near(place, k, fp, fq, fg)
+    return near(place, k, fq, fp, fg)
+
+
+def greet(place):
+    barrier = pltpu.get_barrier_semaphore()
+    peers = [near(place, k=1), near(place, k=2), near(place, k=3)]
+    peers += [near(place, fy=1), near(place, fx=1), near(place, fg=1)]
+    for peer in peers:
+        pl.semaphore_signal(barrier, inc=1, device_id=device_at(peer), device_id_type=MESH)
+    pl.semaphore_wait(barrier, len(peers))
+
+
+def remote(src, dst, send_sem, recv_sem, coords):
+    return pltpu.make_async_remote_copy(
+        src_ref=src,
+        dst_ref=dst,
+        send_sem=send_sem,
+        recv_sem=recv_sem,
+        device_id=device_at(coords),
+        device_id_type=MESH,
+    )
+
+
+class Gather:
+    def __init__(self, place, orders, ins, outs, send, recv, local):
+        self.place, self.orders, self.ins, self.outs = place, orders, ins, outs
+        self.send, self.recv, self.local = send, recv, local
+        self.started = []
+
+    def push(self, a, src, slot, index, coords):
+        copy = remote(
+            src, self.outs[a].at[slot], self.send.at[a, index], self.recv.at[a, index], coords
+        )
+        copy.start()
+        self.started.append(copy)
+
+    def spread(self, a, k, fp, fq):
+        place, order = self.place, self.orders[a]
+        slot = slot_at(near_pq(place, order, k, fp, fq))
+        own = k == 0 and fp == 0 and fq == 0
+        src = self.ins[a] if own else self.outs[a].at[slot]
+        if own:
+            for j in (1, 2, 3):
+                self.push(a, src, slot, j * 4, near(place, k=j))
+        if fp == 0 and fq == 0:
+            self.push(a, src, slot, k * 4 + 2, near_pq(place, order, fp=1))
+        if fq == 0:
+            self.push(a, src, slot, k * 4 + fp * 2 + 1, near_pq(place, order, fq=1))
+        self.push(a, src, slot, 16 + k * 4 + fp * 2 + fq, near(place, fg=1))
+
+    def arrived(self, a, k, fp, fq, fg=0):
+        slot = slot_at(near_pq(self.place, self.orders[a], k, fp, fq, fg))
+        index = 16 * fg + k * 4 + fp * 2 + fq
+        block = self.outs[a].at[slot]
+        remote(
+            block, block, self.send.at[a, index], self.recv.at[a, index], near(self.place, fg=1)
+        ).wait_recv()
+
+    def own_copy(self, a):
+        slot = slot_at(self.place)
+        return pltpu.make_async_copy(self.ins[a], self.outs[a].at[slot], self.local.at[a])
+
+    def begin(self, arrays):
+        for a in arrays:
+            self.spread(a, 0, 0, 0)
+            self.own_copy(a).start()
+
+    def pass_on(self, arrays, slabs):
+        for slab in slabs:
+            for a in arrays:
+                self.arrived(a, *slab)
+                self.spread(a, *slab)
+
+    def finish(self, arrays):
+        for a in arrays:
+            self.own_copy(a).wait()
+            for k in range(4):
+                for fp in range(2):
+                    for fq in range(2):
+                        self.arrived(a, k, fp, fq, 1)
+        for copy in self.started:
+            copy.wait_send()
+
+
+Z_SLABS = [(1, 0, 0), (2, 0, 0), (3, 0, 0)]
+P_SLABS = [(k, 1, 0) for k in range(4)]
+Q_SLABS = [(k, fp, 1) for fp in range(2) for k in range(4)]
+
+
+def gather_kernel(orders, *refs):
+    n = len(orders)
+    ins, outs = refs[:n], refs[n : 2 * n]
+    send, recv, local = refs[2 * n :]
+    place = chip_place()
+    greet(place)
+    gather = Gather(place, orders, ins, outs, send, recv, local)
+    arrays = range(n)
+    gather.begin(arrays)
+    gather.pass_on(arrays, Z_SLABS + P_SLABS + Q_SLABS)
+    gather.finish(arrays)
+
+
+def gather_shards(shards, orders, collective_id, name):
+    n = len(shards)
+    return pl.pallas_call(
+        partial(gather_kernel, orders),
+        in_specs=[pl.BlockSpec(memory_space=pl.ANY)] * n,
+        out_specs=[pl.BlockSpec(memory_space=pl.ANY)] * n,
+        out_shape=[jax.ShapeDtypeStruct((SLABS,) + s.shape, s.dtype) for s in shards],
+        scratch_shapes=[
+            pltpu.SemaphoreType.DMA((n, 32)),
+            pltpu.SemaphoreType.DMA((n, 32)),
+            pltpu.SemaphoreType.DMA((n,)),
+        ],
+        compiler_params=pltpu.CompilerParams(collective_id=collective_id, has_side_effects=True),
+        name=name,
+    )(*shards)
+
+
+class Reduce:
+    def __init__(self, place, orders, ins, outs, accs, boxes, send, recv, local):
+        self.place, self.orders, self.ins, self.outs = place, orders, ins, outs
+        self.accs, self.boxes = accs, boxes
+        self.send, self.recv, self.local = send, recv, local
+        self.started = []
+
+    def mail(self, a, src, index, coords):
+        copy = remote(
+            src, self.boxes[a].at[index], self.send.at[a, index], self.recv.at[a, index], coords
+        )
+        copy.start()
+        self.started.append(copy)
+
+    def load(self, a, k, fp, fq):
+        slot = slot_at(near_pq(self.place, self.orders[a], k, fp, fq))
+        sid = k * 4 + fp * 2 + fq
+        return pltpu.make_async_copy(
+            self.ins[a].at[slot], self.accs[a].at[sid], self.local.at[a, sid]
+        )
+
+    def begin(self, arrays, slabs):
+        for k, fp, fq in slabs:
+            for a in arrays:
+                slot = slot_at(near_pq(self.place, self.orders[a], k, fp, fq, 1))
+                sid = k * 4 + fp * 2 + fq
+                self.mail(a, self.ins[a].at[slot], sid, near(self.place, fg=1))
+                self.load(a, k, fp, fq).start()
+
+    def arrived(self, a, index):
+        box = self.boxes[a].at[index]
+        remote(
+            box, box, self.send.at[a, index], self.recv.at[a, index], near(self.place, fg=1)
+        ).wait_recv()
+        return box[...].astype(jnp.float32)
+
+    def step(self, a, k, fp, fq):
+        sid = k * 4 + fp * 2 + fq
+        self.load(a, k, fp, fq).wait()
+        total = self.accs[a][sid].astype(jnp.float32) + self.arrived(a, sid)
+        place, order = self.place, self.orders[a]
+        if fq == 0:
+            total = total + self.arrived(a, 16 + k * 2 + fp)
+        if fq == 0 and fp == 0:
+            total = total + self.arrived(a, 24 + k)
+        if (k, fp, fq) == (0, 0, 0):
+            for j in (1, 2, 3):
+                total = total + self.arrived(a, 27 + j)
+            self.outs[a][...] = total
+            return
+        self.accs[a][sid] = total.astype(jnp.bfloat16)
+        src = self.accs[a].at[sid]
+        if fq == 1:
+            self.mail(a, src, 16 + k * 2 + fp, near_pq(place, order, fq=1))
+        elif fp == 1:
+            self.mail(a, src, 24 + k, near_pq(place, order, fp=1))
+        else:
+            self.mail(a, src, 27 + k, near(place, k=k))
+
+    def finish(self):
+        for copy in self.started:
+            copy.wait_send()
+
+
+SUM_SLABS = (
+    [(k, 1, 1) for k in (3, 2, 1, 0)]
+    + [(k, 0, 1) for k in (3, 2, 1, 0)]
+    + [(k, 1, 0) for k in (3, 2, 1, 0)]
+    + [(k, 0, 0) for k in (3, 2, 1, 0)]
+)
+
+
+def reduce_kernel(orders, *refs):
+    n = len(orders)
+    ins, outs, accs, boxes = (refs[i * n : (i + 1) * n] for i in range(4))
+    send, recv, local = refs[4 * n :]
+    place = chip_place()
+    greet(place)
+    reduce = Reduce(place, orders, ins, outs, accs, boxes, send, recv, local)
+    arrays = range(n)
+    reduce.begin(arrays, SUM_SLABS)
+    for slab in SUM_SLABS:
+        for a in arrays:
+            reduce.step(a, *slab)
+    reduce.finish()
+
+
+def reduce_shards(terms, orders, collective_id, name):
+    n = len(terms)
+    return pl.pallas_call(
+        partial(reduce_kernel, orders),
+        in_specs=[pl.BlockSpec(memory_space=pl.ANY)] * n,
+        out_specs=[pl.BlockSpec(memory_space=pltpu.VMEM)] * n,
+        out_shape=[jax.ShapeDtypeStruct(t.shape[1:], jnp.float32) for t in terms],
+        scratch_shapes=[pltpu.VMEM((16,) + t.shape[1:], t.dtype) for t in terms]
+        + [pltpu.VMEM((31,) + t.shape[1:], t.dtype) for t in terms]
+        + [
+            pltpu.SemaphoreType.DMA((n, 31)),
+            pltpu.SemaphoreType.DMA((n, 31)),
+            pltpu.SemaphoreType.DMA((n, 16)),
+        ],
+        compiler_params=pltpu.CompilerParams(
+            collective_id=collective_id, has_side_effects=True, vmem_limit_bytes=58 << 20
+        ),
+        name=name,
+    )(*terms)
+
+
+def kv_route(place, half, fp=0, fq=0):
+    if half == 0:
+        return near(place, fy=fp, fx=fq)
+    return near(place, fy=fq, fx=fp)
+
+
+def kv_slot(coords, plane):
+    return plane * 4 + coords[1] * 2 + coords[2]
+
+
+def kv_gather_kernel(kv_ref, all_ref, send, recv, local):
+    place = chip_place()
+    z, y, x, g = place
+    rows = kv_ref.shape[0] // 2
+    greet(place)
+
+    def at_z(zz):
+        return (zz, y, x, g)
+
+    def block(slot, half=None):
+        if half is None:
+            return all_ref.at[slot]
+        return all_ref.at[slot, pl.ds(half * rows, rows)]
+
+    def waiter(ref, index):
+        remote(ref, ref, send.at[index], recv.at[index], near(place, fg=1)).wait_recv()
+
+    own = pltpu.make_async_copy(kv_ref, block(kv_slot(place, z % 2)), local.at[0])
+
+    def own_push(index, zz):
+        return remote(
+            kv_ref, block(kv_slot(place, z % 2)), send.at[index], recv.at[z % 2], at_z(zz)
+        )
+
+    def relay(plane):
+        ref = block(kv_slot(place, plane))
+        return remote(ref, ref, send.at[plane], recv.at[plane], at_z(3))
+
+    @pl.when(z < 2)
+    def _():
+        own_push(0, 1 - z % 2).start()
+        own_push(1, 2).start()
+        own.start()
+
+    started = []
+
+    def push(ref, index, coords):
+        copy = remote(ref, ref, send.at[index], recv.at[index], coords)
+        copy.start()
+        started.append(copy)
+
+    @pl.when(z < 2)
+    def _():
+        own.wait()
+
+    def here(plane):
+        @pl.when(z != plane)
+        def _():
+            waiter(block(kv_slot(place, plane)), plane)
+
+        @pl.when(z == 2)
+        def _():
+            relay(plane).start()
+
+    for plane in (1, 0):
+        here(plane)
+        for half in range(2):
+            ref = block(kv_slot(place, plane), half)
+            push(ref, 2 + plane * 2 + half, kv_route(place, half, fp=1))
+            push(ref, 6 + plane * 4 + half, kv_route(place, half, fq=1))
+    for plane in (1, 0):
+        for half in range(2):
+            ref = block(kv_slot(kv_route(place, half, fp=1), plane), half)
+            waiter(ref, 2 + plane * 2 + half)
+            push(ref, 6 + plane * 4 + 2 + half, kv_route(place, half, fq=1))
+    for plane in (1, 0):
+        for fp in range(2):
+            for half in range(2):
+                ref = block(kv_slot(kv_route(place, half, fp, 1), plane), half)
+                waiter(ref, 6 + plane * 4 + fp * 2 + half)
+    for copy in started:
+        copy.wait_send()
+
+    @pl.when(z < 2)
+    def _():
+        own_push(0, 1 - z % 2).wait_send()
+        own_push(1, 2).wait_send()
+
+    @pl.when(z == 2)
+    def _():
+        relay(0).wait_send()
+        relay(1).wait_send()
+
+
+def gather_kv(key_value, collective_id):
+    return pl.pallas_call(
+        kv_gather_kernel,
+        in_specs=[pl.BlockSpec(memory_space=pl.ANY)],
+        out_specs=pl.BlockSpec(memory_space=pl.ANY),
+        out_shape=jax.ShapeDtypeStruct((PDEV,) + key_value.shape, key_value.dtype),
+        scratch_shapes=[
+            pltpu.SemaphoreType.DMA((14,)),
+            pltpu.SemaphoreType.DMA((14,)),
+            pltpu.SemaphoreType.DMA((1,)),
+        ],
+        compiler_params=pltpu.CompilerParams(collective_id=collective_id, has_side_effects=True),
+        name="gather_kv",
+    )(key_value)
+
+
+def kv_reduce_kernel(in_ref, out_ref, acc, q_box, p_box, z_box, send, recv):
+    place = chip_place()
+    z, y, x, g = place
+    greet(place)
+    started = []
+
+    def at_z(zz):
+        return (zz, y, x, g)
+
+    def mail(src, dst, index, coords):
+        copy = remote(src, dst, send.at[index], recv.at[index], coords)
+        copy.start()
+        started.append(copy)
+
+    def arrived(box, index):
+        remote(box, box, send.at[index], recv.at[index], near(place, fg=1)).wait_recv()
+        return box[...].astype(jnp.float32)
+
+    def slot(plane, half, fp=0, fq=0):
+        return kv_slot(kv_route(place, half, fp, fq), plane)
+
+    order = [(plane, half) for plane in (0, 1) for half in (0, 1)]
+    for fp in (1, 0):
+        for plane, half in order:
+            index = plane * 4 + fp * 2 + half
+            mail(
+                in_ref.at[slot(plane, half, fp, 1), half],
+                q_box.at[index],
+                index,
+                kv_route(place, half, fq=1),
+            )
+    for plane, half in order:
+        index = plane * 2 + half
+        box = q_box.at[plane * 4 + 2 + half]
+        total = in_ref[slot(plane, half, 1, 0), half].astype(jnp.float32) + arrived(
+            box, plane * 4 + 2 + half
+        )
+        acc[4 + index] = total.astype(acc.dtype)
+        mail(acc.at[4 + index], p_box.at[index], 8 + index, kv_route(place, half, fp=1))
+
+    def to_z(index, box, zz):
+        return remote(acc.at[index], z_box.at[box], send.at[12 + index], recv.at[12 + box], at_z(zz))
+
+    for plane, half in order:
+        index = plane * 2 + half
+        total = in_ref[slot(plane, half), half].astype(jnp.float32)
+        total = total + arrived(q_box.at[plane * 4 + half], plane * 4 + half)
+        total = total + arrived(p_box.at[index], 8 + index)
+
+        @pl.when(z == 2)
+        def _():
+            acc[index] = (total + arrived(z_box.at[index], 12 + index)).astype(acc.dtype)
+            to_z(index, half, plane).start()
+
+        @pl.when(z == 3)
+        def _():
+            acc[index] = total.astype(acc.dtype)
+            to_z(index, index, 2).start()
+
+        @pl.when(z == 1 - plane)
+        def _():
+            acc[index] = total.astype(acc.dtype)
+            to_z(index, 2 + half, plane).start()
+
+        @pl.when(z == plane)
+        def _():
+            out_ref[half] = total
+
+    @pl.when(z < 2)
+    def _():
+        for half in range(2):
+            first = arrived(z_box.at[2 + half], 14 + half)
+            second = arrived(z_box.at[half], 12 + half)
+            out_ref[half] = out_ref[half] + first + second
+
+    @pl.when(z >= 2)
+    def _():
+        out_ref[...] = jnp.zeros_like(out_ref)
+
+    for copy in started:
+        copy.wait_send()
+    for plane, half in order:
+        index = plane * 2 + half
+
+        @pl.when(z == 2)
+        def _():
+            to_z(index, half, plane).wait_send()
+
+        @pl.when(z == 3)
+        def _():
+            to_z(index, index, 2).wait_send()
+
+        @pl.when(z == 1 - plane)
+        def _():
+            to_z(index, 2 + half, plane).wait_send()
+
+
+def reduce_kv(terms, collective_id):
+    slab = terms.shape[2:]
+    return pl.pallas_call(
+        kv_reduce_kernel,
+        in_specs=[pl.BlockSpec(memory_space=pltpu.VMEM)],
+        out_specs=pl.BlockSpec(memory_space=pltpu.VMEM),
+        out_shape=jax.ShapeDtypeStruct(terms.shape[1:], jnp.float32),
+        scratch_shapes=[
+            pltpu.VMEM((8,) + slab, terms.dtype),
+            pltpu.VMEM((8,) + slab, terms.dtype),
+            pltpu.VMEM((4,) + slab, terms.dtype),
+            pltpu.VMEM((4,) + slab, terms.dtype),
+            pltpu.SemaphoreType.DMA((16,)),
+            pltpu.SemaphoreType.DMA((16,)),
+        ],
+        compiler_params=pltpu.CompilerParams(collective_id=collective_id, has_side_effects=True),
+        name="reduce_kv",
+    )(terms)
+
+
+def pack_small(flat, rows_above, columns):
+    shards, count = flat.shape
+    rows = -(-count // columns)
+    rows += -(rows_above + rows) % 8
+    flat = jnp.pad(flat, ((0, 0), (0, rows * columns - count)))
+    return flat.reshape(shards, rows, columns)
 
 
 def unpack_small(packed, sizes):
@@ -227,6 +713,7 @@
 
 
 def per_device(
+    direct,
     tokens,
     branch_points,
     qkv_weight,
@@ -257,9 +744,18 @@
         second_shift,
     ]
     sizes = [s.shape[0] for s in small]
-    head = jnp.concatenate([qkv_weight, pack_small(small, qkv_weight.shape[1])], axis=0)
-    head_all = lax.all_gather(head, AXES, axis=0, tiled=False)
-    qkv_rows = qkv_weight.shape[0]
+    qkv_rows, columns = qkv_weight.shape
+    packed = pack_small(jnp.concatenate(small)[None], qkv_rows, columns)[0]
+    head = jnp.concatenate([qkv_weight, packed], axis=0)
+    weights = (head, out_weight, up_weight, down_weight)
+    if direct:
+        gathered = gather_shards(weights, ROUTES, 0, "gather")
+    else:
+        gathered = [lax.all_gather(w, AXES, axis=0, tiled=False) for w in weights]
+    head_all, out_full, up_full, down_full = gathered
+    out_full = out_full.reshape(-1, out_full.shape[2])
+    up_full = up_full.reshape(-1, up_full.shape[2])
+    down_full = down_full.reshape(-1, down_full.shape[2])
     qkv_full = head_all[:, :qkv_rows].reshape(shards * qkv_rows, -1)
     (
         query_full,
@@ -271,10 +767,6 @@
         gain_two,
         shift_two,
     ) = [p.astype(jnp.float32) for p in unpack_small(head_all[:, qkv_rows:], sizes)]
-    out_full = lax.all_gather(out_weight, AXES, axis=0, tiled=True)
-    up_full = lax.all_gather(up_weight, AXES, axis=0, tiled=True)
-    down_full = lax.all_gather(down_weight, AXES, axis=0, tiled=True)
-
     block_index = lax.axis_index("tok")
     is_cont = block_index >= PDEV
     offsets = jnp.arange(row_count, dtype=jnp.int32)
@@ -297,8 +789,11 @@
     )
     key_value = turn(projected[:, width:], key_tables, 1.0).astype(jnp.bfloat16)
     prompt_len = PDEV * row_count
-    all_kv = lax.all_gather(key_value, "tok", axis=0, tiled=True)
-    keys_values = jnp.concatenate([all_kv[:prompt_len], key_value], axis=0)
+    if direct:
+        prompt_kv = gather_kv(key_value, 1).reshape(prompt_len, 2 * HDIM)
+    else:
+        prompt_kv = lax.all_gather(key_value, "tok", axis=0, tiled=True)[:prompt_len]
+    keys_values = jnp.concatenate([prompt_kv, key_value], axis=0)
 
     grad_rows = cotangent[0]
     grad_float = grad_rows.astype(jnp.float32)
@@ -309,15 +804,18 @@
     context_low, d_query, d_keys_t, d_values_t = attention(
         queries, d_context, keys_values, limit
     )
-    kv_terms = jnp.concatenate([d_keys_t, d_values_t], axis=0).T
-    own_term = kv_terms[prompt_len:]
-    group_rows = row_count * lax.axis_size("tok")
-    sent = jnp.pad(
-        kv_terms[:prompt_len].astype(jnp.bfloat16), ((0, group_rows - prompt_len), (0, 0))
-    )
-    kv_grad = own_term + lax.psum_scatter(
-        sent, "tok", scatter_dimension=0, tiled=True
-    ).astype(jnp.float32)
+    kv_terms = jnp.stack([d_keys_t, d_values_t])
+    own_term = kv_terms[:, :, prompt_len:]
+    sent = kv_terms[:, :, :prompt_len].astype(jnp.bfloat16)
+    sent = sent.reshape(2, HDIM, PDEV, row_count).transpose(2, 0, 1, 3)
+    if direct:
+        summed = reduce_kv(sent, 2)
+    else:
+        idle = lax.axis_size("tok") - PDEV
+        sent = jnp.pad(sent, ((0, idle), (0, 0), (0, 0), (0, 0)))
+        summed = lax.psum_scatter(sent, "tok", scatter_dimension=0, tiled=False)
+        summed = summed.astype(jnp.float32)
+    kv_grad = (own_term + summed).reshape(2 * HDIM, row_count).T
 
     pre_act = matmul(second_low, up_full, (((1,), (0,)), ((), ()))) + up_bias_full
     hidden, gelu_back = jax.vjp(partial(jax.nn.gelu, approximate=False), pre_act)
@@ -361,27 +859,22 @@
         grad_shift_two,
     ]
     grad_sizes = [g.shape[0] // shards for g in small_grads]
-    small_flat = jnp.concatenate(
-        [g.reshape(shards, -1) for g in small_grads], axis=1
-    )
-    columns = qkv_weight.shape[1]
-    small_rows = -(-small_flat.shape[1] // columns)
-    small_flat = jnp.pad(
-        small_flat, ((0, 0), (0, small_rows * columns - small_flat.shape[1]))
-    ).reshape(shards, small_rows, columns)
-    tail = jnp.concatenate(
-        [grad_qkv_w.reshape(shards, qkv_rows, columns), small_flat], axis=1
-    )
-
-    def scattered(term):
-        return lax.psum_scatter(
-            term.astype(jnp.bfloat16), AXES, scatter_dimension=0, tiled=True
-        ).astype(jnp.float32)
-
-    sum_up_w = scattered(grad_up_w)
-    sum_down_w = scattered(grad_down_w)
-    sum_out_w = scattered(grad_out_w)
-    sum_tail = scattered(tail)[0]
+    small_flat = jnp.concatenate([g.reshape(shards, -1) for g in small_grads], axis=1)
+    small_flat = pack_small(small_flat, qkv_rows, columns)
+
+    def by_shard(term):
+        return term.astype(jnp.bfloat16).reshape(shards, -1, term.shape[1])
+
+    tail = jnp.concatenate([by_shard(grad_qkv_w), small_flat.astype(jnp.bfloat16)], axis=1)
+    terms = (tail, by_shard(grad_out_w), by_shard(grad_up_w), by_shard(grad_down_w))
+    if direct:
+        sums = reduce_shards(terms, ROUTES, 3, "reduce")
+    else:
+        sums = [
+            lax.psum_scatter(t, AXES, scatter_dimension=0, tiled=False).astype(jnp.float32)
+            for t in terms
+        ]
+    sum_tail, sum_out_w, sum_up_w, sum_down_w = sums
     sum_qkv_w = sum_tail[:qkv_rows]
     (
         sum_query_b,
@@ -412,6 +905,7 @@
 
 
 def solution(mesh):
+    direct = dict(mesh.shape) == {"grp": 2, "tok": 4 * Z_CHIPS}
     placed = (
         P("grp", "tok", None),
         P("grp", "tok"),
@@ -430,7 +924,7 @@
         P("grp", "tok", None),
     )
     return jax.shard_map(
-        per_device,
+        partial(per_device, direct),
         mesh=mesh,
         in_specs=placed,
         out_specs=(

time: 884 us -> 433 us (0.49)
  waiting for transfers between devices: 612 us -> 0 us
  Pallas kernels: 109 us -> 304 us
  between operations: 16 us -> 2.74 us
  other arithmetic: 30.4 us -> 18.6 us
  matrix products: 69.4 us -> 59.2 us
    reduce_scatter x5 -> x0, waiting for transfers between devices: 466 us -> none  [the longest x4 421 us: scattered(): lax.psum_scatter(term.astype(jnp.bfloat16), AXES, scatter_dimension=0, ti...]
    pallas_call x0 -> x4, Pallas kernels: none -> 195 us  [the longest x1 77.8 us: reduce_shards(): pl.pallas_call(partial(reduce_kernel, orders), in_specs=[pl.BlockSpec(mem...]
    all_gather x5 -> x0, waiting for transfers between devices: 144 us -> none  [the longest x1 54.2 us: per_device(): head_all = lax.all_gather(head, AXES, axis=0, tiled=False)]
  transfers between devices with their start and end apart: 10 -> 0, of which waited for: 8 -> 0; matrix products, arithmetic and copies ran while one was open for 14% -> 0% of each run, Pallas kernels for 12% -> 0%
where the time goes in v2:
time: 433 us; the launch traced here: 426 us
  Pallas kernels  304 us (70%)
  matrix products  59.2 us (14%)
  local copies, waits for them, and re-layouts  41 us (9%)
  other arithmetic  18.6 us (4%)
    pallas_call x1, Pallas kernels, attention(): pl.pallas_call(partial(attention_kernel, key_count), grid=(width // pair,...  109 us
    pallas_call x1, Pallas kernels, reduce_shards(): pl.pallas_call(partial(reduce_kernel, orders), in_specs=[pl.BlockSpec(mem...  77.8 us
    pallas_call x1, Pallas kernels, gather_shards(): pl.pallas_call(partial(gather_kernel, orders), in_specs=[pl.BlockSpec(mem...  71.2 us
    pallas_call x1, Pallas kernels, reduce_kv(): pl.pallas_call(kv_reduce_kernel, in_specs=[pl.BlockSpec(memory_space=pltp...  25.9 us
    pallas_call x1, Pallas kernels, gather_kv(): pl.pallas_call(kv_gather_kernel, in_specs=[pl.BlockSpec(memory_space=pl.A...  19.8 us
    dot_general x1, matrix products, per_device(): matmul(second_low, up_full, (((1,), (0,)), ((), ()))) + up_bias_full  18.7 us
    unnamed x130, local copies, waits for them, and re-layouts  10.3 us
    another operation x6, local copies, waits for them, and re-layouts, turn(): own, from_right, from_left = (jnp.tile(t, (1, reps)) for t in tables)  9.28 us

profile of v2, /device:TPU:0, one launch (start us, length us, event | category | flops | bytes accessed | tf_op | source)
XLA Modules:
  0.0 425.6 jit_solution(10813637993712509550)
XLA Ops:
  0.7 5.5 %concatenate.54 = bf16[264]{0:T(512)(128)(2,1)S(1)} concatenate(bf16[24]{0:T(256)(128)(2,1)} %param.21, bf16[24]{0:T(256)(128)(2,1)} %param.22, bf16[96]{0:T(256)(128)(2,1)} %param.23, bf16[24]{0:T(256)(128)(2,1)} %param.24, bf16[24]{0:T(256)(128)(2,1)} %param.25, bf16[24]{0:T(256)(128)(2,1)} %param.26, bf16[24]{0:T(256)(128)(2,1)} %param.27, bf16[24]{0:T(256)(128)(2,1)} %param.28), dimensions={0} | concatenate | bytes 1056 | tf_op jit(solution)/shard_map/concatenate | solution.py:748
  7.7 71.2 %gather.1 = (bf16[32,32,896]{2,1,0:T(8,128)(2,1)}, bf16[32,24,768]{2,1,0:T(8,128)(2,1)}, bf16[32,24,3072]{2,1,0:T(8,128)(2,1)}, bf16[32,96,768]{2,1,0:T(8,128)(2,1)}) custom-call(bf16[32,896]{1,0:T(8,128)(2,1)} %pad_maximum_fusion.8.refs_0_, bf16[24,768]{1,0:T(8,128)(2,1)} %refs_1_.1, bf16[24,3072]{1,0:T(8,128)(2,1)} %refs_2_.1, bf16[96,768]{1,0:T(8,128)(2,1)} %refs_3_.1), custom_call_target="tpu_custom_call" | custom-call | tf_op jit(solution)/shard_map/gather/pallas_call | solution.py:346
  87.7 19.8 %gather_kv.1 = bf16[8,512,128]{2,1,0:T(8,128)(2,1)} custom-call(bf16[512,128]{1,0:T(8,128)(2,1)} %copy.54.kv_ref), custom_call_target="tpu_custom_call" | custom-call | tf_op jit(solution)/shard_map/gather_kv/pallas_call | solution.py:564
  115.0 2.3 tile.26
  117.2 1.9 copy.46
  120.5 3.1 copy.47
  127.2 1.8 fusion.83.q_ref
  129.0 2.0 convolution_bitcast_fusion.dc_ref
  131.6 109.3 %attention.1 = (bf16[512,768]{1,0:T(8,128)(2,1)}, f32[512,768]{1,0:T(8,128)}, f32[64,4608]{1,0:T(8,128)}, f32[64,4608]{1,0:T(8,128)}) custom-call(bf16[512,768]{1,0:T(8,128)(2,1)} %fusion.83.q_ref, f32[512,768]{1,0:T(8,128)} %convolution_bitcast_fusion.dc_ref, bf16[4608,128]{1,0:T(8,128)(2,1)} %copy.56.k2_ref, bf16[128,4608]{1,0:T(8,128)(2,1)} %get-tuple-element.101.k2t_ref, ...), custom_call_target="tpu_custom_call" | custom-call | flops 21743271936 | bytes 12582912 | tf_op jit(solution)/shard_map/attention/pallas_call | solution.py:177
  241.0 2.5 fusion.119
  243.6 1.8 fusion.114
  246.7 25.9 %reduce_kv.1 = f32[2,64,512]{2,1,0:T(8,128)} custom-call(bf16[8,2,64,512]{3,2,1,0:T(8,128)(2,1)} %bitcast.210), custom_call_target="tpu_custom_call" | custom-call | tf_op jit(solution)/shard_map/reduce_kv/pallas_call | solution.py:678
  275.1 2.3 convolution_convert_fusion.2
  278.5 18.7 %multiply_convert_fusion = (bf16[512,3072]{1,0:T(8,128)(2,1)}, f32[512,3072]{1,0:T(8,128)S(1)}, f32[512,3072]{1,0:T(8,128)S(1)}) fusion(f32[3072]{0:T(1024)S(1)} %reshape.458, bf16[768,3072]{1,0:T(8,128)(2,1)} %bitcast.230, bf16[1,512,768]{2,1,0:T(8,128)(2,1)S(1)} %copy-done.3, f32[768]{0:T(1024)S(1)} %reshape.457, f32[768]{0:T(1024)S(1)} %reshape.456, ...), kind=kOutput, calls=%fused_computation.11 | convolution fusion | flops 2522087424 | bytes 21256192 | tf_op jit(solution)/shard_map/dot_general | solution.py:820
  297.2 6.8 %fusion.125 = (bf16[3072]{0:T(1024)(128)(2,1)S(1)}, bf16[512,3072]{1,0:T(8,128)(2,1)S(1)}) fusion(f32[512,3072]{1,0:T(8,128)S(1)} %get-tuple-element.82, bf16[3072,768]{1,0:T(8,128)(2,1)} %bitcast.228, bf16[1,512,768]{2,1,0:T(8,128)(2,1)S(1)} %copy-done.13, f32[512,3072]{1,0:T(8,128)S(1)} %get-tuple-element.128, f32[3072]{0:T(1024)S(1)} %reshape.458), kind=kOutput, calls=%fused_computation.203 | convolution fusion | flops 2441081856 | bytes 21252096 | tf_op jit(solution)/shard_map/dot_general | solution.py:834
  304.0 6.1 %fusion.127 = f32[512,768]{1,0:T(8,128)S(1)} fusion(bf16[512,3072]{1,0:T(8,128)(2,1)S(1)} %get-tuple-element.131, bf16[768,3072]{1,0:T(8,128)(2,1)} %bitcast.231), kind=kOutput, calls=%fused_computation.205 | convolution fusion | flops 2415919104 | bytes 9437184 | tf_op jit(solution)/shard_map/dot_general | solution.py:847
  316.6 1.8 convolution_convert_fusion.3
  318.8 4.8 %convolution_convert_fusion.1 = bf16[768,3072]{1,0:T(8,128)(2,1)} fusion(bf16[512,3072]{1,0:T(8,128)(2,1)S(1)} %copy-done.57, bf16[1,512,768]{2,1,0:T(8,128)(2,1)S(1)} %copy-done.3, f32[768]{0:T(1024)S(1)} %reshape.457, f32[768]{0:T(1024)S(1)} %reshape.456, f32[512]{0:T(512)S(1)} %copy-done.37, f32[512]{0:T(512)S(1)} %copy-done.35), kind=kOutput, calls=%fused_computation.26 | convolution fusion | flops 2420637696 | bytes 8660992 | tf_op jit(solution)/shard_map/dot_general | solution.py:839
  323.6 4.6 %convolution_convert_fusion = bf16[3072,768]{1,0:T(8,128)(2,1)} fusion(bf16[512,3072]{1,0:T(8,128)(2,1)S(1)} %copy-done.54, bf16[1,512,768]{2,1,0:T(8,128)(2,1)S(1)} %copy-done.13), kind=kOutput, calls=%fused_computation.25 | convolution fusion | flops 2418278400 | bytes 8650752 | tf_op jit(solution)/shard_map/dot_general | solution.py:840
  328.2 77.8 %reduce.10 = (f32[32,896]{1,0:T(8,128)}, f32[24,768]{1,0:T(8,128)}, f32[24,3072]{1,0:T(8,128)}, f32[96,768]{1,0:T(8,128)}) custom-call(bf16[32,32,896]{2,1,0:T(8,128)(2,1)} %pad_maximum_fusion.1.refs_0_, bf16[32,24,768]{2,1,0:T(8,128)(2,1)} %bitcast.222, bf16[32,24,3072]{2,1,0:T(8,128)(2,1)} %bitcast.204, bf16[32,96,768]{2,1,0:T(8,128)(2,1)} %bitcast.205), custom_call_target="tpu_custom_call" | custom-call | tf_op jit(solution)/shard_map/reduce/pallas_call | solution.py:450
  406.0 1.5 slice.176
  409.5 2.0 add_bitcast_fusion
  411.9 6.3 %fusion.126 = f32[512,768]{1,0:T(8,128)} fusion(bf16[512,3072]{1,0:T(8,128)(2,1)S(1)} %copy-done.55, bf16[3072,768]{1,0:T(8,128)(2,1)} %bitcast.229), kind=kOutput, calls=%fused_computation.204 | convolution fusion | flops 2415919104 | bytes 9437184 | tf_op jit(solution)/shard_map/dot_general | solution.py:830
  418.4 3.4 fusion.54
  (201 shorter events, 39.5 us)
Async XLA Ops:
  0.6 81.0 %copy-start.2 = (bf16[1,512,768]{2,1,0:T(8,128)(2,1)S(1)}, bf16[1,512,768]{2,1,0:T(8,128)(2,1)}, u32[]{:S(2)}) copy-start(bf16[1,512,768]{2,1,0:T(8,128)(2,1)} %param.15) | copy-start | bytes 2359300
  85.9 21.6 %copy-start.24 = (f32[512,8]{0,1:T(8,128)}, f32[512,8]{0,1:T(8,128)S(1)}, u32[]{:S(2)}) copy-start(f32[512,8]{0,1:T(8,128)S(1)} %get-tuple-element.125) | copy-start | bytes 49156
  85.9 21.6 %copy-start.42 = (pred[128]{0:T(512)(128)(4,1)}, pred[128]{0:T(512)(128)(4,1)S(1)}, u32[]{:S(2)}) copy-start(pred[128]{0:T(512)(128)(4,1)S(1)} %get-tuple-element.132) | copy-start | bytes 388
  85.9 21.6 %copy-start.44 = (pred[128]{0:T(512)(128)(4,1)}, pred[128]{0:T(512)(128)(4,1)S(1)}, u32[]{:S(2)}) copy-start(pred[128]{0:T(512)(128)(4,1)S(1)} %get-tuple-element.133) | copy-start | bytes 388
  85.9 21.5 %copy-start.46 = (pred[128]{0:T(512)(128)(4,1)}, pred[128]{0:T(512)(128)(4,1)S(1)}, u32[]{:S(2)}) copy-start(pred[128]{0:T(512)(128)(4,1)S(1)} %get-tuple-element.134) | copy-start | bytes 388
  86.0 21.5 %copy-start.48 = (pred[128]{0:T(512)(128)(4,1)}, pred[128]{0:T(512)(128)(4,1)S(1)}, u32[]{:S(2)}) copy-start(pred[128]{0:T(512)(128)(4,1)S(1)} %get-tuple-element.135) | copy-start | bytes 388
  120.5 3.1 copy-start.31
  241.0 2.5 copy-start
  245.6 27.0 %copy-start.9 = (f32[64,4608]{1,0:T(8,128)S(1)}, f32[64,4608]{1,0:T(8,128)}, u32[]{:S(2)}) copy-start(f32[64,4608]{1,0:T(8,128)} %get-tuple-element.33) | copy-start | bytes 3538948
  245.6 27.0 %copy-start.11 = (f32[64,4608]{1,0:T(8,128)S(1)}, f32[64,4608]{1,0:T(8,128)}, u32[]{:S(2)}) copy-start(f32[64,4608]{1,0:T(8,128)} %get-tuple-element.34) | copy-start | bytes 3538948
  275.1 2.4 copy-start.29
  278.4 18.7 %copy-start.13 = (bf16[1,512,768]{2,1,0:T(8,128)(2,1)S(1)}, bf16[1,512,768]{2,1,0:T(8,128)(2,1)}, u32[]{:S(2)}) copy-start(bf16[1,512,768]{2,1,0:T(8,128)(2,1)} %param.29) | copy-start | bytes 2359300
  304.0 6.2 %copy-start.56 = (bf16[512,3072]{1,0:T(8,128)(2,1)}, bf16[512,3072]{1,0:T(8,128)(2,1)S(1)}, u32[]{:S(2)}) copy-start(bf16[512,3072]{1,0:T(8,128)(2,1)S(1)} %get-tuple-element.131) | copy-start | bytes 9437188
  304.0 6.2 %copy-start.17 = (bf16[32,24,896]{2,1,0:T(8,128)(2,1)S(1)}, bf16[32,24,896]{2,1,0:T(8,128)(2,1)}, u32[]{:S(2)}) copy-start(bf16[32,24,896]{2,1,0:T(8,128)(2,1)} %copy-done.16) | copy-start | bytes 4128772
  304.0 6.2 %copy-start.20 = (bf16[512,768]{1,0:T(8,128)(2,1)S(1)}, bf16[512,768]{1,0:T(8,128)(2,1)}, u32[]{:S(2)}) copy-start(bf16[512,768]{1,0:T(8,128)(2,1)} %get-tuple-element.80) | copy-start | bytes 2359300
  318.8 4.8 %copy-start.54 = (bf16[512,3072]{1,0:T(8,128)(2,1)S(1)}, bf16[512,3072]{1,0:T(8,128)(2,1)}, u32[]{:S(2)}) copy-start(bf16[512,3072]{1,0:T(8,128)(2,1)} %get-tuple-element.81) | copy-start | bytes 9437188
  328.2 81.4 %copy-start.7 = (f32[512,768]{1,0:T(8,128)S(1)}, f32[512,768]{1,0:T(8,128)}, u32[]{:S(2)}) copy-start(f32[512,768]{1,0:T(8,128)} %copy-done.6) | copy-start | bytes 4718596
  409.0 13.6 %copy-start.50 = (f32[24]{0:T(128)}, f32[24]{0:T(128)S(1)}, u32[]{:S(2)}) copy-start(f32[24]{0:T(128)S(1)} %get-tuple-element.189) | copy-start | bytes 292
  411.9 6.3 %copy-start.28 = (f32[32,24]{1,0:T(8,128)S(1)}, f32[32,24]{1,0:T(8,128)}, u32[]{:S(2)}) copy-start(f32[32,24]{1,0:T(8,128)} %get-tuple-element.103) | copy-start | bytes 9220
  411.9 6.4 %copy-start.27 = (f32[32,24]{1,0:T(8,128)S(1)}, f32[32,24]{1,0:T(8,128)}, u32[]{:S(2)}) copy-start(f32[32,24]{1,0:T(8,128)} %get-tuple-element.104) | copy-start | bytes 9220
  411.9 6.5 %copy-start.52 = (bf16[32,24,768]{2,1,0:T(8,128)(2,1)S(1)}, bf16[32,24,768]{2,1,0:T(8,128)(2,1)}, u32[]{:S(2)}) copy-start(bf16[32,24,768]{2,1,0:T(8,128)(2,1)} %get-tuple-element.28) | copy-start | bytes 3538948
  418.3 4.7 %copy-start.26 = (f32[24,768]{1,0:T(8,128)S(1)}, f32[24,768]{1,0:T(8,128)}, u32[]{:S(2)}) copy-start(f32[24,768]{1,0:T(8,128)} %get-tuple-element.185) | copy-start | bytes 221188
  418.3 5.4 %copy-start.23 = (f32[24,3072]{1,0:T(8,128)S(1)}, f32[24,3072]{1,0:T(8,128)}, u32[]{:S(2)}) copy-start(f32[24,3072]{1,0:T(8,128)} %get-tuple-element.186) | copy-start | bytes 884740
  418.3 6.1 %copy-start.22 = (f32[96,768]{1,0:T(8,128)S(1)}, f32[96,768]{1,0:T(8,128)}, u32[]{:S(2)}) copy-start(f32[96,768]{1,0:T(8,128)} %get-tuple-element.187) | copy-start | bytes 884740
  (34 other events, 49.6 us)

commit v3 on v2

--- a/solution.py
+++ b/solution.py
@@ -50,168 +50,9 @@
     )
 
 
-def attention_kernel(
-    key_count,
-    q_ref,
-    dc_ref,
-    k2_ref,
-    k2t_ref,
-    v2_ref,
-    v2t_ref,
-    bias_ref,
-    ctx_ref,
-    dq_ref,
-    dkt_ref,
-    dvt_ref,
-    s_ref,
-    e_ref,
-):
-    rows = q_ref.shape[0]
-    pair = 2 * HDIM
-    prompt = key_count - rows
-    unroll = 4
-
-    @pl.when(pl.program_id(0) == 0)
-    def _():
-        dkt_ref[...] = jnp.zeros_like(dkt_ref)
-        dvt_ref[...] = jnp.zeros_like(dvt_ref)
-
-    first_head = lax.broadcasted_iota(jnp.int32, (rows, pair), 1) < HDIM
-
-    def stacked(both):
-        return jnp.concatenate(
-            [jnp.where(first_head, both, 0.0), jnp.where(first_head, 0.0, both)], axis=0
-        ).astype(jnp.bfloat16)
-
-    def turned(both):
-        flipped = both.T.astype(jnp.bfloat16)
-        return jnp.concatenate([flipped[:HDIM], flipped[HDIM:]], axis=1)
-
-    q_both = q_ref[...].astype(jnp.float32)
-    q_rows = stacked(q_both)
-    q_cols = turned(q_both)
-
-    def lane_max(top, scores):
-        for j in range(scores.shape[1] // pair):
-            top = jnp.maximum(top, scores[:, j * pair : (j + 1) * pair])
-        return top
-
-    def score_step(c, top):
-        cols = pl.ds(pl.multiple_of(c * CHUNK, CHUNK), CHUNK)
-        scores = jnp.dot(q_rows, k2t_ref[:, cols], preferred_element_type=jnp.float32)
-        scores = scores + bias_ref[0:1, cols]
-        s_ref[:, cols] = scores
-        return lane_max(top, scores)
-
-    top = lax.fori_loop(
-        0,
-        prompt // CHUNK,
-        score_step,
-        jnp.full((2 * rows, pair), NEGATIVE, jnp.float32),
-        unroll=unroll,
-    )
-    row_id = lax.broadcasted_iota(jnp.int32, (2 * rows, rows), 0) % rows
-    col_id = lax.broadcasted_iota(jnp.int32, (2 * rows, rows), 1)
-    scores = jnp.dot(q_rows, k2t_ref[:, prompt:], preferred_element_type=jnp.float32)
-    scores = jnp.where(col_id <= row_id, scores, NEGATIVE)
-    s_ref[:, prompt:] = scores
-    top = jnp.max(lane_max(top, scores), axis=1, keepdims=True)
-
-    def weight_step(c, carry):
-        total, mixed = carry
-        cols = pl.ds(pl.multiple_of(c * CHUNK, CHUNK), CHUNK)
-        weights = jnp.exp(s_ref[:, cols] - top)
-        for j in range(CHUNK // pair):
-            total = total + weights[:, j * pair : (j + 1) * pair]
-        low = weights.astype(jnp.bfloat16)
-        e_ref[:, cols] = low
-        mixed = mixed + jnp.dot(low, v2_ref[cols, :], preferred_element_type=jnp.float32)
-        return total, mixed
-
-    zero = jnp.zeros((2 * rows, pair), jnp.float32)
-    total, mixed = lax.fori_loop(
-        0, key_count // CHUNK, weight_step, (zero, zero), unroll=unroll
-    )
-    scale = 1.0 / jnp.sum(total, axis=1, keepdims=True)
-    mixed = mixed * scale
-    context = jnp.where(first_head, mixed[:rows], mixed[rows:])
-    ctx_ref[...] = context.astype(ctx_ref.dtype)
-    d_context = dc_ref[...]
-    product = d_context * context
-    delta_a = jnp.sum(jnp.where(first_head, product, 0.0), axis=1, keepdims=True)
-    delta_b = jnp.sum(jnp.where(first_head, 0.0, product), axis=1, keepdims=True)
-    delta = jnp.concatenate([delta_a, delta_b], axis=0) * scale
-    d_both = d_context * jnp.where(first_head, scale[:rows], scale[rows:])
-    d_rows = stacked(d_both)
-    d_cols = turned(d_both)
-
-    def grad_step(c, d_query):
-        cols = pl.ds(pl.multiple_of(c * CHUNK, CHUNK), CHUNK)
-        d_probs = jnp.dot(d_rows, v2t_ref[:, cols], preferred_element_type=jnp.float32)
-        low = e_ref[:, cols]
-        d_scores = (low.astype(jnp.float32) * (d_probs - delta)).astype(jnp.bfloat16)
-        dvt_ref[:, cols] += jnp.dot(d_cols, low, preferred_element_type=jnp.float32)
-        dkt_ref[:, cols] += jnp.dot(q_cols, d_scores, preferred_element_type=jnp.float32)
-        return d_query + jnp.dot(d_scores, k2_ref[cols, :], preferred_element_type=jnp.float32)
-
-    d_query = lax.fori_loop(0, key_count // CHUNK, grad_step, zero, unroll=unroll)
-    dq_ref[...] = jnp.where(first_head, d_query[:rows], d_query[rows:]) * SCORE_SCALE
-
-
-def attention(queries, d_context, keys_values, limit):
-    key_count = keys_values.shape[0]
-    rows, width = queries.shape
-    pair = 2 * HDIM
-    keys = keys_values[:, :HDIM]
-    values = keys_values[:, HDIM:]
-    k2 = jnp.concatenate([keys, keys], axis=1)
-    v2 = jnp.concatenate([values, values], axis=1)
-    column = jnp.arange(key_count, dtype=jnp.int32)
-    shown = jnp.logical_or(column < limit, column >= key_count - rows)
-    bias = jnp.broadcast_to(jnp.where(shown, 0.0, NEGATIVE)[None], (8, key_count))
-
-    def whole(*shape):
-        return pl.BlockSpec(shape, lambda i: (0, 0))
-
-    block = pl.BlockSpec((rows, pair), lambda i: (0, i))
-    return pl.pallas_call(
-        partial(attention_kernel, key_count),
-        grid=(width // pair,),
-        in_specs=[
-            block,
-            block,
-            whole(key_count, pair),
-            whole(pair, key_count),
-            whole(key_count, pair),
-            whole(pair, key_count),
-            whole(8, key_count),
-        ],
-        out_specs=[block, block, whole(HDIM, key_count), whole(HDIM, key_count)],
-        out_shape=[
-            jax.ShapeDtypeStruct((rows, width), jnp.bfloat16),
-            jax.ShapeDtypeStruct((rows, width), jnp.float32),
-            jax.ShapeDtypeStruct((HDIM, key_count), jnp.float32),
-            jax.ShapeDtypeStruct((HDIM, key_count), jnp.float32),
-        ],
-        scratch_shapes=[
-            pltpu.VMEM((2 * rows, key_count), jnp.float32),
-            pltpu.VMEM((2 * rows, key_count), jnp.bfloat16),
-        ],
-        compiler_params=pltpu.CompilerParams(
-            dimension_semantics=("arbitrary",), vmem_limit_bytes=58 << 20
-        ),
-        cost_estimate=pl.CostEstimate(
-            flops=12 * rows * width * key_count,
-            bytes_accessed=8 * rows * width + 16 * key_count * pair,
-            transcendentals=rows * HEADS * key_count,
-        ),
-        name="attention",
-    )(queries, d_context, k2, k2.T, v2, v2.T, bias)
-
-
 MESH = pl.DeviceIdType.MESH
 Z_CHIPS = 4
-ROUTES = ("yx", "xy", "yx", "xy")
+ROUTES = ("yx", "xy")
 SLABS = 32
 
 
@@ -268,26 +109,27 @@
         self.send, self.recv, self.local = send, recv, local
         self.started = []
 
-    def push(self, a, src, slot, index, coords):
-        copy = remote(
-            src, self.outs[a].at[slot], self.send.at[a, index], self.recv.at[a, index], coords
-        )
-        copy.start()
-        self.started.append(copy)
+    def push(self, a, slab, index, target):
+        def build():
+            place, order = self.place, self.orders[a]
+            slot = slot_at(near_pq(place, order, *slab))
+            dst = self.outs[a].at[slot]
+            src = self.ins[a] if slab == (0, 0, 0) else dst
+            return remote(src, dst, self.send.at[a, index], self.recv.at[a, index], target())
+
+        build().start()
+        self.started.append(build)
 
     def spread(self, a, k, fp, fq):
-        place, order = self.place, self.orders[a]
-        slot = slot_at(near_pq(place, order, k, fp, fq))
-        own = k == 0 and fp == 0 and fq == 0
-        src = self.ins[a] if own else self.outs[a].at[slot]
-        if own:
+        place, order, slab = self.place, self.orders[a], (k, fp, fq)
+        if slab == (0, 0, 0):
             for j in (1, 2, 3):
-                self.push(a, src, slot, j * 4, near(place, k=j))
+                self.push(a, slab, j * 4, partial(near, place, k=j))
         if fp == 0 and fq == 0:
-            self.push(a, src, slot, k * 4 + 2, near_pq(place, order, fp=1))
+            self.push(a, slab, k * 4 + 2, partial(near_pq, place, order, fp=1))
         if fq == 0:
-            self.push(a, src, slot, k * 4 + fp * 2 + 1, near_pq(place, order, fq=1))
-        self.push(a, src, slot, 16 + k * 4 + fp * 2 + fq, near(place, fg=1))
+            self.push(a, slab, k * 4 + fp * 2 + 1, partial(near_pq, place, order, fq=1))
+        self.push(a, slab, 16 + k * 4 + fp * 2 + fq, partial(near, place, fg=1))
 
     def arrived(self, a, k, fp, fq, fg=0):
         slot = slot_at(near_pq(self.place, self.orders[a], k, fp, fq, fg))
@@ -319,8 +161,8 @@
                 for fp in range(2):
                     for fq in range(2):
                         self.arrived(a, k, fp, fq, 1)
-        for copy in self.started:
-            copy.wait_send()
+        for build in self.started:
+            build().wait_send()
 
 
 Z_SLABS = [(1, 0, 0), (2, 0, 0), (3, 0, 0)]
@@ -365,12 +207,16 @@
         self.send, self.recv, self.local = send, recv, local
         self.started = []
 
-    def mail(self, a, src, index, coords):
-        copy = remote(
-            src, self.boxes[a].at[index], self.send.at[a, index], self.recv.at[a, index], coords
-        )
-        copy.start()
-        self.started.append(copy)
+    def mail(self, a, src, index, target):
+        def build():
+            box = self.boxes[a].at[index]
+            return remote(src(), box, self.send.at[a, index], self.recv.at[a, index], target())
+
+        build().start()
+        self.started.append(build)
+
+    def far_term(self, a, slab):
+        return self.ins[a].at[slot_at(near_pq(self.place, self.orders[a], *slab, 1))]
 
     def load(self, a, k, fp, fq):
         slot = slot_at(near_pq(self.place, self.orders[a], k, fp, fq))
@@ -382,9 +228,9 @@
     def begin(self, arrays, slabs):
         for k, fp, fq in slabs:
             for a in arrays:
-                slot = slot_at(near_pq(self.place, self.orders[a], k, fp, fq, 1))
                 sid = k * 4 + fp * 2 + fq
-                self.mail(a, self.ins[a].at[slot], sid, near(self.place, fg=1))
+                src = partial(self.far_term, a, (k, fp, fq))
+                self.mail(a, src, sid, partial(near, self.place, fg=1))
                 self.load(a, k, fp, fq).start()
 
     def arrived(self, a, index):
@@ -409,17 +255,25 @@
             self.outs[a][...] = total
             return
         self.accs[a][sid] = total.astype(jnp.bfloat16)
-        src = self.accs[a].at[sid]
+
+        def src():
+            return self.accs[a].at[sid]
+
         if fq == 1:
-            self.mail(a, src, 16 + k * 2 + fp, near_pq(place, order, fq=1))
+            self.mail(a, src, 16 + k * 2 + fp, partial(near_pq, place, order, fq=1))
         elif fp == 1:
-            self.mail(a, src, 24 + k, near_pq(place, order, fp=1))
+            self.mail(a, src, 24 + k, partial(near_pq, place, order, fp=1))
         else:
-            self.mail(a, src, 27 + k, near(place, k=k))
+            self.mail(a, src, 27 + k, partial(near, place, k=k))
+
+    def steps(self, arrays, slabs):
+        for slab in slabs:
+            for a in arrays:
+                self.step(a, *slab)
 
     def finish(self):
-        for copy in self.started:
-            copy.wait_send()
+        for build in self.started:
+            build().wait_send()
 
 
 SUM_SLABS = (
@@ -439,9 +293,7 @@
     reduce = Reduce(place, orders, ins, outs, accs, boxes, send, recv, local)
     arrays = range(n)
     reduce.begin(arrays, SUM_SLABS)
-    for slab in SUM_SLABS:
-        for a in arrays:
-            reduce.step(a, *slab)
+    reduce.steps(arrays, SUM_SLABS)
     reduce.finish()
 
 
@@ -691,6 +543,301 @@
         compiler_params=pltpu.CompilerParams(collective_id=collective_id, has_side_effects=True),
         name="reduce_kv",
     )(terms)
+
+
+def attention_kernel(last, plan, counts, *refs):
+    inputs, outputs, comm_ins, comm_outs = counts
+    q_ref, dc_ref, k2_ref, k2t_ref, v2_ref, v2t_ref, bias_ref = refs[:7]
+    carried = refs[7:inputs]
+    cut = inputs + comm_ins
+    ctx_ref, dq_ref = refs[cut : cut + 2]
+    results = refs[cut + 2 : cut + outputs]
+    scratch = refs[cut + outputs + comm_outs :]
+    s_ref, e_ref = scratch[:2]
+    if last:
+        dkt_ref, dvt_ref = scratch[2:4]
+        comm_scratch = scratch[4:]
+    else:
+        dkt_ref, dvt_ref = results
+        comm_scratch = scratch[2:]
+    rows = q_ref.shape[0]
+    key_count = k2_ref.shape[0]
+    pair = 2 * HDIM
+    prompt = key_count - rows
+    unroll = 4
+    step = pl.program_id(0)
+    events = {}
+    if plan is not None:
+        events = plan(refs[inputs:cut], refs[cut + outputs : cut + outputs + comm_outs], comm_scratch)
+
+    def point(index):
+        for at_step, at_point in sorted(events):
+            if at_point == index:
+                pl.when(step == at_step)(events[at_step, at_point])
+
+    @pl.when(step == 0)
+    def _():
+        if carried:
+            dkt_ref[...] = carried[0][...]
+            dvt_ref[...] = carried[1][...]
+        else:
+            dkt_ref[...] = jnp.zeros_like(dkt_ref)
+            dvt_ref[...] = jnp.zeros_like(dvt_ref)
+
+    point(0)
+    first_head = lax.broadcasted_iota(jnp.int32, (rows, pair), 1) < HDIM
+
+    def stacked(both):
+        return jnp.concatenate(
+            [jnp.where(first_head, both, 0.0), jnp.where(first_head, 0.0, both)], axis=0
+        ).astype(jnp.bfloat16)
+
+    def turned(both):
+        flipped = both.T.astype(jnp.bfloat16)
+        return jnp.concatenate([flipped[:HDIM], flipped[HDIM:]], axis=1)
+
+    q_both = q_ref[...].astype(jnp.float32)
+    q_rows = stacked(q_both)
+    q_cols = turned(q_both)
+
+    def lane_max(top, scores):
+        for j in range(scores.shape[1] // pair):
+            top = jnp.maximum(top, scores[:, j * pair : (j + 1) * pair])
+        return top
+
+    def score_step(c, top):
+        cols = pl.ds(pl.multiple_of(c * CHUNK, CHUNK), CHUNK)
+        scores = jnp.dot(q_rows, k2t_ref[:, cols], preferred_element_type=jnp.float32)
+        scores = scores + bias_ref[0:1, cols]
+        s_ref[:, cols] = scores
+        return lane_max(top, scores)
+
+    top = lax.fori_loop(
+        0,
+        prompt // CHUNK,
+        score_step,
+        jnp.full((2 * rows, pair), NEGATIVE, jnp.float32),
+        unroll=unroll,
+    )
+    row_id = lax.broadcasted_iota(jnp.int32, (2 * rows, rows), 0) % rows
+    col_id = lax.broadcasted_iota(jnp.int32, (2 * rows, rows), 1)
+    scores = jnp.dot(q_rows, k2t_ref[:, prompt:], preferred_element_type=jnp.float32)
+    scores = jnp.where(col_id <= row_id, scores, NEGATIVE)
+    s_ref[:, prompt:] = scores
+    top = jnp.max(lane_max(top, scores), axis=1, keepdims=True)
+    point(1)
+
+    def weight_step(c, carry):
+        total, mixed = carry
+        cols = pl.ds(pl.multiple_of(c * CHUNK, CHUNK), CHUNK)
+        weights = jnp.exp(s_ref[:, cols] - top)
+        for j in range(CHUNK // pair):
+            total = total + weights[:, j * pair : (j + 1) * pair]
+        low = weights.astype(jnp.bfloat16)
+        e_ref[:, cols] = low
+        mixed = mixed + jnp.dot(low, v2_ref[cols, :], preferred_element_type=jnp.float32)
+        return total, mixed
+
+    zero = jnp.zeros((2 * rows, pair), jnp.float32)
+    total, mixed = lax.fori_loop(
+        0, key_count // CHUNK, weight_step, (zero, zero), unroll=unroll
+    )
+    point(2)
+    scale = 1.0 / jnp.sum(total, axis=1, keepdims=True)
+    mixed = mixed * scale
+    context = jnp.where(first_head, mixed[:rows], mixed[rows:])
+    ctx_ref[...] = context.astype(ctx_ref.dtype)
+    d_context = dc_ref[...]
+    product = d_context * context
+    delta_a = jnp.sum(jnp.where(first_head, product, 0.0), axis=1, keepdims=True)
+    delta_b = jnp.sum(jnp.where(first_head, 0.0, product), axis=1, keepdims=True)
+    delta = jnp.concatenate([delta_a, delta_b], axis=0) * scale
+    d_both = d_context * jnp.where(first_head, scale[:rows], scale[rows:])
+    d_rows = stacked(d_both)
+    d_cols = turned(d_both)
+
+    def grad_step(c, d_query):
+        cols = pl.ds(pl.multiple_of(c * CHUNK, CHUNK), CHUNK)
+        d_probs = jnp.dot(d_rows, v2t_ref[:, cols], preferred_element_type=jnp.float32)
+        low = e_ref[:, cols]
+        d_scores = (low.astype(jnp.float32) * (d_probs - delta)).astype(jnp.bfloat16)
+        dvt_ref[:, cols] += jnp.dot(d_cols, low, preferred_element_type=jnp.float32)
+        dkt_ref[:, cols] += jnp.dot(q_cols, d_scores, preferred_element_type=jnp.float32)
+        return d_query + jnp.dot(d_scores, k2_ref[cols, :], preferred_element_type=jnp.float32)
+
+    d_query = lax.fori_loop(0, key_count // CHUNK, grad_step, zero, unroll=unroll)
+    dq_ref[...] = jnp.where(first_head, d_query[:rows], d_query[rows:]) * SCORE_SCALE
+    point(3)
+    if last:
+
+        @pl.when(step == pl.num_programs(0) - 1)
+        def _():
+            sent_ref, own_ref = results
+            for part, total_ref in enumerate((dkt_ref, dvt_ref)):
+                for block in range(prompt // rows):
+                    cols = slice(block * rows, (block + 1) * rows)
+                    sent_ref[block, part] = total_ref[:, cols].astype(sent_ref.dtype)
+                own_ref[part] = total_ref[:, prompt:]
+
+
+def attention(half, queries, d_context, tables, carried=None, comm=None, collective_id=None):
+    k2, k2t, v2, v2t, bias = tables
+    key_count, pair = k2.shape
+    rows, width = queries.shape
+    steps = width // pair // 2
+    last = half == 1
+    prompt_blocks = key_count // rows - 1
+
+    def whole(*shape):
+        return pl.BlockSpec(
+            shape, lambda i: (0,) * len(shape), pipeline_mode=pl.Buffered(1)
+        )
+
+    def result(*shape):
+        return pl.BlockSpec(shape, lambda i: (0,) * len(shape))
+
+    block_in = pl.BlockSpec((rows, pair), lambda i: (0, i + half * steps))
+    block = pl.BlockSpec((rows, pair), lambda i: (0, i))
+    args = [queries, d_context, k2, k2t, v2, v2t, bias]
+    in_specs = [block_in, block_in] + [whole(*a.shape) for a in args[2:]]
+    out_specs = [block, block]
+    out_shape = [
+        jax.ShapeDtypeStruct((rows, width // 2), jnp.bfloat16),
+        jax.ShapeDtypeStruct((rows, width // 2), jnp.float32),
+    ]
+    scratch = [
+        pltpu.VMEM((2 * rows, key_count), jnp.float32),
+        pltpu.VMEM((2 * rows, key_count), jnp.bfloat16),
+    ]
+    sums = [jax.ShapeDtypeStruct((HDIM, key_count), jnp.float32)] * 2
+    if last:
+        args += list(carried)
+        in_specs += [whole(*a.shape) for a in carried]
+        out_shape += [
+            jax.ShapeDtypeStruct((prompt_blocks, 2, HDIM, rows), jnp.bfloat16),
+            jax.ShapeDtypeStruct((2, HDIM, rows), jnp.float32),
+        ]
+        scratch += [pltpu.VMEM(s.shape, s.dtype) for s in sums]
+    else:
+        out_shape += sums
+    out_specs += [result(*o.shape) for o in out_shape[2:]]
+    inputs, outputs = len(args), len(out_shape)
+    plan = None
+    comm_ins, comm_outs = 0, 0
+    if comm is not None:
+        plan, more_args, more_out_specs, more_out_shape, more_scratch = comm
+        comm_ins, comm_outs = len(more_args), len(more_out_shape)
+        args += list(more_args)
+        in_specs += [pl.BlockSpec(memory_space=pl.ANY)] * comm_ins
+        out_specs += more_out_specs
+        out_shape += more_out_shape
+        scratch += more_scratch
+    return pl.pallas_call(
+        partial(attention_kernel, last, plan, (inputs, outputs, comm_ins, comm_outs)),
+        grid=(steps,),
+        in_specs=in_specs,
+        out_specs=out_specs,
+        out_shape=out_shape,
+        scratch_shapes=scratch,
+        compiler_params=pltpu.CompilerParams(
+            dimension_semantics=("arbitrary",),
+            vmem_limit_bytes=63 << 20,
+            collective_id=collective_id,
+            has_side_effects=comm is not None,
+        ),
+        cost_estimate=pl.CostEstimate(
+            flops=6 * rows * width * key_count,
+            bytes_accessed=8 * rows * width + 16 * key_count * pair,
+            transcendentals=rows * HEADS * key_count // 2,
+        ),
+        name="attention_with_reduce" if last else "attention_with_gather",
+    )(*args)
+
+
+def gather_beside(shards, orders):
+    n = len(shards)
+    arrays = range(n)
+
+    def plan(ins, outs, scratch):
+        place = chip_place()
+        gather = Gather(place, orders, ins, outs, *scratch)
+
+        def begin():
+            greet(place)
+            gather.begin(arrays)
+
+        return {
+            (0, 0): begin,
+            (0, 2): lambda: gather.pass_on(arrays, Z_SLABS[:1]),
+            (1, 0): lambda: gather.pass_on(arrays, Z_SLABS[1:]),
+            (1, 1): lambda: gather.pass_on(arrays, P_SLABS[:2]),
+            (1, 2): lambda: gather.pass_on(arrays, P_SLABS[2:]),
+            (2, 0): lambda: gather.pass_on(arrays, Q_SLABS[:4]),
+            (2, 2): lambda: gather.pass_on(arrays, Q_SLABS[4:]),
+            (2, 3): lambda: gather.finish(arrays),
+        }
+
+    out_shape = [jax.ShapeDtypeStruct((SLABS,) + s.shape, s.dtype) for s in shards]
+    out_specs = [pl.BlockSpec(memory_space=pl.ANY)] * n
+    scratch = [
+        pltpu.SemaphoreType.DMA((n, 32)),
+        pltpu.SemaphoreType.DMA((n, 32)),
+        pltpu.SemaphoreType.DMA((n,)),
+    ]
+    return plan, shards, out_specs, out_shape, scratch
+
+
+def reduce_beside(terms, orders):
+    n = len(terms)
+    arrays = range(n)
+
+    def plan(ins, outs, scratch):
+        place = chip_place()
+        reduce = Reduce(place, orders, ins, outs, scratch[:n], scratch[n : 2 * n], *scratch[2 * n :])
+
+        def begin():
+            greet(place)
+            reduce.begin(arrays, SUM_SLABS)
+
+        def end():
+            reduce.steps(arrays, SUM_SLABS[15:])
+            reduce.finish()
+
+        return {
+            (0, 0): begin,
+            (0, 2): lambda: reduce.steps(arrays, SUM_SLABS[:4]),
+            (1, 0): lambda: reduce.steps(arrays, SUM_SLABS[4:8]),
+            (1, 2): lambda: reduce.steps(arrays, SUM_SLABS[8:10]),
+            (2, 0): lambda: reduce.steps(arrays, SUM_SLABS[10:12]),
+            (2, 2): lambda: reduce.steps(arrays, SUM_SLABS[12:15]),
+            (2, 3): end,
+        }
+
+    slabs = [t.shape[1:] for t in terms]
+    out_shape = [jax.ShapeDtypeStruct(s, jnp.float32) for s in slabs]
+    out_specs = [pl.BlockSpec(s, lambda i: (0, 0)) for s in slabs]
+    scratch = (
+        [pltpu.VMEM((16,) + s, jnp.bfloat16) for s in slabs]
+        + [pltpu.VMEM((31,) + s, jnp.bfloat16) for s in slabs]
+        + [
+            pltpu.SemaphoreType.DMA((n, 31)),
+            pltpu.SemaphoreType.DMA((n, 31)),
+            pltpu.SemaphoreType.DMA((n, 16)),
+        ]
+    )
+    return plan, terms, out_specs, out_shape, scratch
+
+
+def attention_tables(keys_values, limit, rows):
+    key_count = keys_values.shape[0]
+    keys = keys_values[:, :HDIM]
+    values = keys_values[:, HDIM:]
+    k2 = jnp.concatenate([keys, keys], axis=1)
+    v2 = jnp.concatenate([values, values], axis=1)
+    column = jnp.arange(key_count, dtype=jnp.int32)
+    shown = jnp.logical_or(column < limit, column >= key_count - rows)
+    bias = jnp.broadcast_to(jnp.where(shown, 0.0, NEGATIVE)[None], (8, key_count))
+    return k2, k2.T, v2, v2.T, bias
 
 
 def pack_small(flat, rows_above, columns):
@@ -747,16 +894,19 @@
     qkv_rows, columns = qkv_weight.shape
     packed = pack_small(jnp.concatenate(small)[None], qkv_rows, columns)[0]
     head = jnp.concatenate([qkv_weight, packed], axis=0)
-    weights = (head, out_weight, up_weight, down_weight)
+
+    def all_of(*shards):
+        return [lax.all_gather(w, AXES, axis=0, tiled=False) for w in shards]
+
+    def joined(gathered):
+        return gathered.reshape(-1, gathered.shape[2])
+
     if direct:
-        gathered = gather_shards(weights, ROUTES, 0, "gather")
+        head_all, out_full = gather_shards((head, out_weight), ROUTES, 0, "gather")
     else:
-        gathered = [lax.all_gather(w, AXES, axis=0, tiled=False) for w in weights]
-    head_all, out_full, up_full, down_full = gathered
-    out_full = out_full.reshape(-1, out_full.shape[2])
-    up_full = up_full.reshape(-1, up_full.shape[2])
-    down_full = down_full.reshape(-1, down_full.shape[2])
-    qkv_full = head_all[:, :qkv_rows].reshape(shards * qkv_rows, -1)
+        head_all, out_full = all_of(head, out_weight)
+    out_full = joined(out_full)
+    qkv_full = joined(head_all[:, :qkv_rows])
     (
         query_full,
         out_bias_full,
@@ -801,15 +951,46 @@
     contract_first = (((0,), (0,)), ((), ()))
     matmul = partial(lax.dot_general, preferred_element_type=jnp.float32)
     d_context = matmul(grad_rows, out_full, contract_last)
-    context_low, d_query, d_keys_t, d_values_t = attention(
-        queries, d_context, keys_values, limit
-    )
-    kv_terms = jnp.stack([d_keys_t, d_values_t])
-    own_term = kv_terms[:, :, prompt_len:]
-    sent = kv_terms[:, :, :prompt_len].astype(jnp.bfloat16)
-    sent = sent.reshape(2, HDIM, PDEV, row_count).transpose(2, 0, 1, 3)
+    tables_kv = attention_tables(keys_values, limit, row_count)
+    comm = gather_beside((up_weight, down_weight), ROUTES) if direct else None
+    context_a, d_query_a, d_keys, d_values, *gathered = attention(
+        0, queries, d_context, tables_kv, comm=comm, collective_id=2 if direct else None
+    )
+    up_full, down_full = map(joined, gathered if direct else all_of(up_weight, down_weight))
+
+    pre_act = matmul(second_low, up_full, (((1,), (0,)), ((), ()))) + up_bias_full
+    hidden, gelu_back = jax.vjp(partial(jax.nn.gelu, approximate=False), pre_act)
+    hidden_low = hidden.astype(jnp.bfloat16)
+    d_hidden = matmul(grad_rows, down_full, contract_last)
+    d_pre_low = gelu_back(d_hidden)[0].astype(jnp.bfloat16)
+    grad_up_w = matmul(second_low, d_pre_low, contract_first)
+    grad_down_w = matmul(hidden_low, grad_rows, contract_first)
+
+    def by_shard(term):
+        return term.astype(jnp.bfloat16).reshape(shards, -1, term.shape[1])
+
+    def sum_of(*terms):
+        return [
+            lax.psum_scatter(t, AXES, scatter_dimension=0, tiled=False).astype(jnp.float32)
+            for t in terms
+        ]
+
+    wide_terms = (by_shard(grad_up_w), by_shard(grad_down_w))
+    comm = reduce_beside(wide_terms, ROUTES) if direct else None
+    context_b, d_query_b, sent, own_term, *summed = attention(
+        1,
+        queries,
+        d_context,
+        tables_kv,
+        carried=(d_keys, d_values),
+        comm=comm,
+        collective_id=3 if direct else None,
+    )
+    sum_up_w, sum_down_w = summed if direct else sum_of(*wide_terms)
+    context_low = jnp.concatenate([context_a, context_b], axis=1)
+    d_query = jnp.concatenate([d_query_a, d_query_b], axis=1)
     if direct:
-        summed = reduce_kv(sent, 2)
+        summed = reduce_kv(sent, 4)
     else:
         idle = lax.axis_size("tok") - PDEV
         sent = jnp.pad(sent, ((0, idle), (0, 0), (0, 0), (0, 0)))
@@ -817,9 +998,6 @@
         summed = summed.astype(jnp.float32)
     kv_grad = (own_term + summed).reshape(2 * HDIM, row_count).T
 
-    pre_act = matmul(second_low, up_full, (((1,), (0,)), ((), ()))) + up_bias_full
-    hidden, gelu_back = jax.vjp(partial(jax.nn.gelu, approximate=False), pre_act)
-    hidden_low = hidden.astype(jnp.bfloat16)
     result = (
         inputs
         + jnp.dot(context_low, out_full, preferred_element_type=jnp.float32)
@@ -831,13 +1009,9 @@
         + down_bias_full
     )
     layer_out = result.astype(jnp.bfloat16)[None]
-    d_hidden = matmul(grad_rows, down_full, contract_last)
-    d_pre_low = gelu_back(d_hidden)[0].astype(jnp.bfloat16)
     d_query_back = turn(d_query, tables, -1.0)
     d_kv_back = turn(kv_grad, key_tables, -1.0)
     d_projected = jnp.concatenate([d_query_back, d_kv_back], axis=1).astype(jnp.bfloat16)
-    grad_up_w = matmul(second_low, d_pre_low, contract_first)
-    grad_down_w = matmul(hidden_low, grad_rows, contract_first)
     grad_out_w = matmul(context_low, grad_rows, contract_first)
     grad_qkv_w = matmul(first_low, d_projected, contract_first)
     grad_query_b = jnp.sum(d_projected[:, :width].astype(jnp.float32), axis=0)
@@ -862,19 +1036,12 @@
     small_flat = jnp.concatenate([g.reshape(shards, -1) for g in small_grads], axis=1)
     small_flat = pack_small(small_flat, qkv_rows, columns)
 
-    def by_shard(term):
-        return term.astype(jnp.bfloat16).reshape(shards, -1, term.shape[1])
-
     tail = jnp.concatenate([by_shard(grad_qkv_w), small_flat.astype(jnp.bfloat16)], axis=1)
-    terms = (tail, by_shard(grad_out_w), by_shard(grad_up_w), by_shard(grad_down_w))
+    terms = (tail, by_shard(grad_out_w))
     if direct:
-        sums = reduce_shards(terms, ROUTES, 3, "reduce")
+        sum_tail, sum_out_w = reduce_shards(terms, ROUTES, 5, "reduce")
     else:
-        sums = [
-            lax.psum_scatter(t, AXES, scatter_dimension=0, tiled=False).astype(jnp.float32)
-            for t in terms
-        ]
-    sum_tail, sum_out_w, sum_up_w, sum_down_w = sums
+        sum_tail, sum_out_w = sum_of(*terms)
     sum_qkv_w = sum_tail[:qkv_rows]
     (
         sum_query_b,

time: 433 us -> 383 us (0.88)
  Pallas kernels: 304 us -> 252 us
    pallas_call x1, Pallas kernels: 77.8 us -> 26.1 us  [reduce_shards(): pl.pallas_call(partial(reduce_kernel, orders), in_specs=[pl.BlockSpec(mem...]
    pallas_call x1 -> x2, Pallas kernels: 109 us -> 158 us  [attention(): pl.pallas_call(partial(attention_kernel, last, plan, (inputs, outputs, co...]
    pallas_call x1, Pallas kernels: 71.2 us -> 26.4 us  [gather_shards(): pl.pallas_call(partial(gather_kernel, orders), in_specs=[pl.BlockSpec(mem...]
    unnamed x130 -> x140, local copies, waits for them, and re-layouts: 10.3 us -> 11 us
where the time goes in v3:
time: 383 us; the launch traced here: 375 us
  Pallas kernels  252 us (66%)
  matrix products  60.2 us (16%)
  local copies, waits for them, and re-layouts  42.7 us (11%)
  other arithmetic  17.7 us (5%)
    pallas_call x2, Pallas kernels, attention(): pl.pallas_call(partial(attention_kernel, last, plan, (inputs, outputs, co...  158 us
    pallas_call x1, Pallas kernels, gather_shards(): pl.pallas_call(partial(gather_kernel, orders), in_specs=[pl.BlockSpec(mem...  26.4 us
    pallas_call x1, Pallas kernels, reduce_shards(): pl.pallas_call(partial(reduce_kernel, orders), in_specs=[pl.BlockSpec(mem...  26.1 us
    pallas_call x1, Pallas kernels, reduce_kv(): pl.pallas_call(kv_reduce_kernel, in_specs=[pl.BlockSpec(memory_space=pltp...  23.2 us
    dot_general x1, matrix products, per_device(): matmul(second_low, up_full, (((1,), (0,)), ((), ()))) + up_bias_full  19.3 us
    pallas_call x1, Pallas kernels, gather_kv(): pl.pallas_call(kv_gather_kernel, in_specs=[pl.BlockSpec(memory_space=pl.A...  18.2 us
    unnamed x140, local copies, waits for them, and re-layouts  11 us
    another operation x6, local copies, waits for them, and re-layouts, turn(): own, from_right, from_left = (jnp.tile(t, (1, reps)) for t in tables)  10.5 us

profile of v3, /device:TPU:0, one launch (start us, length us, event | category | flops | bytes accessed | tf_op | source)
XLA Modules:
  0.0 375.4 jit_solution(15183273666909833723)
XLA Ops:
  0.7 5.5 %concatenate.60 = bf16[264]{0:T(512)(128)(2,1)S(1)} concatenate(bf16[24]{0:T(256)(128)(2,1)} %param.21, bf16[24]{0:T(256)(128)(2,1)} %param.22, bf16[96]{0:T(256)(128)(2,1)} %param.23, bf16[24]{0:T(256)(128)(2,1)} %param.24, bf16[24]{0:T(256)(128)(2,1)} %param.25, bf16[24]{0:T(256)(128)(2,1)} %param.26, bf16[24]{0:T(256)(128)(2,1)} %param.27, bf16[24]{0:T(256)(128)(2,1)} %param.28), dimensions={0} | concatenate | bytes 1056 | tf_op jit(solution)/shard_map/concatenate | solution.py:895
  7.7 26.4 %gather.1 = (bf16[32,32,896]{2,1,0:T(8,128)(2,1)}, bf16[32,24,768]{2,1,0:T(8,128)(2,1)}) custom-call(bf16[32,896]{1,0:T(8,128)(2,1)} %pad_maximum_fusion.7.refs_0_, bf16[24,768]{1,0:T(8,128)(2,1)} %refs_1_.1), custom_call_target="tpu_custom_call" | custom-call | tf_op jit(solution)/shard_map/gather/pallas_call | solution.py:188
  42.8 18.2 %gather_kv.1 = bf16[8,512,128]{2,1,0:T(8,128)(2,1)} custom-call(bf16[512,128]{1,0:T(8,128)(2,1)} %copy.56.kv_ref), custom_call_target="tpu_custom_call" | custom-call | tf_op jit(solution)/shard_map/gather_kv/pallas_call | solution.py:416
  68.7 2.5 tile.26
  71.1 1.9 copy.48
  73.0 2.5 tile.28
  75.5 3.0 copy.49
  82.1 1.8 fusion.82.refs_0_
  84.6 2.0 convolution_bitcast_fusion.refs_1_
  86.6 80.0 %attention_with_gather.1 = (bf16[512,384]{1,0:T(8,128)(2,1)}, f32[512,384]{1,0:T(8,128)}, f32[64,4608]{1,0:T(8,128)}, f32[64,4608]{1,0:T(8,128)}, bf16[32,24,307...) custom-call(bf16[512,768]{1,0:T(8,128)(2,1)} %fusion.82.refs_0_, f32[512,768]{1,0:T(8,128)} %convolution_bitcast_fusion.refs_1_, ...), custom_call_target="tpu_custom_call" | custom-call | flops 10871635968 | bytes 12582912 | tf_op jit(solution)/shard_map/attention_with_gather/pallas_call | solution.py:735
  169.2 19.3 %multiply_convert_fusion = (bf16[512,3072]{1,0:T(8,128)(2,1)S(1)}, f32[512,3072]{1,0:T(8,128)S(1)}, f32[512,3072]{1,0:T(8,128)}) fusion(f32[3072]{0:T(1024)S(1)} %reshape.453, bf16[768,3072]{1,0:T(8,128)(2,1)} %bitcast.215, bf16[1,512,768]{2,1,0:T(8,128)(2,1)S(1)} %copy-done.7, f32[768]{0:T(1024)S(1)} %reshape.452, f32[768]{0:T(1024)S(1)} %reshape.451, ...), kind=kOutput, calls=%fused_computation.11 | convolution fusion | flops 2522087424 | bytes 21256192 | tf_op jit(solution)/shard_map/dot_general | solution.py:961
  188.5 8.3 %fusion.121 = (bf16[3072]{0:T(1024)(128)(2,1)}, bf16[512,3072]{1,0:T(8,128)(2,1)S(1)}) fusion(f32[512,3072]{1,0:T(8,128)S(1)} %get-tuple-element.90, bf16[3072,768]{1,0:T(8,128)(2,1)S(1)} %bitcast.214, bf16[1,512,768]{2,1,0:T(8,128)(2,1)S(1)} %copy-done.13, f32[512,3072]{1,0:T(8,128)} %get-tuple-element.134, f32[3072]{0:T(1024)S(1)} %reshape.453), kind=kOutput, calls=%fused_computation.199 | convolution fusion | flops 2441081856 | bytes 21252096 | tf_op jit(solution)/shard_map/dot_general | solution.py:964
  196.8 4.7 %convolution_convert_fusion.1 = bf16[768,3072]{1,0:T(8,128)(2,1)} fusion(bf16[512,3072]{1,0:T(8,128)(2,1)S(1)} %get-tuple-element.137, bf16[1,512,768]{2,1,0:T(8,128)(2,1)S(1)} %copy-done.7, f32[768]{0:T(1024)S(1)} %reshape.452, f32[768]{0:T(1024)S(1)} %reshape.451, f32[512]{0:T(512)S(1)} %copy-done.40, f32[512]{0:T(512)S(1)} %copy-done.37), kind=kOutput, calls=%fused_computation.26 | convolution fusion | flops 2420637696 | bytes 8660992 | tf_op jit(solution)/shard_map/dot_general | solution.py:966
  201.6 4.3 %convolution_convert_fusion = bf16[3072,768]{1,0:T(8,128)(2,1)} fusion(bf16[512,3072]{1,0:T(8,128)(2,1)S(1)} %get-tuple-element.89, bf16[1,512,768]{2,1,0:T(8,128)(2,1)S(1)} %copy-done.13), kind=kOutput, calls=%fused_computation.25 | convolution fusion | flops 2418278400 | bytes 8650752 | tf_op jit(solution)/shard_map/dot_general | solution.py:967
  205.9 78.2 %attention_with_reduce.1 = (bf16[512,384]{1,0:T(8,128)(2,1)}, f32[512,384]{1,0:T(8,128)}, bf16[8,2,64,512]{3,2,1,0:T(8,128)(2,1)}, f32[2,64,512]{2,1,0:T(8,128)}, f32[24,3072]{1,0:T(8,128)}, /*index=5*/f32[96,768]{1,0:T(8,128)}) custom-call(bf16[512,768]{1,0:T(8,128)(2,1)} %fusion.82.refs_0_, f32[512,768]{1,0:T(8,128)} %convolution_bitcast_fusion.refs_1_, ...), custom_call_target="tpu_custom_call" | custom-call | flops 10871635968 | bytes 12582912 | tf_op jit(solution)/shard_map/attention_with_reduce/pallas_call | solution.py:735
  288.8 23.2 %reduce_kv.1 = f32[2,64,512]{2,1,0:T(8,128)} custom-call(bf16[8,2,64,512]{3,2,1,0:T(8,128)(2,1)} %get-tuple-element.42.in_ref), custom_call_target="tpu_custom_call" | custom-call | tf_op jit(solution)/shard_map/reduce_kv/pallas_call | solution.py:530
  313.6 2.3 convolution_convert_fusion.2
  315.9 5.1 %fusion.123 = f32[512,768]{1,0:T(8,128)S(1)} fusion(bf16[512,3072]{1,0:T(8,128)(2,1)S(1)} %copy-done.61, bf16[768,3072]{1,0:T(8,128)(2,1)} %bitcast.216), kind=kOutput, calls=%fused_computation.201 | convolution fusion | flops 2415919104 | bytes 9437184 | tf_op jit(solution)/shard_map/dot_general | solution.py:1021
  322.4 1.6 fusion.30
  328.0 1.9 convolution_convert_fusion.3
  329.8 26.1 %reduce.10 = (f32[32,896]{1,0:T(8,128)}, f32[24,768]{1,0:T(8,128)}) custom-call(bf16[32,32,896]{2,1,0:T(8,128)(2,1)} %pad_maximum_fusion.refs_0_, bf16[32,24,768]{2,1,0:T(8,128)(2,1)} %bitcast.205), custom_call_target="tpu_custom_call" | custom-call | tf_op jit(solution)/shard_map/reduce/pallas_call | solution.py:302
  359.4 2.0 add_bitcast_fusion
  361.8 6.3 %fusion.122 = f32[512,768]{1,0:T(8,128)} fusion(bf16[512,3072]{1,0:T(8,128)(2,1)S(1)} %copy-done.59, bf16[3072,768]{1,0:T(8,128)(2,1)} %bitcast.213), kind=kOutput, calls=%fused_computation.200 | convolution fusion | flops 2415919104 | bytes 9437184 | tf_op jit(solution)/shard_map/dot_general | solution.py:1008
  368.3 3.5 fusion.53
  (213 shorter events, 42.0 us)
Async XLA Ops:
  0.6 36.1 %copy-start.6 = (bf16[1,512,768]{2,1,0:T(8,128)(2,1)S(1)}, bf16[1,512,768]{2,1,0:T(8,128)(2,1)}, u32[]{:S(2)}) copy-start(bf16[1,512,768]{2,1,0:T(8,128)(2,1)} %param.15) | copy-start | bytes 2359300
  41.0 20.1 %copy-start.47 = (pred[128]{0:T(512)(128)(4,1)}, pred[128]{0:T(512)(128)(4,1)S(1)}, u32[]{:S(2)}) copy-start(pred[128]{0:T(512)(128)(4,1)S(1)} %get-tuple-element.138) | copy-start | bytes 388
  41.0 20.1 %copy-start.49 = (pred[128]{0:T(512)(128)(4,1)}, pred[128]{0:T(512)(128)(4,1)S(1)}, u32[]{:S(2)}) copy-start(pred[128]{0:T(512)(128)(4,1)S(1)} %get-tuple-element.139) | copy-start | bytes 388
  41.0 20.1 %copy-start.51 = (pred[128]{0:T(512)(128)(4,1)}, pred[128]{0:T(512)(128)(4,1)S(1)}, u32[]{:S(2)}) copy-start(pred[128]{0:T(512)(128)(4,1)S(1)} %get-tuple-element.140) | copy-start | bytes 388
  41.0 20.0 %copy-start.53 = (pred[128]{0:T(512)(128)(4,1)}, pred[128]{0:T(512)(128)(4,1)S(1)}, u32[]{:S(2)}) copy-start(pred[128]{0:T(512)(128)(4,1)S(1)} %get-tuple-element.141) | copy-start | bytes 388
  68.7 12.2 %copy-start = (f32[512,768]{1,0:T(8,128)}, f32[512,768]{1,0:T(8,128)S(1)}, u32[]{:S(2)}) copy-start(f32[512,768]{1,0:T(8,128)S(1)} %copy.47) | copy-start | bytes 4718596
  73.0 7.8 %copy-start.2 = (f32[512,768]{1,0:T(8,128)}, f32[512,768]{1,0:T(8,128)S(1)}, u32[]{:S(2)}) copy-start(f32[512,768]{1,0:T(8,128)S(1)} %copy.48) | copy-start | bytes 4718596
  86.6 82.5 %copy-start.7 = (bf16[1,512,768]{2,1,0:T(8,128)(2,1)S(1)}, bf16[1,512,768]{2,1,0:T(8,128)(2,1)}, u32[]{:S(2)}) copy-start(bf16[1,512,768]{2,1,0:T(8,128)(2,1)} %param.15) | copy-start | bytes 2359300
  167.5 29.4 %copy-start.34 = (f32[768]{0:T(1024)}, f32[768]{0:T(1024)S(1)}, u32[]{:S(2)}) copy-start(f32[768]{0:T(1024)S(1)} %reshape.451) | copy-start | bytes 9220
  169.1 19.3 %copy-start.13 = (bf16[1,512,768]{2,1,0:T(8,128)(2,1)S(1)}, bf16[1,512,768]{2,1,0:T(8,128)(2,1)}, u32[]{:S(2)}) copy-start(bf16[1,512,768]{2,1,0:T(8,128)(2,1)} %param.29) | copy-start | bytes 2359300
  169.1 19.3 %copy-start.57 = (bf16[32,96,768]{2,1,0:T(8,128)(2,1)S(1)}, bf16[32,96,768]{2,1,0:T(8,128)(2,1)}, u32[]{:S(2)}) copy-start(bf16[32,96,768]{2,1,0:T(8,128)(2,1)} %get-tuple-element.37) | copy-start | bytes 14155780
  188.5 13.1 %copy-start.58 = (bf16[512,3072]{1,0:T(8,128)(2,1)}, bf16[512,3072]{1,0:T(8,128)(2,1)S(1)}, u32[]{:S(2)}) copy-start(bf16[512,3072]{1,0:T(8,128)(2,1)S(1)} %get-tuple-element.89) | copy-start | bytes 9437188
  188.5 8.3 %copy-start.37 = (f32[512]{0:T(512)S(1)}, f32[512]{0:T(512)}, u32[]{:S(2)}) copy-start(f32[512]{0:T(512)} %copy-done.36) | copy-start | bytes 6148
  188.5 8.3 %copy-start.40 = (f32[512]{0:T(512)S(1)}, f32[512]{0:T(512)}, u32[]{:S(2)}) copy-start(f32[512]{0:T(512)} %copy-done.39) | copy-start | bytes 6148
  288.0 24.1 %copy-start.26 = (f32[2,64,512]{2,1,0:T(8,128)S(1)}, f32[2,64,512]{2,1,0:T(8,128)}, u32[]{:S(2)}) copy-start(f32[2,64,512]{2,1,0:T(8,128)} %get-tuple-element.41) | copy-start | bytes 786436
  288.8 24.4 %copy-start.48 = (pred[128]{0:T(512)(128)(4,1)S(1)}, pred[128]{0:T(512)(128)(4,1)}, u32[]{:S(2)}) copy-start(pred[128]{0:T(512)(128)(4,1)} %copy-done.47) | copy-start | bytes 388
  288.8 24.4 %copy-start.50 = (pred[128]{0:T(512)(128)(4,1)S(1)}, pred[128]{0:T(512)(128)(4,1)}, u32[]{:S(2)}) copy-start(pred[128]{0:T(512)(128)(4,1)} %copy-done.49) | copy-start | bytes 388
  288.8 24.4 %copy-start.52 = (pred[128]{0:T(512)(128)(4,1)S(1)}, pred[128]{0:T(512)(128)(4,1)}, u32[]{:S(2)}) copy-start(pred[128]{0:T(512)(128)(4,1)} %copy-done.51) | copy-start | bytes 388
  288.8 24.4 %copy-start.54 = (pred[128]{0:T(512)(128)(4,1)S(1)}, pred[128]{0:T(512)(128)(4,1)}, u32[]{:S(2)}) copy-start(pred[128]{0:T(512)(128)(4,1)} %copy-done.53) | copy-start | bytes 388
  329.8 29.6 %copy-start.11 = (f32[512,768]{1,0:T(8,128)S(1)}, f32[512,768]{1,0:T(8,128)}, u32[]{:S(2)}) copy-start(f32[512,768]{1,0:T(8,128)} %copy-done.10) | copy-start | bytes 4718596
  358.8 13.7 %copy-start.55 = (f32[24]{0:T(128)}, f32[24]{0:T(128)S(1)}, u32[]{:S(2)}) copy-start(f32[24]{0:T(128)S(1)} %get-tuple-element.195) | copy-start | bytes 292
  361.8 6.5 %copy-start.28 = (bf16[512,768]{1,0:T(8,128)(2,1)S(1)}, bf16[512,768]{1,0:T(8,128)(2,1)}, u32[]{:S(2)}) copy-start(bf16[512,768]{1,0:T(8,128)(2,1)} %copy-done.27) | copy-start | bytes 2359300
  368.3 5.5 %copy-start.25 = (f32[24,3072]{1,0:T(8,128)S(1)}, f32[24,3072]{1,0:T(8,128)}, u32[]{:S(2)}) copy-start(f32[24,3072]{1,0:T(8,128)} %get-tuple-element.192) | copy-start | bytes 884740
  368.3 6.2 %copy-start.24 = (f32[96,768]{1,0:T(8,128)S(1)}, f32[96,768]{1,0:T(8,128)}, u32[]{:S(2)}) copy-start(f32[96,768]{1,0:T(8,128)} %get-tuple-element.193) | copy-start | bytes 884740
  (38 other events, 80.1 us)

commit v4 on v3

--- a/solution.py
+++ b/solution.py
@@ -32,6 +32,18 @@
     reps = width // half
     cosine = jnp.tile(jnp.cos(angles), (1, reps))
     sine = jnp.tile(jnp.sin(angles), (1, reps))
+    own = jnp.where(lane < ROT, cosine, 1.0)
+    from_right = jnp.where(lane < half, -sine, 0.0)
+    from_left = jnp.where(jnp.logical_and(lane >= half, lane < ROT), sine, 0.0)
+    return own, from_right, from_left
+
+
+def lane_tables(positions, width):
+    half = ROT // 2
+    lane = jnp.arange(width, dtype=jnp.int32) % HDIM
+    frequency = 10000.0 ** (-((lane % half).astype(jnp.float32) * 2.0) / ROT)
+    angles = positions[:, None] * frequency[None, :]
+    cosine, sine = jnp.cos(angles), jnp.sin(angles)
     own = jnp.where(lane < ROT, cosine, 1.0)
     from_right = jnp.where(lane < half, -sine, 0.0)
     from_left = jnp.where(jnp.logical_and(lane >= half, lane < ROT), sine, 0.0)
@@ -231,7 +243,8 @@
                 sid = k * 4 + fp * 2 + fq
                 src = partial(self.far_term, a, (k, fp, fq))
                 self.mail(a, src, sid, partial(near, self.place, fg=1))
-                self.load(a, k, fp, fq).start()
+                if self.local is not None:
+                    self.load(a, k, fp, fq).start()
 
     def arrived(self, a, index):
         box = self.boxes[a].at[index]
@@ -242,9 +255,13 @@
 
     def step(self, a, k, fp, fq):
         sid = k * 4 + fp * 2 + fq
-        self.load(a, k, fp, fq).wait()
-        total = self.accs[a][sid].astype(jnp.float32) + self.arrived(a, sid)
         place, order = self.place, self.orders[a]
+        if self.local is not None:
+            self.load(a, k, fp, fq).wait()
+            total = self.accs[a][sid].astype(jnp.float32)
+        else:
+            total = self.ins[a][slot_at(near_pq(place, order, k, fp, fq))].astype(jnp.float32)
+        total = total + self.arrived(a, sid)
         if fq == 0:
             total = total + self.arrived(a, 16 + k * 2 + fp)
         if fq == 0 and fp == 0:
@@ -284,40 +301,6 @@
 )
 
 
-def reduce_kernel(orders, *refs):
-    n = len(orders)
-    ins, outs, accs, boxes = (refs[i * n : (i + 1) * n] for i in range(4))
-    send, recv, local = refs[4 * n :]
-    place = chip_place()
-    greet(place)
-    reduce = Reduce(place, orders, ins, outs, accs, boxes, send, recv, local)
-    arrays = range(n)
-    reduce.begin(arrays, SUM_SLABS)
-    reduce.steps(arrays, SUM_SLABS)
-    reduce.finish()
-
-
-def reduce_shards(terms, orders, collective_id, name):
-    n = len(terms)
-    return pl.pallas_call(
-        partial(reduce_kernel, orders),
-        in_specs=[pl.BlockSpec(memory_space=pl.ANY)] * n,
-        out_specs=[pl.BlockSpec(memory_space=pltpu.VMEM)] * n,
-        out_shape=[jax.ShapeDtypeStruct(t.shape[1:], jnp.float32) for t in terms],
-        scratch_shapes=[pltpu.VMEM((16,) + t.shape[1:], t.dtype) for t in terms]
-        + [pltpu.VMEM((31,) + t.shape[1:], t.dtype) for t in terms]
-        + [
-            pltpu.SemaphoreType.DMA((n, 31)),
-            pltpu.SemaphoreType.DMA((n, 31)),
-            pltpu.SemaphoreType.DMA((n, 16)),
-        ],
-        compiler_params=pltpu.CompilerParams(
-            collective_id=collective_id, has_side_effects=True, vmem_limit_bytes=58 << 20
-        ),
-        name=name,
-    )(*terms)
-
-
 def kv_route(place, half, fp=0, fq=0):
     if half == 0:
         return near(place, fy=fp, fx=fq)
@@ -328,227 +311,10 @@
     return plane * 4 + coords[1] * 2 + coords[2]
 
 
-def kv_gather_kernel(kv_ref, all_ref, send, recv, local):
-    place = chip_place()
-    z, y, x, g = place
-    rows = kv_ref.shape[0] // 2
-    greet(place)
-
-    def at_z(zz):
-        return (zz, y, x, g)
-
-    def block(slot, half=None):
-        if half is None:
-            return all_ref.at[slot]
-        return all_ref.at[slot, pl.ds(half * rows, rows)]
-
-    def waiter(ref, index):
-        remote(ref, ref, send.at[index], recv.at[index], near(place, fg=1)).wait_recv()
-
-    own = pltpu.make_async_copy(kv_ref, block(kv_slot(place, z % 2)), local.at[0])
-
-    def own_push(index, zz):
-        return remote(
-            kv_ref, block(kv_slot(place, z % 2)), send.at[index], recv.at[z % 2], at_z(zz)
-        )
-
-    def relay(plane):
-        ref = block(kv_slot(place, plane))
-        return remote(ref, ref, send.at[plane], recv.at[plane], at_z(3))
-
-    @pl.when(z < 2)
-    def _():
-        own_push(0, 1 - z % 2).start()
-        own_push(1, 2).start()
-        own.start()
-
-    started = []
-
-    def push(ref, index, coords):
-        copy = remote(ref, ref, send.at[index], recv.at[index], coords)
-        copy.start()
-        started.append(copy)
-
-    @pl.when(z < 2)
-    def _():
-        own.wait()
-
-    def here(plane):
-        @pl.when(z != plane)
-        def _():
-            waiter(block(kv_slot(place, plane)), plane)
-
-        @pl.when(z == 2)
-        def _():
-            relay(plane).start()
-
-    for plane in (1, 0):
-        here(plane)
-        for half in range(2):
-            ref = block(kv_slot(place, plane), half)
-            push(ref, 2 + plane * 2 + half, kv_route(place, half, fp=1))
-            push(ref, 6 + plane * 4 + half, kv_route(place, half, fq=1))
-    for plane in (1, 0):
-        for half in range(2):
-            ref = block(kv_slot(kv_route(place, half, fp=1), plane), half)
-            waiter(ref, 2 + plane * 2 + half)
-            push(ref, 6 + plane * 4 + 2 + half, kv_route(place, half, fq=1))
-    for plane in (1, 0):
-        for fp in range(2):
-            for half in range(2):
-                ref = block(kv_slot(kv_route(place, half, fp, 1), plane), half)
-                waiter(ref, 6 + plane * 4 + fp * 2 + half)
-    for copy in started:
-        copy.wait_send()
-
-    @pl.when(z < 2)
-    def _():
-        own_push(0, 1 - z % 2).wait_send()
-        own_push(1, 2).wait_send()
-
-    @pl.when(z == 2)
-    def _():
-        relay(0).wait_send()
-        relay(1).wait_send()
-
-
-def gather_kv(key_value, collective_id):
-    return pl.pallas_call(
-        kv_gather_kernel,
-        in_specs=[pl.BlockSpec(memory_space=pl.ANY)],
-        out_specs=pl.BlockSpec(memory_space=pl.ANY),
-        out_shape=jax.ShapeDtypeStruct((PDEV,) + key_value.shape, key_value.dtype),
-        scratch_shapes=[
-            pltpu.SemaphoreType.DMA((14,)),
-            pltpu.SemaphoreType.DMA((14,)),
-            pltpu.SemaphoreType.DMA((1,)),
-        ],
-        compiler_params=pltpu.CompilerParams(collective_id=collective_id, has_side_effects=True),
-        name="gather_kv",
-    )(key_value)
-
-
-def kv_reduce_kernel(in_ref, out_ref, acc, q_box, p_box, z_box, send, recv):
-    place = chip_place()
-    z, y, x, g = place
-    greet(place)
-    started = []
-
-    def at_z(zz):
-        return (zz, y, x, g)
-
-    def mail(src, dst, index, coords):
-        copy = remote(src, dst, send.at[index], recv.at[index], coords)
-        copy.start()
-        started.append(copy)
-
-    def arrived(box, index):
-        remote(box, box, send.at[index], recv.at[index], near(place, fg=1)).wait_recv()
-        return box[...].astype(jnp.float32)
-
-    def slot(plane, half, fp=0, fq=0):
-        return kv_slot(kv_route(place, half, fp, fq), plane)
-
-    order = [(plane, half) for plane in (0, 1) for half in (0, 1)]
-    for fp in (1, 0):
-        for plane, half in order:
-            index = plane * 4 + fp * 2 + half
-            mail(
-                in_ref.at[slot(plane, half, fp, 1), half],
-                q_box.at[index],
-                index,
-                kv_route(place, half, fq=1),
-            )
-    for plane, half in order:
-        index = plane * 2 + half
-        box = q_box.at[plane * 4 + 2 + half]
-        total = in_ref[slot(plane, half, 1, 0), half].astype(jnp.float32) + arrived(
-            box, plane * 4 + 2 + half
-        )
-        acc[4 + index] = total.astype(acc.dtype)
-        mail(acc.at[4 + index], p_box.at[index], 8 + index, kv_route(place, half, fp=1))
-
-    def to_z(index, box, zz):
-        return remote(acc.at[index], z_box.at[box], send.at[12 + index], recv.at[12 + box], at_z(zz))
-
-    for plane, half in order:
-        index = plane * 2 + half
-        total = in_ref[slot(plane, half), half].astype(jnp.float32)
-        total = total + arrived(q_box.at[plane * 4 + half], plane * 4 + half)
-        total = total + arrived(p_box.at[index], 8 + index)
-
-        @pl.when(z == 2)
-        def _():
-            acc[index] = (total + arrived(z_box.at[index], 12 + index)).astype(acc.dtype)
-            to_z(index, half, plane).start()
-
-        @pl.when(z == 3)
-        def _():
-            acc[index] = total.astype(acc.dtype)
-            to_z(index, index, 2).start()
-
-        @pl.when(z == 1 - plane)
-        def _():
-            acc[index] = total.astype(acc.dtype)
-            to_z(index, 2 + half, plane).start()
-
-        @pl.when(z == plane)
-        def _():
-            out_ref[half] = total
-
-    @pl.when(z < 2)
-    def _():
-        for half in range(2):
-            first = arrived(z_box.at[2 + half], 14 + half)
-            second = arrived(z_box.at[half], 12 + half)
-            out_ref[half] = out_ref[half] + first + second
-
-    @pl.when(z >= 2)
-    def _():
-        out_ref[...] = jnp.zeros_like(out_ref)
-
-    for copy in started:
-        copy.wait_send()
-    for plane, half in order:
-        index = plane * 2 + half
-
-        @pl.when(z == 2)
-        def _():
-            to_z(index, half, plane).wait_send()
-
-        @pl.when(z == 3)
-        def _():
-            to_z(index, index, 2).wait_send()
-
-        @pl.when(z == 1 - plane)
-        def _():
-            to_z(index, 2 + half, plane).wait_send()
-
-
-def reduce_kv(terms, collective_id):
-    slab = terms.shape[2:]
-    return pl.pallas_call(
-        kv_reduce_kernel,
-        in_specs=[pl.BlockSpec(memory_space=pltpu.VMEM)],
-        out_specs=pl.BlockSpec(memory_space=pltpu.VMEM),
-        out_shape=jax.ShapeDtypeStruct(terms.shape[1:], jnp.float32),
-        scratch_shapes=[
-            pltpu.VMEM((8,) + slab, terms.dtype),
-            pltpu.VMEM((8,) + slab, terms.dtype),
-            pltpu.VMEM((4,) + slab, terms.dtype),
-            pltpu.VMEM((4,) + slab, terms.dtype),
-            pltpu.SemaphoreType.DMA((16,)),
-            pltpu.SemaphoreType.DMA((16,)),
-        ],
-        compiler_params=pltpu.CompilerParams(collective_id=collective_id, has_side_effects=True),
-        name="reduce_kv",
-    )(terms)
-
-
 def attention_kernel(last, plan, counts, *refs):
     inputs, outputs, comm_ins, comm_outs = counts
-    q_ref, dc_ref, k2_ref, k2t_ref, v2_ref, v2t_ref, bias_ref = refs[:7]
-    carried = refs[7:inputs]
+    q_ref, dc_ref, kv_ref, kvt_ref, bias_ref = refs[:5]
+    carried = refs[5:inputs]
     cut = inputs + comm_ins
     ctx_ref, dq_ref = refs[cut : cut + 2]
     results = refs[cut + 2 : cut + outputs]
@@ -561,7 +327,7 @@
         dkt_ref, dvt_ref = results
         comm_scratch = scratch[2:]
     rows = q_ref.shape[0]
-    key_count = k2_ref.shape[0]
+    key_count = kv_ref.shape[0]
     pair = 2 * HDIM
     prompt = key_count - rows
     unroll = 4
@@ -587,17 +353,20 @@
     point(0)
     first_head = lax.broadcasted_iota(jnp.int32, (rows, pair), 1) < HDIM
 
-    def stacked(both):
-        return jnp.concatenate(
-            [jnp.where(first_head, both, 0.0), jnp.where(first_head, 0.0, both)], axis=0
-        ).astype(jnp.bfloat16)
+    def stacked(both, on_values):
+        swapped = pltpu.roll(both, HDIM, 1)
+        if on_values:
+            parts = [jnp.where(first_head, 0.0, swapped), jnp.where(first_head, 0.0, both)]
+        else:
+            parts = [jnp.where(first_head, both, 0.0), jnp.where(first_head, swapped, 0.0)]
+        return jnp.concatenate(parts, axis=0).astype(jnp.bfloat16)
 
     def turned(both):
         flipped = both.T.astype(jnp.bfloat16)
         return jnp.concatenate([flipped[:HDIM], flipped[HDIM:]], axis=1)
 
     q_both = q_ref[...].astype(jnp.float32)
-    q_rows = stacked(q_both)
+    q_rows = stacked(q_both, False)
     q_cols = turned(q_both)
 
     def lane_max(top, scores):
@@ -607,7 +376,7 @@
 
     def score_step(c, top):
         cols = pl.ds(pl.multiple_of(c * CHUNK, CHUNK), CHUNK)
-        scores = jnp.dot(q_rows, k2t_ref[:, cols], preferred_element_type=jnp.float32)
+        scores = jnp.dot(q_rows, kvt_ref[:, cols], preferred_element_type=jnp.float32)
         scores = scores + bias_ref[0:1, cols]
         s_ref[:, cols] = scores
         return lane_max(top, scores)
@@ -621,7 +390,7 @@
     )
     row_id = lax.broadcasted_iota(jnp.int32, (2 * rows, rows), 0) % rows
     col_id = lax.broadcasted_iota(jnp.int32, (2 * rows, rows), 1)
-    scores = jnp.dot(q_rows, k2t_ref[:, prompt:], preferred_element_type=jnp.float32)
+    scores = jnp.dot(q_rows, kvt_ref[:, prompt:], preferred_element_type=jnp.float32)
     scores = jnp.where(col_id <= row_id, scores, NEGATIVE)
     s_ref[:, prompt:] = scores
     top = jnp.max(lane_max(top, scores), axis=1, keepdims=True)
@@ -635,7 +404,7 @@
             total = total + weights[:, j * pair : (j + 1) * pair]
         low = weights.astype(jnp.bfloat16)
         e_ref[:, cols] = low
-        mixed = mixed + jnp.dot(low, v2_ref[cols, :], preferred_element_type=jnp.float32)
+        mixed = mixed + jnp.dot(low, kv_ref[cols, :], preferred_element_type=jnp.float32)
         return total, mixed
 
     zero = jnp.zeros((2 * rows, pair), jnp.float32)
@@ -645,7 +414,7 @@
     point(2)
     scale = 1.0 / jnp.sum(total, axis=1, keepdims=True)
     mixed = mixed * scale
-    context = jnp.where(first_head, mixed[:rows], mixed[rows:])
+    context = jnp.where(first_head, pltpu.roll(mixed[:rows], HDIM, 1), mixed[rows:])
     ctx_ref[...] = context.astype(ctx_ref.dtype)
     d_context = dc_ref[...]
     product = d_context * context
@@ -653,20 +422,21 @@
     delta_b = jnp.sum(jnp.where(first_head, 0.0, product), axis=1, keepdims=True)
     delta = jnp.concatenate([delta_a, delta_b], axis=0) * scale
     d_both = d_context * jnp.where(first_head, scale[:rows], scale[rows:])
-    d_rows = stacked(d_both)
+    d_rows = stacked(d_both, True)
     d_cols = turned(d_both)
 
     def grad_step(c, d_query):
         cols = pl.ds(pl.multiple_of(c * CHUNK, CHUNK), CHUNK)
-        d_probs = jnp.dot(d_rows, v2t_ref[:, cols], preferred_element_type=jnp.float32)
+        d_probs = jnp.dot(d_rows, kvt_ref[:, cols], preferred_element_type=jnp.float32)
         low = e_ref[:, cols]
         d_scores = (low.astype(jnp.float32) * (d_probs - delta)).astype(jnp.bfloat16)
         dvt_ref[:, cols] += jnp.dot(d_cols, low, preferred_element_type=jnp.float32)
         dkt_ref[:, cols] += jnp.dot(q_cols, d_scores, preferred_element_type=jnp.float32)
-        return d_query + jnp.dot(d_scores, k2_ref[cols, :], preferred_element_type=jnp.float32)
+        return d_query + jnp.dot(d_scores, kv_ref[cols, :], preferred_element_type=jnp.float32)
 
     d_query = lax.fori_loop(0, key_count // CHUNK, grad_step, zero, unroll=unroll)
-    dq_ref[...] = jnp.where(first_head, d_query[:rows], d_query[rows:]) * SCORE_SCALE
+    second = pltpu.roll(d_query[rows:], HDIM, 1)
+    dq_ref[...] = jnp.where(first_head, d_query[:rows], second) * SCORE_SCALE
     point(3)
     if last:
 
@@ -681,8 +451,8 @@
 
 
 def attention(half, queries, d_context, tables, carried=None, comm=None, collective_id=None):
-    k2, k2t, v2, v2t, bias = tables
-    key_count, pair = k2.shape
+    keys_values, flipped, bias = tables
+    key_count, pair = keys_values.shape
     rows, width = queries.shape
     steps = width // pair // 2
     last = half == 1
@@ -698,7 +468,7 @@
 
     block_in = pl.BlockSpec((rows, pair), lambda i: (0, i + half * steps))
     block = pl.BlockSpec((rows, pair), lambda i: (0, i))
-    args = [queries, d_context, k2, k2t, v2, v2t, bias]
+    args = [queries, d_context, keys_values, flipped, bias]
     in_specs = [block_in, block_in] + [whole(*a.shape) for a in args[2:]]
     out_specs = [block, block]
     out_shape = [
@@ -830,14 +600,711 @@
 
 def attention_tables(keys_values, limit, rows):
     key_count = keys_values.shape[0]
-    keys = keys_values[:, :HDIM]
-    values = keys_values[:, HDIM:]
-    k2 = jnp.concatenate([keys, keys], axis=1)
-    v2 = jnp.concatenate([values, values], axis=1)
     column = jnp.arange(key_count, dtype=jnp.int32)
     shown = jnp.logical_or(column < limit, column >= key_count - rows)
     bias = jnp.broadcast_to(jnp.where(shown, 0.0, NEGATIVE)[None], (8, key_count))
-    return k2, k2.T, v2, v2.T, bias
+    return keys_values, keys_values.T, bias
+
+
+def tile_turn(values, own, from_right, from_left, sign):
+    half = ROT // 2
+    lanes = values.shape[1]
+    ahead = pltpu.roll(values, lanes - half, 1)
+    behind = pltpu.roll(values, half, 1)
+    return values * own + sign * (ahead * from_right + behind * from_left)
+
+
+def unit_rows(values):
+    centered = values - jnp.mean(values, axis=-1, keepdims=True)
+    variance = jnp.mean(centered * centered, axis=-1, keepdims=True)
+    scale = lax.rsqrt(variance + 1e-05)
+    return centered * scale, scale
+
+
+NT = (((1,), (1,)), ((), ()))
+TN = (((0,), (0,)), ((), ()))
+dot_of = partial(lax.dot_general, preferred_element_type=jnp.float32)
+
+
+class KvGather:
+    def __init__(self, place, kv_ref, all_ref, send, recv):
+        self.place, self.kv_ref, self.all_ref = place, kv_ref, all_ref
+        self.send, self.recv = send, recv
+        self.rows = kv_ref.shape[0] // 2
+        self.started = []
+
+    def at_z(self, zz):
+        return (zz,) + self.place[1:]
+
+    def block(self, slot, half=None):
+        if half is None:
+            return self.all_ref.at[slot]
+        return self.all_ref.at[slot, pl.ds(half * self.rows, self.rows)]
+
+    def wait(self, ref, index):
+        remote(
+            ref, ref, self.send.at[index], self.recv.at[index], near(self.place, fg=1)
+        ).wait_recv()
+
+    def own_push(self, index, zz):
+        plane = self.place[0] % 2
+        dst = self.block(kv_slot(self.place, plane))
+        return remote(
+            self.kv_ref, dst, self.send.at[index], self.recv.at[plane], self.at_z(zz)
+        )
+
+    def relay(self, plane):
+        ref = self.block(kv_slot(self.place, plane))
+        return remote(ref, ref, self.send.at[plane], self.recv.at[plane], self.at_z(3))
+
+    def push(self, ref, index, coords):
+        copy = remote(ref, ref, self.send.at[index], self.recv.at[index], coords)
+        copy.start()
+        self.started.append(copy)
+
+    def begin(self):
+        @pl.when(self.place[0] < 2)
+        def _():
+            self.own_push(0, 1 - self.place[0] % 2).start()
+            self.own_push(1, 2).start()
+
+    def planes(self):
+        z = self.place[0]
+        for plane in (1, 0):
+
+            @pl.when(z != plane)
+            def _():
+                self.wait(self.block(kv_slot(self.place, plane)), plane)
+
+            @pl.when(z == 2)
+            def _():
+                self.relay(plane).start()
+
+            for half in range(2):
+                ref = self.block(kv_slot(self.place, plane), half)
+                self.push(ref, 2 + plane * 2 + half, kv_route(self.place, half, fp=1))
+                self.push(ref, 6 + plane * 4 + half, kv_route(self.place, half, fq=1))
+
+    def middle(self):
+        for plane in (1, 0):
+            for half in range(2):
+                ref = self.block(kv_slot(kv_route(self.place, half, fp=1), plane), half)
+                self.wait(ref, 2 + plane * 2 + half)
+                self.push(ref, 6 + plane * 4 + 2 + half, kv_route(self.place, half, fq=1))
+
+    def finish(self):
+        for plane in (1, 0):
+            for fp in range(2):
+                for half in range(2):
+                    slot = kv_slot(kv_route(self.place, half, fp, 1), plane)
+                    self.wait(self.block(slot, half), 6 + plane * 4 + fp * 2 + half)
+        for copy in self.started:
+            copy.wait_send()
+        z = self.place[0]
+
+        @pl.when(z < 2)
+        def _():
+            self.own_push(0, 1 - z % 2).wait_send()
+            self.own_push(1, 2).wait_send()
+
+        @pl.when(z == 2)
+        def _():
+            self.relay(0).wait_send()
+            self.relay(1).wait_send()
+
+
+def project_kernel(
+    x_ref,
+    cot_ref,
+    qkv_ref,
+    out_ref,
+    par_ref,
+    own_ref,
+    right_ref,
+    left_ref,
+    q_ref,
+    kv_ref,
+    all_ref,
+    kvt_ref,
+    dc_ref,
+    first_ref,
+    second_ref,
+    send,
+    recv,
+):
+    place = chip_place()
+    greet(place)
+    rows = kv_ref.shape[0]
+    pair = 2 * HDIM
+    width = q_ref.shape[1]
+    unit, _ = unit_rows(x_ref[0].astype(jnp.float32))
+    first = (unit * par_ref[3:4] + par_ref[4:5]).astype(jnp.bfloat16)
+    first_ref[...] = first
+    own, right, left = own_ref[...], right_ref[...], left_ref[...]
+    is_key = lax.broadcasted_iota(jnp.int32, (rows, pair), 1) < HDIM
+    raw = jnp.dot(first, qkv_ref[:, width:], preferred_element_type=jnp.float32)
+    turned_kv = jnp.where(is_key, tile_turn(raw, own, right, left, 1.0), raw)
+    kv = turned_kv.astype(jnp.bfloat16)
+    kv_ref[...] = kv
+    all_ref[PDEV] = kv
+
+    @pl.when(place[0] < 2)
+    def _():
+        all_ref[kv_slot(place, place[0] % 2)] = kv_ref[...]
+
+    second_ref[...] = (unit * par_ref[5:6] + par_ref[6:7]).astype(jnp.bfloat16)
+    gather = KvGather(place, kv_ref, all_ref, send, recv)
+    gather.begin()
+    for tile in range(width // pair):
+        cols = slice(tile * pair, (tile + 1) * pair)
+        part = jnp.dot(first_ref[...], qkv_ref[:, cols], preferred_element_type=jnp.float32)
+        part = tile_turn(part + par_ref[0:1, cols], own, right, left, 1.0)
+        low = part.astype(jnp.bfloat16).astype(jnp.float32)
+        q_ref[:, cols] = (low * SCORE_SCALE).astype(jnp.bfloat16)
+    gather.planes()
+    dc_ref[...] = dot_of(cot_ref[0], out_ref[...], NT)
+    gather.middle()
+
+    def turn_over(slot):
+        flipped = all_ref[slot].astype(jnp.float32).T
+        kvt_ref[:, slot * rows : (slot + 1) * rows] = flipped.astype(jnp.bfloat16)
+
+    turn_over(PDEV)
+    gather.finish()
+    for slot in range(PDEV):
+        turn_over(slot)
+
+
+def vmem_spec():
+    return pl.BlockSpec(memory_space=pltpu.VMEM)
+
+
+def project(tokens, cotangent, qkv_full, out_full, params, tables, collective_id):
+    rows, width = tokens.shape[1:]
+    pair = 2 * HDIM
+    keys = (PDEV + 1) * rows
+    low = jnp.bfloat16
+    return pl.pallas_call(
+        project_kernel,
+        in_specs=[vmem_spec()] * 8,
+        out_specs=[vmem_spec()] * 7,
+        out_shape=[
+            jax.ShapeDtypeStruct((rows, width), low),
+            jax.ShapeDtypeStruct((rows, pair), low),
+            jax.ShapeDtypeStruct((PDEV + 1, rows, pair), low),
+            jax.ShapeDtypeStruct((pair, keys), low),
+            jax.ShapeDtypeStruct((rows, width), jnp.float32),
+            jax.ShapeDtypeStruct((rows, width), low),
+            jax.ShapeDtypeStruct((rows, width), low),
+        ],
+        scratch_shapes=[pltpu.SemaphoreType.DMA((14,)), pltpu.SemaphoreType.DMA((14,))],
+        compiler_params=pltpu.CompilerParams(
+            collective_id=collective_id, has_side_effects=True, vmem_limit_bytes=48 << 20
+        ),
+        name="project_with_gather",
+    )(tokens, cotangent, qkv_full, out_full, params, *tables)
+
+
+def mlp_kernel(
+    second_ref, cot_ref, up_ref, bias_ref, down_ref, upg_ref, downg_ref, out_ref, dsec_ref, bg_ref
+):
+    step = pl.program_id(0)
+    second = second_ref[...]
+    cot = cot_ref[0]
+    pre = jnp.dot(second, up_ref[...], preferred_element_type=jnp.float32) + bias_ref[...]
+    below = 0.5 + 0.5 * lax.erf(pre * 0.7071067811865476)
+    hidden = (pre * below).astype(jnp.bfloat16)
+    slope = below + pre * (jnp.exp(pre * pre * -0.5) * 0.3989422804014327)
+    d_pre = (dot_of(cot, down_ref[...], NT) * slope).astype(jnp.bfloat16)
+    upg_ref[...] = dot_of(second, d_pre, TN).astype(jnp.bfloat16)
+    downg_ref[...] = dot_of(hidden, cot, TN).astype(jnp.bfloat16)
+    bg_ref[...] = jnp.sum(d_pre.astype(jnp.float32), axis=0, keepdims=True)
+    out = jnp.dot(hidden, down_ref[...], preferred_element_type=jnp.float32)
+    d_second = dot_of(d_pre, up_ref[...], NT)
+
+    @pl.when(step == 0)
+    def _():
+        out_ref[...] = out
+        dsec_ref[...] = d_second
+
+    @pl.when(step > 0)
+    def _():
+        out_ref[...] += out
+        dsec_ref[...] += d_second
+
+
+def mlp(second_low, cotangent, up_full, up_bias, down_full):
+    rows, width = second_low.shape
+    inner = up_full.shape[1]
+    tile = 512
+    return pl.pallas_call(
+        mlp_kernel,
+        grid=(inner // tile,),
+        in_specs=[
+            pl.BlockSpec((rows, width), lambda i: (0, 0)),
+            pl.BlockSpec((1, rows, width), lambda i: (0, 0, 0)),
+            pl.BlockSpec((width, tile), lambda i: (0, i)),
+            pl.BlockSpec((1, tile), lambda i: (0, i)),
+            pl.BlockSpec((tile, width), lambda i: (i, 0)),
+        ],
+        out_specs=[
+            pl.BlockSpec((width, tile), lambda i: (0, i)),
+            pl.BlockSpec((tile, width), lambda i: (i, 0)),
+            pl.BlockSpec((rows, width), lambda i: (0, 0)),
+            pl.BlockSpec((rows, width), lambda i: (0, 0)),
+            pl.BlockSpec((1, tile), lambda i: (0, i)),
+        ],
+        out_shape=[
+            jax.ShapeDtypeStruct((width, inner), jnp.bfloat16),
+            jax.ShapeDtypeStruct((inner, width), jnp.bfloat16),
+            jax.ShapeDtypeStruct((rows, width), jnp.float32),
+            jax.ShapeDtypeStruct((rows, width), jnp.float32),
+            jax.ShapeDtypeStruct((1, inner), jnp.float32),
+        ],
+        compiler_params=pltpu.CompilerParams(
+            dimension_semantics=("arbitrary",), vmem_limit_bytes=48 << 20
+        ),
+        name="mlp",
+    )(second_low, cotangent, up_full, up_bias, down_full)
+
+
+class KvReduce:
+    order = [(plane, half) for plane in (0, 1) for half in (0, 1)]
+
+    def __init__(self, place, in_ref, out_ref, acc, q_box, p_box, z_box, send, recv):
+        self.place, self.in_ref, self.out_ref, self.acc = place, in_ref, out_ref, acc
+        self.q_box, self.p_box, self.z_box = q_box, p_box, z_box
+        self.send, self.recv = send, recv
+        self.started = []
+
+    def mail(self, src, dst, index, coords):
+        copy = remote(src, dst, self.send.at[index], self.recv.at[index], coords)
+        copy.start()
+        self.started.append(copy)
+
+    def arrived(self, box, index):
+        remote(
+            box, box, self.send.at[index], self.recv.at[index], near(self.place, fg=1)
+        ).wait_recv()
+        return box[...].astype(jnp.float32)
+
+    def slot(self, plane, half, fp=0, fq=0):
+        return kv_slot(kv_route(self.place, half, fp, fq), plane)
+
+    def to_z(self, index, box, zz):
+        return remote(
+            self.acc.at[index],
+            self.z_box.at[box],
+            self.send.at[12 + index],
+            self.recv.at[12 + box],
+            (zz,) + self.place[1:],
+        )
+
+    def begin(self):
+        for fp in (1, 0):
+            for plane, half in self.order:
+                index = plane * 4 + fp * 2 + half
+                src = self.in_ref.at[self.slot(plane, half, fp, 1), half]
+                self.mail(src, self.q_box.at[index], index, kv_route(self.place, half, fq=1))
+
+    def middle(self):
+        for plane, half in self.order:
+            index = plane * 2 + half
+            box = plane * 4 + 2 + half
+            total = self.in_ref[self.slot(plane, half, 1, 0), half].astype(jnp.float32)
+            total = total + self.arrived(self.q_box.at[box], box)
+            self.acc[4 + index] = total.astype(self.acc.dtype)
+            src = self.acc.at[4 + index]
+            self.mail(src, self.p_box.at[index], 8 + index, kv_route(self.place, half, fp=1))
+
+    def planes(self):
+        z = self.place[0]
+        for plane, half in self.order:
+            index = plane * 2 + half
+            box = plane * 4 + half
+            total = self.in_ref[self.slot(plane, half), half].astype(jnp.float32)
+            total = total + self.arrived(self.q_box.at[box], box)
+            total = total + self.arrived(self.p_box.at[index], 8 + index)
+
+            @pl.when(z == 2)
+            def _():
+                passed = total + self.arrived(self.z_box.at[index], 12 + index)
+                self.acc[index] = passed.astype(self.acc.dtype)
+                self.to_z(index, half, plane).start()
+
+            @pl.when(z == 3)
+            def _():
+                self.acc[index] = total.astype(self.acc.dtype)
+                self.to_z(index, index, 2).start()
+
+            @pl.when(z == 1 - plane)
+            def _():
+                self.acc[index] = total.astype(self.acc.dtype)
+                self.to_z(index, 2 + half, plane).start()
+
+            @pl.when(z == plane)
+            def _():
+                self.out_ref[half] = total
+
+    def finish(self):
+        z = self.place[0]
+
+        @pl.when(z < 2)
+        def _():
+            for half in range(2):
+                first = self.arrived(self.z_box.at[2 + half], 14 + half)
+                second = self.arrived(self.z_box.at[half], 12 + half)
+                self.out_ref[half] = self.out_ref[half] + first + second
+
+        @pl.when(z >= 2)
+        def _():
+            self.out_ref[...] = jnp.zeros_like(self.out_ref)
+
+    def close(self):
+        z = self.place[0]
+        for copy in self.started:
+            copy.wait_send()
+        for plane, half in self.order:
+            index = plane * 2 + half
+
+            @pl.when(z == 2)
+            def _():
+                self.to_z(index, half, plane).wait_send()
+
+            @pl.when(z == 3)
+            def _():
+                self.to_z(index, index, 2).wait_send()
+
+            @pl.when(z == 1 - plane)
+            def _():
+                self.to_z(index, 2 + half, plane).wait_send()
+
+
+SMALL_ROWS = 16
+
+
+def finish_kernel(
+    x_ref,
+    cot_ref,
+    ctxa_ref,
+    ctxb_ref,
+    dqa_ref,
+    dqb_ref,
+    sent_ref,
+    ownkv_ref,
+    own_ref,
+    right_ref,
+    left_ref,
+    first_ref,
+    par_ref,
+    qkv_ref,
+    out_ref,
+    mlp_ref,
+    dsec_ref,
+    bg_ref,
+    layer_ref,
+    xgrad_ref,
+    qkvg_ref,
+    outg_ref,
+    small_ref,
+    kv_sum,
+    kv_acc,
+    q_box,
+    p_box,
+    z_box,
+    kv_send,
+    kv_recv,
+    proj_ref,
+    dfirst_ref,
+    qkv_terms,
+    out_terms,
+    qkv_acc,
+    out_acc,
+    qkv_box,
+    out_box,
+    send,
+    recv,
+    small_acc,
+    small_box,
+    small_send,
+    small_recv,
+):
+    place = chip_place()
+    greet(place)
+    kv = KvReduce(place, sent_ref, kv_sum, kv_acc, q_box, p_box, z_box, kv_send, kv_recv)
+    kv.begin()
+    rows, width = x_ref.shape[1:]
+    pair = 2 * HDIM
+    cot = cot_ref[0]
+    half_width = width // 2
+    shard_rows = qkvg_ref.shape[0]
+    reduce = Reduce(
+        place,
+        ("yx", "xy"),
+        (qkv_terms, out_terms),
+        (qkvg_ref, outg_ref),
+        (qkv_acc, out_acc),
+        (qkv_box, out_box),
+        send,
+        recv,
+        None,
+    )
+
+    def lay(terms, value, first_row, cols):
+        for s in range(value.shape[0] // shard_rows):
+            part = value[s * shard_rows : (s + 1) * shard_rows]
+            terms[first_row // shard_rows + s, :, cols] = part.astype(jnp.bfloat16)
+
+    whole = slice(0, width)
+    lay(out_terms, dot_of(ctxa_ref[...], cot, TN), 0, whole)
+    lay(out_terms, dot_of(ctxb_ref[...], cot, TN), half_width, whole)
+    kv.middle()
+    reduce.begin([1], SUM_SLABS)
+    own, right, left = own_ref[...], right_ref[...], left_ref[...]
+    for side, ref in enumerate((dqa_ref, dqb_ref)):
+        for tile in range(half_width // pair):
+            at = tile * pair
+            part = tile_turn(ref[:, at : at + pair], own, right, left, -1.0)
+            at = at + side * half_width
+            proj_ref[:, at : at + pair] = part.astype(jnp.bfloat16)
+    layer = x_ref[0].astype(jnp.float32)
+    layer = layer + jnp.dot(ctxa_ref[...], out_ref[:half_width], preferred_element_type=jnp.float32)
+    layer = layer + jnp.dot(ctxb_ref[...], out_ref[half_width:], preferred_element_type=jnp.float32)
+    layer = layer + mlp_ref[...] + (par_ref[1:2] + par_ref[2:3])
+    layer_ref[0] = layer.astype(jnp.bfloat16)
+    kv.planes()
+    proj_q = proj_ref[:, :width]
+    lay(qkv_terms, dot_of(first_ref[...], proj_q, TN), 0, whole)
+    dfirst_ref[...] = dot_of(proj_q, qkv_ref[:, :width], NT)
+    reduce.steps([1], SUM_SLABS[:8])
+    kv.finish()
+    kv_grad = (ownkv_ref[...] + kv_sum[...]).reshape(pair, rows).T
+    is_key = lax.broadcasted_iota(jnp.int32, (rows, pair), 1) < HDIM
+    turned_kv = jnp.where(is_key, tile_turn(kv_grad, own, right, left, -1.0), kv_grad)
+    proj_kv = turned_kv.astype(jnp.bfloat16)
+    lay(qkv_terms, dot_of(first_ref[...], proj_kv, TN), 0, slice(width, width + pair))
+    d_first = dfirst_ref[...] + dot_of(proj_kv, qkv_ref[:, width:], NT)
+    dfirst_ref[...] = d_first
+    reduce.begin([0], SUM_SLABS)
+    unit, scale = unit_rows(x_ref[0].astype(jnp.float32))
+    d_second = dsec_ref[...]
+
+    def column_sum(value):
+        return jnp.sum(value, axis=0, keepdims=True)
+
+    small_acc[0:1] = column_sum(proj_ref[:, :width].astype(jnp.float32))
+    small_acc[1:2] = column_sum(cot.astype(jnp.float32))
+    for j in range(bg_ref.shape[1] // width):
+        small_acc[2 + j : 3 + j] = bg_ref[:, j * width : (j + 1) * width]
+    small_acc[6:7] = column_sum(d_first * unit)
+    small_acc[7:8] = column_sum(d_first)
+    small_acc[8:9] = column_sum(d_second * unit)
+    small_acc[9:10] = column_sum(d_second)
+    small_acc[10:] = jnp.zeros_like(small_acc[10:])
+    peers = [near(place, fg=1), near(place, fx=1), near(place, fy=1)]
+    peers += [near(place, k=k) for k in (1, 2, 3)]
+    sums_out = []
+
+    def small_mail(stage, copy_of):
+        copy = remote(
+            small_box.at[6 + copy_of],
+            small_box.at[stage],
+            small_send.at[stage],
+            small_recv.at[stage],
+            peers[stage],
+        )
+        copy.start()
+        sums_out.append(copy)
+
+    def small_in(stage):
+        box = small_box.at[stage]
+        remote(box, box, small_send.at[stage], small_recv.at[stage], peers[0]).wait_recv()
+        return box[...]
+
+    small_box[6] = small_acc[...]
+    small_mail(0, 0)
+    d_unit = d_first * par_ref[3:4] + d_second * par_ref[5:6]
+    d_unit = d_unit - jnp.mean(d_unit, axis=-1, keepdims=True) - unit * jnp.mean(
+        d_unit * unit, axis=-1, keepdims=True
+    )
+    xgrad_ref[0] = cot.astype(jnp.float32) + scale * d_unit
+    for stage in range(1, 3):
+        small_box[6 + stage] = small_box[5 + stage] + small_in(stage - 1)
+        slabs = SUM_SLABS[:4] if stage == 1 else SUM_SLABS[4:8]
+        reduce.steps([0], slabs)
+        small_mail(stage, stage)
+    small_box[9] = small_box[8] + small_in(2)
+    reduce.steps([1, 0], SUM_SLABS[8:12])
+    for stage in (3, 4, 5):
+        small_mail(stage, 3)
+    reduce.steps([1, 0], SUM_SLABS[12:])
+    total = small_box[9] + small_in(3) + small_in(4) + small_in(5)
+    shard = slot_at(place)
+    lead = pltpu.roll(total, (width - shard * shard_rows) % width, 1)[:, :pair]
+    inner_share = bg_ref.shape[1] // SLABS
+    per_row = width // inner_share
+    wide = pltpu.roll(total, (width - (shard % per_row) * inner_share) % width, 1)[:, :pair]
+    row_id = lax.broadcasted_iota(jnp.int32, wide.shape, 0)
+    wide = column_sum(jnp.where(row_id == 2 + shard // per_row, wide, 0.0))
+    small_ref[...] = lead
+    small_ref[10:11] = wide
+    kv.close()
+    reduce.finish()
+    for copy in sums_out:
+        copy.wait_send()
+
+
+def finish(args, shapes, collective_id):
+    rows, width, columns, shard_rows = shapes
+    pair = 2 * HDIM
+    low = jnp.bfloat16
+    slab = (HDIM, rows)
+    qkv_slab, out_slab = (shard_rows, columns), (shard_rows, width)
+    return pl.pallas_call(
+        finish_kernel,
+        in_specs=[vmem_spec()] * len(args),
+        out_specs=[vmem_spec()] * 5,
+        out_shape=[
+            jax.ShapeDtypeStruct((1, rows, width), low),
+            jax.ShapeDtypeStruct((1, rows, width), jnp.float32),
+            jax.ShapeDtypeStruct(qkv_slab, jnp.float32),
+            jax.ShapeDtypeStruct(out_slab, jnp.float32),
+            jax.ShapeDtypeStruct((SMALL_ROWS, pair), jnp.float32),
+        ],
+        scratch_shapes=[
+            pltpu.VMEM((2,) + slab, jnp.float32),
+            pltpu.VMEM((8,) + slab, low),
+            pltpu.VMEM((8,) + slab, low),
+            pltpu.VMEM((4,) + slab, low),
+            pltpu.VMEM((4,) + slab, low),
+            pltpu.SemaphoreType.DMA((16,)),
+            pltpu.SemaphoreType.DMA((16,)),
+            pltpu.VMEM((rows, width), low),
+            pltpu.VMEM((rows, width), jnp.float32),
+            pltpu.VMEM((SLABS,) + qkv_slab, low),
+            pltpu.VMEM((SLABS,) + out_slab, low),
+            pltpu.VMEM((16,) + qkv_slab, low),
+            pltpu.VMEM((16,) + out_slab, low),
+            pltpu.VMEM((31,) + qkv_slab, low),
+            pltpu.VMEM((31,) + out_slab, low),
+            pltpu.SemaphoreType.DMA((2, 31)),
+            pltpu.SemaphoreType.DMA((2, 31)),
+            pltpu.VMEM((SMALL_ROWS, width), jnp.float32),
+            pltpu.VMEM((10, SMALL_ROWS, width), jnp.float32),
+            pltpu.SemaphoreType.DMA((6,)),
+            pltpu.SemaphoreType.DMA((6,)),
+        ],
+        compiler_params=pltpu.CompilerParams(
+            collective_id=collective_id, has_side_effects=True, vmem_limit_bytes=56 << 20
+        ),
+        name="finish_with_reduce",
+    )(*args)
+
+
+def per_device_direct(
+    tokens,
+    branch_points,
+    qkv_weight,
+    out_weight,
+    up_weight,
+    down_weight,
+    query_bias,
+    out_bias,
+    up_bias,
+    down_bias,
+    first_gain,
+    first_shift,
+    second_gain,
+    second_shift,
+    cotangent,
+):
+    row_count, width = tokens.shape[1:]
+    shard_rows, columns = qkv_weight.shape
+    pair = 2 * HDIM
+    names = (query_bias, out_bias, down_bias, first_gain, first_shift, second_gain, second_shift)
+    small = jnp.stack([jnp.pad(v, (0, pair - v.shape[0])) for v in names + (up_bias,)])
+    block_index = lax.axis_index("tok")
+    limit = jnp.where(block_index >= PDEV, branch_points[0, 0], block_index * row_count)
+    positions = (limit + jnp.arange(row_count, dtype=jnp.int32)).astype(jnp.float32)
+    tables = lane_tables(positions, pair)
+    key_count = (PDEV + 1) * row_count
+    column = jnp.arange(key_count, dtype=jnp.int32)
+    shown = jnp.logical_or(column < limit, column >= key_count - row_count)
+    bias = jnp.broadcast_to(jnp.where(shown, 0.0, NEGATIVE)[None], (8, key_count))
+
+    def joined(gathered):
+        return gathered.reshape(-1, gathered.shape[2])
+
+    qkv_full, out_full, small_all = gather_shards(
+        (qkv_weight, out_weight, small), ("yx", "xy", "xy"), 0, "gather"
+    )
+    qkv_full, out_full = joined(qkv_full), joined(out_full)
+    lead = small_all[:, :, :shard_rows].transpose(1, 0, 2).reshape(8, width)
+    params = lead.astype(jnp.float32)
+    up_bias_full = small_all[:, 7, : up_bias.shape[0]].reshape(1, -1).astype(jnp.float32)
+    queries, key_value, all_kv, kv_t, d_context, first_low, second_low = project(
+        tokens, cotangent, qkv_full, out_full, params, tables, 1
+    )
+    kv = (all_kv.reshape(key_count, pair), kv_t, bias)
+    context_a, d_query_a, d_keys, d_values, up_full, down_full = attention(
+        0, queries, d_context, kv, comm=gather_beside((up_weight, down_weight), ROUTES), collective_id=2
+    )
+    up_full, down_full = joined(up_full), joined(down_full)
+    up_term, down_term, mlp_out, d_second, up_bias_term = mlp(
+        second_low, cotangent, up_full, up_bias_full, down_full
+    )
+    terms = (up_term.reshape(SLABS, -1, up_term.shape[1]), down_term.reshape(SLABS, -1, width))
+    context_b, d_query_b, sent, own_term, sum_up_w, sum_down_w = attention(
+        1,
+        queries,
+        d_context,
+        kv,
+        carried=(d_keys, d_values),
+        comm=reduce_beside(terms, ROUTES),
+        collective_id=3,
+    )
+    args = (
+        tokens,
+        cotangent,
+        context_a,
+        context_b,
+        d_query_a,
+        d_query_b,
+        sent,
+        own_term,
+        *tables,
+        first_low,
+        params,
+        qkv_full,
+        out_full,
+        mlp_out,
+        d_second,
+        up_bias_term,
+    )
+    layer_out, input_grad, sum_qkv_w, sum_out_w, sums = finish(
+        args, (row_count, width, columns, shard_rows), 4
+    )
+
+    def small_sum(row):
+        return sums[row, :shard_rows]
+
+    return (
+        layer_out,
+        key_value[None],
+        input_grad,
+        sum_qkv_w,
+        sum_out_w,
+        sum_up_w,
+        sum_down_w,
+        small_sum(0),
+        small_sum(1),
+        sums[10, : up_bias.shape[0]],
+        small_sum(1),
+        small_sum(6),
+        small_sum(7),
+        small_sum(8),
+        small_sum(9),
+    )
 
 
 def pack_small(flat, rows_above, columns):
@@ -860,7 +1327,6 @@
 
 
 def per_device(
-    direct,
     tokens,
     branch_points,
     qkv_weight,
@@ -901,10 +1367,7 @@
     def joined(gathered):
         return gathered.reshape(-1, gathered.shape[2])
 
-    if direct:
-        head_all, out_full = gather_shards((head, out_weight), ROUTES, 0, "gather")
-    else:
-        head_all, out_full = all_of(head, out_weight)
+    head_all, out_full = all_of(head, out_weight)
     out_full = joined(out_full)
     qkv_full = joined(head_all[:, :qkv_rows])
     (
@@ -939,10 +1402,7 @@
     )
     key_value = turn(projected[:, width:], key_tables, 1.0).astype(jnp.bfloat16)
     prompt_len = PDEV * row_count
-    if direct:
-        prompt_kv = gather_kv(key_value, 1).reshape(prompt_len, 2 * HDIM)
-    else:
-        prompt_kv = lax.all_gather(key_value, "tok", axis=0, tiled=True)[:prompt_len]
+    prompt_kv = lax.all_gather(key_value, "tok", axis=0, tiled=True)[:prompt_len]
     keys_values = jnp.concatenate([prompt_kv, key_value], axis=0)
 
     grad_rows = cotangent[0]
@@ -952,11 +1412,8 @@
     matmul = partial(lax.dot_general, preferred_element_type=jnp.float32)
     d_context = matmul(grad_rows, out_full, contract_last)
     tables_kv = attention_tables(keys_values, limit, row_count)
-    comm = gather_beside((up_weight, down_weight), ROUTES) if direct else None
-    context_a, d_query_a, d_keys, d_values, *gathered = attention(
-        0, queries, d_context, tables_kv, comm=comm, collective_id=2 if direct else None
-    )
-    up_full, down_full = map(joined, gathered if direct else all_of(up_weight, down_weight))
+    context_a, d_query_a, d_keys, d_values = attention(0, queries, d_context, tables_kv)
+    up_full, down_full = map(joined, all_of(up_weight, down_weight))
 
     pre_act = matmul(second_low, up_full, (((1,), (0,)), ((), ()))) + up_bias_full
     hidden, gelu_back = jax.vjp(partial(jax.nn.gelu, approximate=False), pre_act)
@@ -976,26 +1433,16 @@
         ]
 
     wide_terms = (by_shard(grad_up_w), by_shard(grad_down_w))
-    comm = reduce_beside(wide_terms, ROUTES) if direct else None
-    context_b, d_query_b, sent, own_term, *summed = attention(
-        1,
-        queries,
-        d_context,
-        tables_kv,
-        carried=(d_keys, d_values),
-        comm=comm,
-        collective_id=3 if direct else None,
-    )
-    sum_up_w, sum_down_w = summed if direct else sum_of(*wide_terms)
+    context_b, d_query_b, sent, own_term = attention(
+        1, queries, d_context, tables_kv, carried=(d_keys, d_values)
+    )
+    sum_up_w, sum_down_w = sum_of(*wide_terms)
     context_low = jnp.concatenate([context_a, context_b], axis=1)
     d_query = jnp.concatenate([d_query_a, d_query_b], axis=1)
-    if direct:
-        summed = reduce_kv(sent, 4)
-    else:
-        idle = lax.axis_size("tok") - PDEV
-        sent = jnp.pad(sent, ((0, idle), (0, 0), (0, 0), (0, 0)))
-        summed = lax.psum_scatter(sent, "tok", scatter_dimension=0, tiled=False)
-        summed = summed.astype(jnp.float32)
+    idle = lax.axis_size("tok") - PDEV
+    sent = jnp.pad(sent, ((0, idle), (0, 0), (0, 0), (0, 0)))
+    summed = lax.psum_scatter(sent, "tok", scatter_dimension=0, tiled=False)
+    summed = summed.astype(jnp.float32)
     kv_grad = (own_term + summed).reshape(2 * HDIM, row_count).T
 
     result = (
@@ -1038,10 +1485,7 @@
 
     tail = jnp.concatenate([by_shard(grad_qkv_w), small_flat.astype(jnp.bfloat16)], axis=1)
     terms = (tail, by_shard(grad_out_w))
-    if direct:
-        sum_tail, sum_out_w = reduce_shards(terms, ROUTES, 5, "reduce")
-    else:
-        sum_tail, sum_out_w = sum_of(*terms)
+    sum_tail, sum_out_w = sum_of(*terms)
     sum_qkv_w = sum_tail[:qkv_rows]
     (
         sum_query_b,
@@ -1091,7 +1535,7 @@
         P("grp", "tok", None),
     )
     return jax.shard_map(
-        partial(per_device, direct),
+        per_device_direct if direct else per_device,
         mesh=mesh,
         in_specs=placed,
         out_specs=(

time: 383 us -> 311 us (0.81)
  matrix products: 60.2 us -> 0 us
  Pallas kernels: 252 us -> 278 us
  local copies, waits for them, and re-layouts: 42.7 us -> 21.2 us
  other arithmetic: 17.7 us -> 2.8 us
    dot_general x12 -> x0, matrix products: 60.2 us -> none  [the longest x1 19.3 us: per_device(): matmul(second_low, up_full, (((1,), (0,)), ((), ()))) + up_bias_full]
    pallas_call x3, Pallas kernels: 67.5 us -> 95.3 us  [the longest x1 51.9 us: finish(): pl.pallas_call(finish_kernel, in_specs=[vmem_spec()] * len(args), out_spe...]
    concatenate x6 -> x0, local copies, waits for them, and re-layouts: 8.55 us -> none  [the longest x1 5.51 us: per_device(): packed = pack_small(jnp.concatenate(small)[None], qkv_rows, columns)[0]]
    another operation x8 -> x5, local copies, waits for them, and re-layouts: 10.7 us -> 3.31 us  [per_device_direct(): jnp.stack([jnp.pad(v, (0, pair - v.shape[0])) for v in names + (up_bias,)])]
    slice x13 -> x0, local copies, waits for them, and re-layouts: 5.58 us -> none  [the longest x4 2.43 us: turn(): jnp.roll(values, -half, axis=1) * from_right]
    unnamed x140 -> x48, local copies, waits for them, and re-layouts: 11 us -> 14.3 us
where the time goes in v4:
time: 311 us; the launch traced here: 305 us
  Pallas kernels  278 us (89%)
  local copies, waits for them, and re-layouts  21.2 us (7%)
    pallas_call x2, Pallas kernels, attention(): pl.pallas_call(partial(attention_kernel, last, plan, (inputs, outputs, co...  157 us
    pallas_call x1, Pallas kernels, finish(): pl.pallas_call(finish_kernel, in_specs=[vmem_spec()] * len(args), out_spe...  51.9 us
    pallas_call x1, Pallas kernels, gather_shards(): pl.pallas_call(partial(gather_kernel, orders), in_specs=[pl.BlockSpec(mem...  25.6 us
    pallas_call x1, Pallas kernels, project(): pl.pallas_call(project_kernel, in_specs=[vmem_spec()] * 8, out_specs=[vme...  22 us
    pallas_call x1, Pallas kernels, mlp(): pl.pallas_call(mlp_kernel, grid=(inner // tile,), in_specs=[pl.BlockSpec(...  21.4 us
    unnamed x48, local copies, waits for them, and re-layouts  14.3 us

profile of v4, /device:TPU:0, one launch (start us, length us, event | category | flops | bytes accessed | tf_op | source)
XLA Modules:
  0.0 304.5 jit_solution(9127579181811475786)
XLA Ops:
  1.5 0.7 pad_bitcast_fusion.6
  4.8 0.7 broadcast_in_dim.44.refs_4_
  5.5 1.0 fusion
  6.5 25.6 %gather.1 = (bf16[32,24,896]{2,1,0:T(8,128)(2,1)}, bf16[32,24,768]{2,1,0:T(8,128)(2,1)}, bf16[32,8,128]{2,1,0:T(8,128)(2,1)}) custom-call(bf16[24,896]{1,0:T(8,128)(2,1)} %refs_0_.1, bf16[24,768]{1,0:T(8,128)(2,1)} %refs_1_.1, bf16[8,128]{1,0:T(8,128)(2,1)} %stack.35.refs_2_), custom_call_target="tpu_custom_call" | custom-call | tf_op jit(solution)/shard_map/gather/pallas_call | solution.py:200
  32.2 0.9 convert_reduce_fusion
  33.2 0.9 convert_bitcast_fusion
  34.2 22.0 %project_with_gather.1 = (bf16[512,768]{1,0:T(8,128)(2,1)S(1)}, bf16[512,128]{1,0:T(8,128)(2,1)S(1)}, bf16[9,512,128]{2,1,0:T(8,128)(2,1)S(1)}, bf16[128,4608]{1...) custom-call(bf16[1,512,768]{2,1,0:T(8,128)(2,1)S(1)} %copy-done.1, ...), custom_call_target="tpu_custom_call" | custom-call | tf_op jit(solution)/shard_map/project_with_gather/pallas_call | solution.py:787
  56.3 0.9 copy-done.7
  57.2 0.9 copy-done.8
  58.1 1.1 copy-done.12
  59.2 0.9 copy-done.13
  60.1 79.7 %attention_with_gather.1 = (bf16[512,384]{1,0:T(8,128)(2,1)}, f32[512,384]{1,0:T(8,128)}, f32[64,4608]{1,0:T(8,128)}, f32[64,4608]{1,0:T(8,128)}, bf16[32,24,307...) custom-call(bf16[512,768]{1,0:T(8,128)(2,1)} %copy-done.13, f32[512,768]{1,0:T(8,128)} %get-tuple-element.51.refs_1_, ...), custom_call_target="tpu_custom_call" | custom-call | flops 10871635968 | bytes 12582912 | tf_op jit(solution)/shard_map/attention_with_gather/pallas_call | solution.py:505
  139.8 1.1 copy-done.9
  141.0 21.4 %mlp.1 = (bf16[768,3072]{1,0:T(8,128)(2,1)}, bf16[3072,768]{1,0:T(8,128)(2,1)}, f32[512,768]{1,0:T(8,128)S(1)}, f32[512,768]{1,0:T(8,128)S(1)}, f32[1,3072]{1,0:T(1,128)S(1)}) custom-call(bf16[512,768]{1,0:T(8,128)(2,1)S(1)} %copy-done.9, bf16[1,512,768]{2,1,0:T(8,128)(2,1)S(1)} %copy-done, bf16[768,3072]{1,0:T(8,128)(2,1)} %bitcast.49, ...), custom_call_target="tpu_custom_call" | custom-call | tf_op jit(solution)/shard_map/mlp/pallas_call | solution.py:840
  162.3 1.1 copy-done.5
  163.5 1.2 copy-done.6
  164.6 77.7 %attention_with_reduce.1 = (bf16[512,384]{1,0:T(8,128)(2,1)}, f32[512,384]{1,0:T(8,128)}, bf16[8,2,64,512]{3,2,1,0:T(8,128)(2,1)}, f32[2,64,512]{2,1,0:T(8,128)}, f32[24,3072]{1,0:T(8,128)}, /*index=5*/f32[96,768]{1,0:T(8,128)}) custom-call(bf16[512,768]{1,0:T(8,128)(2,1)} %copy-done.13, f32[512,768]{1,0:T(8,128)} %get-tuple-element.51.refs_1_, ...), custom_call_target="tpu_custom_call" | custom-call | flops 10871635968 | bytes 12582912 | tf_op jit(solution)/shard_map/attention_with_reduce/pallas_call | solution.py:505
  242.4 51.9 %finish_with_reduce.1 = (bf16[1,512,768]{2,1,0:T(8,128)(2,1)}, f32[1,512,768]{2,1,0:T(8,128)}, f32[24,896]{1,0:T(8,128)}, f32[24,768]{1,0:T(8,128)}, f32[16,128]{1,0:T(8,128)}) custom-call(bf16[1,512,768]{2,1,0:T(8,128)(2,1)} %x_ref.3, bf16[1,512,768]{2,1,0:T(8,128)(2,1)} %cot_ref.5, bf16[512,384]{1,0:T(8,128)(2,1)} %get-tuple-element.54.ctxa_ref, ...), custom_call_target="tpu_custom_call" | custom-call | tf_op jit(solution)/shard_map/finish_with_reduce/pallas_call | solution.py:1163
  294.3 1.3 slice_bitcast_fusion.4
  295.6 1.4 slice_bitcast_fusion
  297.5 2.1 copy.42
  300.2 1.1 copy.44
  302.7 0.7 copy.47
  303.4 0.7 copy.48
  (49 shorter events, 5.4 us)
Async XLA Ops:
  0.6 33.5 %copy-start = (bf16[1,512,768]{2,1,0:T(8,128)(2,1)S(1)}, bf16[1,512,768]{2,1,0:T(8,128)(2,1)}, u32[]{:S(2)}) copy-start(bf16[1,512,768]{2,1,0:T(8,128)(2,1)} %cot_ref.5) | copy-start | bytes 2359300
  0.7 33.5 %copy-start.1 = (bf16[1,512,768]{2,1,0:T(8,128)(2,1)S(1)}, bf16[1,512,768]{2,1,0:T(8,128)(2,1)}, u32[]{:S(2)}) copy-start(bf16[1,512,768]{2,1,0:T(8,128)(2,1)} %x_ref.3) | copy-start | bytes 2359300
  6.5 49.8 %copy-start.2 = (f32[512,128]{1,0:T(8,128)}, f32[512,128]{1,0:T(8,128)S(1)}, u32[]{:S(2)}) copy-start(f32[512,128]{1,0:T(8,128)S(1)} %get-tuple-element.85.left_ref) | copy-start | bytes 786436
  6.5 49.8 %copy-start.3 = (f32[512,128]{1,0:T(8,128)}, f32[512,128]{1,0:T(8,128)S(1)}, u32[]{:S(2)}) copy-start(f32[512,128]{1,0:T(8,128)S(1)} %get-tuple-element.86.right_ref) | copy-start | bytes 786436
  6.5 49.8 %copy-start.4 = (f32[512,128]{1,0:T(8,128)}, f32[512,128]{1,0:T(8,128)S(1)}, u32[]{:S(2)}) copy-start(f32[512,128]{1,0:T(8,128)S(1)} %get-tuple-element.87.own_ref) | copy-start | bytes 786436
  34.2 22.1 %copy-start.10 = (f32[8,768]{1,0:T(8,128)}, f32[8,768]{1,0:T(8,128)S(1)}, u32[]{:S(2)}) copy-start(f32[8,768]{1,0:T(8,128)S(1)} %reshape.113.par_ref) | copy-start | bytes 73732
  56.3 0.9 copy-start.7
  57.2 0.9 copy-start.8
  58.1 1.1 copy-start.12
  59.2 0.9 copy-start.13
  139.8 1.1 copy-start.9
  162.3 1.1 copy-start.5
  163.5 1.2 copy-start.6
  164.6 77.7 %copy-start.11 = (f32[1,3072]{1,0:T(1,128)}, f32[1,3072]{1,0:T(1,128)S(1)}, u32[]{:S(2)}) copy-start(f32[1,3072]{1,0:T(1,128)S(1)} %get-tuple-element.70.bg_ref) | copy-start | bytes 36868
  294.3 5.9 %copy-start.14 = (f32[1,512,768]{2,1,0:T(8,128)S(1)}, f32[1,512,768]{2,1,0:T(8,128)}, u32[]{:S(2)}) copy-start(f32[1,512,768]{2,1,0:T(8,128)} %get-tuple-element.145) | copy-start | bytes 4718596
  297.0 4.4 %copy-start.19 = (f32[24]{0:T(128)}, f32[24]{0:T(128)S(1)}, u32[]{:S(2)}) copy-start(f32[24]{0:T(128)S(1)} %get-tuple-element.151) | copy-start | bytes 292
  300.2 1.2 copy-start.17
  300.2 1.8 copy-start.18
  300.2 2.4 copy-start.16
  300.2 3.2 %copy-start.15 = (f32[96,768]{1,0:T(8,128)S(1)}, f32[96,768]{1,0:T(8,128)}, u32[]{:S(2)}) copy-start(f32[96,768]{1,0:T(8,128)} %get-tuple-element.149) | copy-start | bytes 884740

commit v5 on v4

--- a/solution.py
+++ b/solution.py
@@ -134,9 +134,6 @@
 
     def spread(self, a, k, fp, fq):
         place, order, slab = self.place, self.orders[a], (k, fp, fq)
-        if slab == (0, 0, 0):
-            for j in (1, 2, 3):
-                self.push(a, slab, j * 4, partial(near, place, k=j))
         if fp == 0 and fq == 0:
             self.push(a, slab, k * 4 + 2, partial(near_pq, place, order, fp=1))
         if fq == 0:
@@ -156,6 +153,9 @@
         return pltpu.make_async_copy(self.ins[a], self.outs[a].at[slot], self.local.at[a])
 
     def begin(self, arrays):
+        for j in (1, 2, 3):
+            for a in arrays:
+                self.push(a, (0, 0, 0), j * 4, partial(near, self.place, k=j))
         for a in arrays:
             self.spread(a, 0, 0, 0)
             self.own_copy(a).start()
@@ -386,7 +386,7 @@
         prompt // CHUNK,
         score_step,
         jnp.full((2 * rows, pair), NEGATIVE, jnp.float32),
-        unroll=unroll,
+        unroll=prompt // CHUNK,
     )
     row_id = lax.broadcasted_iota(jnp.int32, (2 * rows, rows), 0) % rows
     col_id = lax.broadcasted_iota(jnp.int32, (2 * rows, rows), 1)
@@ -411,7 +411,7 @@
     total, mixed = lax.fori_loop(
         0, key_count // CHUNK, weight_step, (zero, zero), unroll=unroll
     )
-    point(2)
+    point(3)
     scale = 1.0 / jnp.sum(total, axis=1, keepdims=True)
     mixed = mixed * scale
     context = jnp.where(first_head, pltpu.roll(mixed[:rows], HDIM, 1), mixed[rows:])
@@ -434,10 +434,15 @@
         dkt_ref[:, cols] += jnp.dot(q_cols, d_scores, preferred_element_type=jnp.float32)
         return d_query + jnp.dot(d_scores, kv_ref[cols, :], preferred_element_type=jnp.float32)
 
-    d_query = lax.fori_loop(0, key_count // CHUNK, grad_step, zero, unroll=unroll)
+    third = key_count // CHUNK // 3
+    d_query = lax.fori_loop(0, third, grad_step, zero, unroll=third)
+    point(4)
+    d_query = lax.fori_loop(third, 2 * third, grad_step, d_query, unroll=third)
+    point(5)
+    d_query = lax.fori_loop(2 * third, key_count // CHUNK, grad_step, d_query, unroll=3)
     second = pltpu.roll(d_query[rows:], HDIM, 1)
     dq_ref[...] = jnp.where(first_head, d_query[:rows], second) * SCORE_SCALE
-    point(3)
+    point(6)
     if last:
 
         @pl.when(step == pl.num_programs(0) - 1)
@@ -524,6 +529,35 @@
     )(*args)
 
 
+GATHER_PLAN = (
+    ((0, 1), [(0, 1, 0)]),
+    ((0, 3), [(1, 0, 0)]),
+    ((0, 4), [(0, 0, 1)]),
+    ((0, 5), [(1, 1, 0), (2, 0, 0)]),
+    ((1, 0), [(0, 1, 1)]),
+    ((1, 1), [(1, 0, 1)]),
+    ((1, 3), [(2, 1, 0), (3, 0, 0)]),
+    ((1, 4), [(1, 1, 1)]),
+    ((1, 5), [(2, 0, 1)]),
+    ((2, 0), [(3, 1, 0)]),
+    ((2, 1), [(2, 1, 1), (3, 0, 1)]),
+    ((2, 4), [(3, 1, 1)]),
+)
+BESIDE_SLABS = [(k, fp, fq) for k in (3, 2, 1, 0) for fp, fq in ((1, 1), (0, 1))]
+BESIDE_SLABS += [(k, fp, 0) for k in (3, 2, 1, 0) for fp in (1, 0)]
+REDUCE_PLAN = (
+    ((0, 1), [(3, 1, 1), (3, 0, 1)]),
+    ((0, 3), [(2, 1, 1), (2, 0, 1)]),
+    ((0, 5), [(3, 1, 0), (1, 1, 1), (1, 0, 1)]),
+    ((1, 1), [(2, 1, 0), (0, 1, 1), (0, 0, 1)]),
+    ((1, 3), [(3, 0, 0)]),
+    ((1, 5), [(1, 1, 0)]),
+    ((2, 0), [(2, 0, 0)]),
+    ((2, 1), [(0, 1, 0)]),
+    ((2, 3), [(1, 0, 0)]),
+)
+
+
 def gather_beside(shards, orders):
     n = len(shards)
     arrays = range(n)
@@ -536,16 +570,11 @@
             greet(place)
             gather.begin(arrays)
 
-        return {
-            (0, 0): begin,
-            (0, 2): lambda: gather.pass_on(arrays, Z_SLABS[:1]),
-            (1, 0): lambda: gather.pass_on(arrays, Z_SLABS[1:]),
-            (1, 1): lambda: gather.pass_on(arrays, P_SLABS[:2]),
-            (1, 2): lambda: gather.pass_on(arrays, P_SLABS[2:]),
-            (2, 0): lambda: gather.pass_on(arrays, Q_SLABS[:4]),
-            (2, 2): lambda: gather.pass_on(arrays, Q_SLABS[4:]),
-            (2, 3): lambda: gather.finish(arrays),
-        }
+        events = {(0, 0): begin}
+        for when, slabs in GATHER_PLAN:
+            events[when] = partial(gather.pass_on, arrays, slabs)
+        events[2, 6] = partial(gather.finish, arrays)
+        return events
 
     out_shape = [jax.ShapeDtypeStruct((SLABS,) + s.shape, s.dtype) for s in shards]
     out_specs = [pl.BlockSpec(memory_space=pl.ANY)] * n
@@ -567,21 +596,16 @@
 
         def begin():
             greet(place)
-            reduce.begin(arrays, SUM_SLABS)
+            reduce.begin(arrays, BESIDE_SLABS)
 
         def end():
             reduce.steps(arrays, SUM_SLABS[15:])
             reduce.finish()
 
-        return {
-            (0, 0): begin,
-            (0, 2): lambda: reduce.steps(arrays, SUM_SLABS[:4]),
-            (1, 0): lambda: reduce.steps(arrays, SUM_SLABS[4:8]),
-            (1, 2): lambda: reduce.steps(arrays, SUM_SLABS[8:10]),
-            (2, 0): lambda: reduce.steps(arrays, SUM_SLABS[10:12]),
-            (2, 2): lambda: reduce.steps(arrays, SUM_SLABS[12:15]),
-            (2, 3): end,
-        }
+        events = {(0, 0): begin, (2, 6): end}
+        for when, slabs in REDUCE_PLAN:
+            events[when] = partial(reduce.steps, arrays, slabs)
+        return events
 
     slabs = [t.shape[1:] for t in terms]
     out_shape = [jax.ShapeDtypeStruct(s, jnp.float32) for s in slabs]

time: 311 us -> 292 us (0.939); the launches traced: 305 us -> 292 us
  Pallas kernels: 278 us -> 266 us
    pallas_call x2, Pallas kernels: 157 us -> 148 us  [attention(): pl.pallas_call(partial(attention_kernel, last, plan, (inputs, outputs, co...]
where the time goes in v5:
time: 292 us
  Pallas kernels  266 us (91%)
  local copies, waits for them, and re-layouts  21.2 us (7%)
    pallas_call x2, Pallas kernels, attention(): pl.pallas_call(partial(attention_kernel, last, plan, (inputs, outputs, co...  148 us
    pallas_call x1, Pallas kernels, finish(): pl.pallas_call(finish_kernel, in_specs=[vmem_spec()] * len(args), out_spe...  49.9 us
    pallas_call x1, Pallas kernels, gather_shards(): pl.pallas_call(partial(gather_kernel, orders), in_specs=[pl.BlockSpec(mem...  25.2 us
    pallas_call x1, Pallas kernels, project(): pl.pallas_call(project_kernel, in_specs=[vmem_spec()] * 8, out_specs=[vme...  21.6 us
    pallas_call x1, Pallas kernels, mlp(): pl.pallas_call(mlp_kernel, grid=(inner // tile,), in_specs=[pl.BlockSpec(...  21.4 us
    unnamed x48, local copies, waits for them, and re-layouts  14.3 us

profile of v5, /device:TPU:0, one launch (start us, length us, event | category | flops | bytes accessed | tf_op | source)
XLA Modules:
  0.0 291.9 jit_solution(9121141409761872087)
XLA Ops:
  1.5 0.7 pad_bitcast_fusion.6
  4.8 0.7 broadcast_in_dim.44.refs_4_
  5.5 1.0 fusion
  6.5 25.2 %gather.1 = (bf16[32,24,896]{2,1,0:T(8,128)(2,1)}, bf16[32,24,768]{2,1,0:T(8,128)(2,1)}, bf16[32,8,128]{2,1,0:T(8,128)(2,1)}) custom-call(bf16[24,896]{1,0:T(8,128)(2,1)} %refs_0_.1, bf16[24,768]{1,0:T(8,128)(2,1)} %refs_1_.1, bf16[8,128]{1,0:T(8,128)(2,1)} %stack.35.refs_2_), custom_call_target="tpu_custom_call" | custom-call | tf_op jit(solution)/shard_map/gather/pallas_call | solution.py:200
  31.7 0.9 convert_reduce_fusion
  32.7 0.9 convert_bitcast_fusion
  33.8 21.6 %project_with_gather.1 = (bf16[512,768]{1,0:T(8,128)(2,1)S(1)}, bf16[512,128]{1,0:T(8,128)(2,1)S(1)}, bf16[9,512,128]{2,1,0:T(8,128)(2,1)S(1)}, bf16[128,4608]{1...) custom-call(bf16[1,512,768]{2,1,0:T(8,128)(2,1)S(1)} %copy-done.1, ...), custom_call_target="tpu_custom_call" | custom-call | tf_op jit(solution)/shard_map/project_with_gather/pallas_call | solution.py:811
  55.4 0.9 copy-done.7
  56.3 0.9 copy-done.8
  57.2 1.1 copy-done.12
  58.3 0.9 copy-done.13
  59.2 71.9 %attention_with_gather.1 = (bf16[512,384]{1,0:T(8,128)(2,1)}, f32[512,384]{1,0:T(8,128)}, f32[64,4608]{1,0:T(8,128)}, f32[64,4608]{1,0:T(8,128)}, bf16[32,24,307...) custom-call(bf16[512,768]{1,0:T(8,128)(2,1)} %copy-done.13, f32[512,768]{1,0:T(8,128)} %get-tuple-element.51.refs_1_, ...), custom_call_target="tpu_custom_call" | custom-call | flops 10871635968 | bytes 12582912 | tf_op jit(solution)/shard_map/attention_with_gather/pallas_call | solution.py:510
  131.1 1.1 copy-done.9
  132.2 21.4 %mlp.1 = (bf16[768,3072]{1,0:T(8,128)(2,1)}, bf16[3072,768]{1,0:T(8,128)(2,1)}, f32[512,768]{1,0:T(8,128)S(1)}, f32[512,768]{1,0:T(8,128)S(1)}, f32[1,3072]{1,0:T(1,128)S(1)}) custom-call(bf16[512,768]{1,0:T(8,128)(2,1)S(1)} %copy-done.9, bf16[1,512,768]{2,1,0:T(8,128)(2,1)S(1)} %copy-done, bf16[768,3072]{1,0:T(8,128)(2,1)} %bitcast.49, ...), custom_call_target="tpu_custom_call" | custom-call | tf_op jit(solution)/shard_map/mlp/pallas_call | solution.py:864
  153.6 1.1 copy-done.5
  154.7 1.2 copy-done.6
  155.9 76.2 %attention_with_reduce.1 = (bf16[512,384]{1,0:T(8,128)(2,1)}, f32[512,384]{1,0:T(8,128)}, bf16[8,2,64,512]{3,2,1,0:T(8,128)(2,1)}, f32[2,64,512]{2,1,0:T(8,128)}, f32[24,3072]{1,0:T(8,128)}, /*index=5*/f32[96,768]{1,0:T(8,128)}) custom-call(bf16[512,768]{1,0:T(8,128)(2,1)} %copy-done.13, f32[512,768]{1,0:T(8,128)} %get-tuple-element.51.refs_1_, ...), custom_call_target="tpu_custom_call" | custom-call | flops 10871635968 | bytes 12582912 | tf_op jit(solution)/shard_map/attention_with_reduce/pallas_call | solution.py:510
  232.0 49.9 %finish_with_reduce.1 = (bf16[1,512,768]{2,1,0:T(8,128)(2,1)}, f32[1,512,768]{2,1,0:T(8,128)}, f32[24,896]{1,0:T(8,128)}, f32[24,768]{1,0:T(8,128)}, f32[16,128]{1,0:T(8,128)}) custom-call(bf16[1,512,768]{2,1,0:T(8,128)(2,1)} %x_ref.3, bf16[1,512,768]{2,1,0:T(8,128)(2,1)} %cot_ref.5, bf16[512,384]{1,0:T(8,128)(2,1)} %get-tuple-element.54.ctxa_ref, ...), custom_call_target="tpu_custom_call" | custom-call | tf_op jit(solution)/shard_map/finish_with_reduce/pallas_call | solution.py:1187
  281.9 1.3 slice_bitcast_fusion.4
  283.2 1.4 slice_bitcast_fusion
  285.1 2.1 copy.42
  287.9 1.1 copy.44
  290.3 0.7 copy.47
  291.0 0.7 copy.48
  (49 shorter events, 5.4 us)
Async XLA Ops:
  0.6 33.1 %copy-start = (bf16[1,512,768]{2,1,0:T(8,128)(2,1)S(1)}, bf16[1,512,768]{2,1,0:T(8,128)(2,1)}, u32[]{:S(2)}) copy-start(bf16[1,512,768]{2,1,0:T(8,128)(2,1)} %cot_ref.5) | copy-start | bytes 2359300
  0.7 33.1 %copy-start.1 = (bf16[1,512,768]{2,1,0:T(8,128)(2,1)S(1)}, bf16[1,512,768]{2,1,0:T(8,128)(2,1)}, u32[]{:S(2)}) copy-start(bf16[1,512,768]{2,1,0:T(8,128)(2,1)} %x_ref.3) | copy-start | bytes 2359300
  6.5 48.9 %copy-start.2 = (f32[512,128]{1,0:T(8,128)}, f32[512,128]{1,0:T(8,128)S(1)}, u32[]{:S(2)}) copy-start(f32[512,128]{1,0:T(8,128)S(1)} %get-tuple-element.85.left_ref) | copy-start | bytes 786436
  6.5 48.9 %copy-start.3 = (f32[512,128]{1,0:T(8,128)}, f32[512,128]{1,0:T(8,128)S(1)}, u32[]{:S(2)}) copy-start(f32[512,128]{1,0:T(8,128)S(1)} %get-tuple-element.86.right_ref) | copy-start | bytes 786436
  6.5 48.9 %copy-start.4 = (f32[512,128]{1,0:T(8,128)}, f32[512,128]{1,0:T(8,128)S(1)}, u32[]{:S(2)}) copy-start(f32[512,128]{1,0:T(8,128)S(1)} %get-tuple-element.87.own_ref) | copy-start | bytes 786436
  33.7 21.7 %copy-start.10 = (f32[8,768]{1,0:T(8,128)}, f32[8,768]{1,0:T(8,128)S(1)}, u32[]{:S(2)}) copy-start(f32[8,768]{1,0:T(8,128)S(1)} %reshape.113.par_ref) | copy-start | bytes 73732
  55.4 0.9 copy-start.7
  56.3 0.9 copy-start.8
  57.2 1.1 copy-start.12
  58.3 0.9 copy-start.13
  131.1 1.1 copy-start.9
  153.6 1.1 copy-start.5
  154.7 1.2 copy-start.6
  155.9 76.2 %copy-start.11 = (f32[1,3072]{1,0:T(1,128)}, f32[1,3072]{1,0:T(1,128)S(1)}, u32[]{:S(2)}) copy-start(f32[1,3072]{1,0:T(1,128)S(1)} %get-tuple-element.70.bg_ref) | copy-start | bytes 36868
  281.9 5.9 %copy-start.14 = (f32[1,512,768]{2,1,0:T(8,128)S(1)}, f32[1,512,768]{2,1,0:T(8,128)}, u32[]{:S(2)}) copy-start(f32[1,512,768]{2,1,0:T(8,128)} %get-tuple-element.145) | copy-start | bytes 4718596
  284.6 4.4 %copy-start.19 = (f32[24]{0:T(128)}, f32[24]{0:T(128)S(1)}, u32[]{:S(2)}) copy-start(f32[24]{0:T(128)S(1)} %get-tuple-element.151) | copy-start | bytes 292
  287.8 1.2 copy-start.17
  287.8 1.8 copy-start.18
  287.8 2.4 copy-start.16
  287.9 3.2 %copy-start.15 = (f32[96,768]{1,0:T(8,128)S(1)}, f32[96,768]{1,0:T(8,128)}, u32[]{:S(2)}) copy-start(f32[96,768]{1,0:T(8,128)} %get-tuple-element.149) | copy-start | bytes 884740
